TPU v7x, 128 devices: a whole 4x4x4 slice. The times are simulated.
128 devices in a mesh: blk: 2 (over core), dp: 64 (over z, y, x).
Axes of the slice: x: 4, y: 4, z: 4, core: 2. Of those that a mesh axis runs over, the one named last changes fastest.
Arguments:
- queries: bfloat16 [16384, 256], P(('blk', 'dp')), may hold values from -1 to 1, as said below
- items: bfloat16 [16384, 256], P(('blk', 'dp')), may hold values from -1 to 1, as said below
Outputs:
- loss: float32 [], replicated
- question_slope: float32 [16384, 256], P(('blk', 'dp'))
- candidate_slope: float32 [16384, 256], P(('blk', 'dp'))
Inputs may be any that keep to these rules, and one draw needn't show every extreme that they name: queries: entries lie between -1 and 1 and no row is zero; each query is close to its own item and to one item of the batch chosen by a random permutation (which may be its own). items: entries lie between -1 and 1 and no row is zero.
All inputs are finite; a program needn't handle non-finite values.
Results may differ from a plain program's by a relative error of at most 0.008.
Values may be sent and summed in bfloat16 or wider, within the bound.
No kernel may reach another device: no remote copies, remote signals or barrier semaphores. Data moves between devices by JAX's collectives and lax.ppermute only.
A program may use at most 64 MiB of HBM per device.

v0:
```python
import functools
import math

import jax
import jax.numpy as jnp
from jax import lax
from jax.sharding import Mesh
from jax.sharding import PartitionSpec as P

BLK_DP = ("blk", "dp_0", "dp_1", "dp_2")


softmax_sharpness = 0.05
tiny_square = 1e-12


def taken_in(shard, axis, dim, absorb, state):
    everything = jax.tree.map(lambda a: lax.all_gather(a, axis, axis=dim, tiled=True), shard)
    return absorb(state, everything, jnp.int32(0))


def over_axes(value, axes):
    return functools.reduce(lax.psum, axes, value)


def unit_rows(matrix):
    widened = matrix.astype(jnp.float32)
    length = jnp.sqrt(jnp.sum(widened * widened, axis=1, keepdims=True) + tiny_square)
    return (widened / length, length)


def direction_slope(grad, unit, length):
    along = jnp.sum(unit * grad, axis=1, keepdims=True)
    return (grad - unit * along) / length


def split_rows(matrix, step_rows):
    return matrix.reshape((matrix.shape[0] // step_rows, step_rows) + matrix.shape[1:])


def per_device(queries, items):
    question_direction, question_magnitude = unit_rows(queries)
    candidate_direction, candidate_magnitude = unit_rows(items)
    normalized_question = question_direction.astype(jnp.bfloat16)
    normalized_candidate = candidate_direction.astype(jnp.bfloat16)
    question_gathered_all = normalized_question.astype(jnp.float32)
    candidate_gathered_all = normalized_candidate.astype(jnp.float32)
    own_rows = normalized_question.shape[0]
    matching_score = (
        jnp.sum(question_gathered_all * candidate_gathered_all, axis=1) / softmax_sharpness
    )

    def norm_step(running, shard_rows, first_row):
        step_rows = math.gcd(shard_rows.shape[0], 512)

        def per_block(state, candidate_slice):
            old_peak, old_total = state
            similarity_scores = (
                jnp.dot(normalized_question, candidate_slice.T, preferred_element_type=jnp.float32)
                / softmax_sharpness
            )
            new_peak = jnp.maximum(old_peak, jnp.max(similarity_scores, axis=1))
            new_total = old_total * jnp.exp(old_peak - new_peak) + jnp.sum(
                jnp.exp(similarity_scores - new_peak[:, None]), axis=1
            )
            return ((new_peak, new_total), None)

        result, _ = lax.scan(per_block, running, split_rows(shard_rows, step_rows))
        return result

    start_state = (jnp.full((own_rows,), -1e30, jnp.float32), jnp.zeros((own_rows,), jnp.float32))
    peak, summed = taken_in(normalized_candidate, BLK_DP, 0, norm_step, start_state)
    log_norm = peak + jnp.log(summed)
    local_loss = jnp.sum(log_norm - matching_score)
    devices = lax.axis_size(BLK_DP)
    loss = over_axes(local_loss, BLK_DP) / (own_rows * devices)
    empty_grad = jnp.zeros(normalized_question.shape, jnp.float32)

    def query_step(running, shard_rows, first_row):
        step_rows = math.gcd(shard_rows.shape[0], 512)

        def per_block(acc_grad, candidate_slice):
            similarity_scores = (
                jnp.dot(normalized_question, candidate_slice.T, preferred_element_type=jnp.float32)
                / softmax_sharpness
            )
            weights = jnp.exp(similarity_scores - log_norm[:, None]).astype(jnp.bfloat16)
            return (
                acc_grad + jnp.dot(weights, candidate_slice, preferred_element_type=jnp.float32),
                None,
            )

        result, _ = lax.scan(per_block, running, split_rows(shard_rows, step_rows))
        return result

    question_count_overall = taken_in(normalized_candidate, BLK_DP, 0, query_step, empty_grad)

    def item_step(running, shard_rows, first_row):
        q_rows, q_norms = shard_rows
        step_rows = math.gcd(q_rows.shape[0], 512)

        def per_block(acc_grad, pieces):
            question_portion, norm_part = pieces
            question_slice_local = question_portion.astype(jnp.bfloat16)
            similarity_scores = (
                jnp.dot(
                    question_slice_local, normalized_candidate.T, preferred_element_type=jnp.float32
                )
                / softmax_sharpness
            )
            weights = jnp.exp(similarity_scores - norm_part[:, None]).astype(jnp.bfloat16)
            return (
                acc_grad
                + jnp.dot(weights.T, question_slice_local, preferred_element_type=jnp.float32),
                None,
            )

        result, _ = lax.scan(
            per_block, running, (split_rows(q_rows, step_rows), split_rows(q_norms, step_rows))
        )
        return result

    candidate_count_overall = taken_in(
        (question_gathered_all, log_norm), BLK_DP, 0, item_step, empty_grad
    )
    question_slope = direction_slope(
        (question_count_overall - candidate_gathered_all) / softmax_sharpness,
        question_direction,
        question_magnitude,
    )
    candidate_slope = direction_slope(
        (candidate_count_overall - question_gathered_all) / softmax_sharpness,
        candidate_direction,
        candidate_magnitude,
    )
    return (loss, question_slope, candidate_slope)


def solution(mesh):
    split = Mesh(mesh.devices.reshape(mesh.shape["blk"], 4, 4, 4), ("blk", "dp_0", "dp_1", "dp_2"))
    return jax.shard_map(
        per_device,
        mesh=split,
        in_specs=(P(BLK_DP, None), P(BLK_DP, None)),
        out_specs=(P(), P(BLK_DP, None), P(BLK_DP, None)),
        check_vma=False,
    )
```

profile of v0, /device:TPU:1, one launch (start us, length us, event | category | flops | bytes accessed | tf_op | source)
XLA Modules:
  0.0 578.1 jit_solution(8274456256658182323)
XLA Ops:
  8.2 1.6 fusion.37
  10.8 1.6 fusion.38
  12.4 72.5 %all-gather.4.cloned.1.call-done = bf16[16384,256]{1,0:T(8,128)(2,1)} async-done(((bf16[128,256]{1,0:T(8,128)(2,1)}), bf16[16384,256]{1,0:T(8,128)(2,1)}) %all-gather.4.cloned.1.call-update) | async-done | bytes 8388624 | tf_op jit(solution)/shard_map/all_gather | solution.py:18
  84.9 43.2 %while.35 = (s32[]{:T(128)}, f32[128]{0:T(128)S(1)}, f32[128]{0:T(128)S(1)}, bf16[32,512,256]{2,1,0:T(8,128)(2,1)}, bf16[128,256]{1,0:T(8,128)(2,1)}, /*index=5*/s32[]{:T(128)}, s32[]{:T(128)}) while((s32[]{:T(128)}, f32[128]{0:T(128)S(1)}, f32[128]{0:T(128)S(1)}, bf16[32,512,256]{2,1,0:T(8,128)(2,1)}, bf16[128,256]{1,0:T(8,128)(2,1)}, ...), condition=%wide.region_5.0_spmd.clone, body=%wide.region_2.5_spmd.clone.sunk | while | flops 33817216 | bytes 859224 | solution.py:68
  128.1 314.3 %all-gather = f32[128,1,128]{2,1,0:T(1,128)S(1)} all-gather(f32[1,1,128]{2,1,0:T(1,128)S(1)} %bitcast.41), channel_id=1, replica_groups=mesh['blk'=2,'dp_0'=4,'dp_1'=4,'dp_2'=4] {'blk','dp_0','dp_1','dp_2'}, dimensions={0}, use_global_device_ids=true | all-gather | bytes 66048 | tf_op jit(solution)/shard_map/all_gather | solution.py:18
  443.9 50.5 %while.36 = (s32[]{:T(128)}, f32[128,256]{1,0:T(8,128)S(1)}, bf16[32,512,256]{2,1,0:T(8,128)(2,1)}, bf16[128,256]{1,0:T(8,128)(2,1)}, f32[128]{0:T(128)S(1)}, /*index=5*/s32[]{:T(128)}, s32[]{:T(128)}) while((s32[]{:T(128)}, f32[128,256]{1,0:T(8,128)S(1)}, bf16[32,512,256]{2,1,0:T(8,128)(2,1)}, bf16[128,256]{1,0:T(8,128)(2,1)}, ...), condition=%wide.region_13.14_spmd.clone, body=%wide.region_12.13_spmd.clone.sunk | while | flops 67371008 | bytes 853591 | solution.py:93
  443.9 1.6 fusion.62
  445.4 1.6 fusion.62
  447.0 1.6 fusion.62
  448.6 1.6 fusion.62
  450.2 1.6 fusion.62
  451.8 1.6 fusion.62
  453.3 1.6 fusion.62
  454.9 1.6 fusion.62
  456.5 1.6 fusion.62
  458.1 1.6 fusion.62
  459.7 1.6 fusion.62
  461.2 1.6 fusion.62
  462.8 1.6 fusion.62
  464.4 1.6 fusion.62
  466.0 1.6 fusion.62
  467.5 1.6 fusion.62
  469.1 1.6 fusion.62
  470.7 1.6 fusion.62
  472.3 1.6 fusion.62
  473.8 1.6 fusion.62
  475.5 1.6 fusion.62
  477.1 1.6 fusion.62
  478.6 1.6 fusion.62
  480.2 1.6 fusion.62
  481.8 1.6 fusion.62
  483.4 1.6 fusion.62
  484.9 1.6 fusion.62
  486.5 1.6 fusion.62
  488.1 1.6 fusion.62
  489.7 1.6 fusion.62
  491.2 1.6 fusion.62
  492.8 1.6 fusion.62
  494.4 50.1 %while.37 = (s32[]{:T(128)}, f32[128,256]{1,0:T(8,128)S(1)}, bf16[32,512,256]{2,1,0:T(8,128)(2,1)}, bf16[128,256]{1,0:T(8,128)(2,1)S(1)}, f32[32,512]{1,0:T(8,128)S(1)}, /*index=5*/s32[]{:T(128)}, s32[]{:T(128)}) while((s32[]{:T(128)}, f32[128,256]{1,0:T(8,128)S(1)}, bf16[32,512,256]{2,1,0:T(8,128)(2,1)}, ...), condition=%wide.region_16.17_spmd.clone, body=%wide.region_15.16_spmd.clone.sunk | while | flops 67371008 | bytes 859227 | solution.py:118
  494.5 1.5 fusion.66
  496.0 1.5 fusion.66
  497.6 1.5 fusion.66
  499.2 1.5 fusion.66
  503.8 1.5 fusion.66
  505.4 1.5 fusion.66
  507.0 1.5 fusion.66
  511.7 1.5 fusion.66
  513.2 1.5 fusion.66
  514.8 1.5 fusion.66
  519.5 1.5 fusion.66
  521.1 1.5 fusion.66
  522.6 1.5 fusion.66
  525.8 1.6 fusion.66
  527.4 1.5 fusion.66
  528.9 1.5 fusion.66
  530.5 1.5 fusion.66
  532.1 1.5 fusion.66
  536.8 1.5 fusion.66
  538.3 1.5 fusion.66
  539.9 1.5 fusion.66
  545.4 3.1 psum.28
  548.5 6.6 %psum.29 = f32[]{:T(128)} all-reduce(f32[]{:T(128)} %psum.28), channel_id=1, replica_groups=mesh['blk'=2,'dp_0'=4,'dp_1'=4,'dp_2'=4] {'dp_0'}, use_global_device_ids=true, to_apply=%region_9.10 | all-reduce | flops 1 | bytes 8 | tf_op jit(solution)/shard_map/psum | solution.py:23
  555.1 6.6 %psum.30 = f32[]{:T(128)} all-reduce(f32[]{:T(128)} %psum.29), channel_id=1, replica_groups=mesh['blk'=2,'dp_0'=4,'dp_1'=4,'dp_2'=4] {'dp_1'}, use_global_device_ids=true, to_apply=%region_10.11 | all-reduce | flops 1 | bytes 8 | tf_op jit(solution)/shard_map/psum | solution.py:23
  561.7 7.0 %psum.31 = f32[]{:T(128)} all-reduce(f32[]{:T(128)} %psum.30), channel_id=1, replica_groups=mesh['blk'=2,'dp_0'=4,'dp_1'=4,'dp_2'=4] {'dp_2'}, use_global_device_ids=true, to_apply=%region_11.12 | all-reduce | flops 1 | bytes 8 | tf_op jit(solution)/shard_map/psum | solution.py:23
  (229 shorter events, 64.5 us)
Async XLA Ops:
  7.2 537.4 %copy-start.1 = (bf16[128,256]{1,0:T(8,128)(2,1)S(1)}, bf16[128,256]{1,0:T(8,128)(2,1)}, u32[]{:S(2)}) copy-start(bf16[128,256]{1,0:T(8,128)(2,1)} %param.9) | copy-start | bytes 196612
  7.2 537.4 %copy-start.2 = (bf16[128,256]{1,0:T(8,128)(2,1)S(1)}, bf16[128,256]{1,0:T(8,128)(2,1)}, u32[]{:S(2)}) copy-start(bf16[128,256]{1,0:T(8,128)(2,1)} %param.8) | copy-start | bytes 196612
  7.2 77.7 %all-gather.4.cloned.1.call-start = ((), (), s32[]{:S(2)}) async-start(), calls=%async_computation | async-start | bytes 8454144 | tf_op jit(solution)/shard_map/all_gather | solution.py:18
  9.8 484.6 %copy-start = (bf16[128,256]{1,0:T(8,128)(2,1)S(1)}, bf16[128,256]{1,0:T(8,128)(2,1)}, u32[]{:S(2)}) copy-start(bf16[128,256]{1,0:T(8,128)(2,1)} %fusion.37) | copy-start | bytes 196612
  9.8 484.6 %all-gather.6.cloned.1.call-start = ((), (), s32[]{:S(2)}) async-start(), calls=%async_computation.1 | async-start | bytes 8454144 | tf_op jit(solution)/shard_map/all_gather | solution.py:18
Sparse Core Ops, SparseCore 0:
  11.7 73.1 all-gather.3
  88.6 67.3 all-gather.5
where the time goes:
time: 586 us; the launch traced here: 578 us
  blocking collectives  338 us (58%)
  matrix products  137 us (23%)
  waiting for transfers between devices  72.5 us (12%)
  between operations  16 us (3%)
  other arithmetic  11.2 us (2%)
    all_gather x1, blocking collectives, taken_in(): lax.all_gather(a, axis, axis=dim, tiled=True)  314 us
    all_gather x2, waiting for transfers between devices, taken_in(): lax.all_gather(a, axis, axis=dim, tiled=True)  72.5 us
    dot_general x32, matrix products, per_block(): jnp.dot(weights, candidate_slice, preferred_element_type=jnp.float32)  49.8 us
    dot_general x32, matrix products, per_block(): jnp.dot(weights.T, question_slice_local, preferred_element_type=jnp.float32)  48.7 us
    dot_general x32, matrix products, per_block(): jnp.dot(normalized_question, candidate_slice.T, preferred_element_type=jn...  38.6 us
    psum x4, blocking collectives, over_axes(): return functools.reduce(lax.psum, axes, value)  23.3 us
  transfers between devices with their start and end apart: 2, of which 1 were waited for; matrix products, arithmetic and copies ran while one was open for 17% of the time, Pallas kernels for 0%

commit v1 on v0

v1 whole, which is shorter than its diff:
```python
import math

import jax
import jax.numpy as jnp
from jax import lax
from jax.experimental import pallas as pl
from jax.experimental.pallas import tpu as pltpu
from jax.sharding import Mesh
from jax.sharding import PartitionSpec as P

AXES = ("blk", "z", "y", "x")
RING = {(0, 0): 0, (1, 0): 1, (1, 1): 2, (0, 1): 3}
BITS = [(a, b, c) for a in (0, 1) for b in (0, 1) for c in (0, 1)]
GROUP = 8

sharpness = 0.05
tiny_square = 1e-12
log2_e = math.log2(math.e)
f32, bf16 = jnp.float32, jnp.bfloat16


def device_of(core, low, high):
    z, y, x = (RING[(l, h)] for l, h in zip(low, high))
    return ((core * 4 + z) * 4 + y) * 4 + x


LOW = [[device_of(c, low, high) for low in BITS] for c in (0, 1) for high in BITS]
HIGH = [[device_of(c, low, high) for high in BITS] for c in (0, 1) for low in BITS]


def exchange(pieces, groups):
    return lax.all_to_all(pieces, AXES, 0, 0, tiled=True, axis_index_groups=groups)


def swap_cores(value):
    return lax.ppermute(value, "blk", [(0, 1), (1, 0)])


def vmem_call(body, outs, name, flops=0, limit=24):
    spec = pl.BlockSpec(memory_space=pltpu.VMEM)
    return pl.pallas_call(
        body,
        out_shape=[jax.ShapeDtypeStruct(s, d) for s, d in outs],
        out_specs=[spec] * len(outs),
        compiler_params=pltpu.CompilerParams(vmem_limit_bytes=limit * 2**20),
        cost_estimate=pl.CostEstimate(flops=flops, bytes_accessed=0, transcendentals=0),
        name=name,
    )


def unit(matrix):
    wide = matrix.astype(f32)
    length = jnp.sqrt(jnp.sum(wide * wide, axis=1, keepdims=True) + tiny_square)
    return wide / length, length


def norm_body(q_ref, v_ref, qt_ref, vt_ref, pos_ref):
    q, v = unit(q_ref[...])[0].astype(bf16), unit(v_ref[...])[0].astype(bf16)
    for k in range(GROUP):
        qt_ref[k] = q
        vt_ref[k] = v
    total = jnp.sum(q.astype(f32) * v.astype(f32)) / sharpness
    pos_ref[...] = jnp.full((8, 128), total, f32)


def score_body(own_ref, oth_ref, q_ref, pos_ref, e_own_ref, e_oth_ref, s_ref, u_ref):
    cols = q_ref.shape[0] * q_ref.shape[1]
    q = q_ref[...].reshape(cols, q_ref.shape[2])
    total = jnp.zeros((1, cols), f32)
    pull = None
    for v_ref, e_ref in ((own_ref, e_own_ref), (oth_ref, e_oth_ref)):
        for k in range(0, GROUP, 2):
            v = v_ref[k : k + 2].reshape(256, 256)
            t = lax.dot_general(v, q, (((1,), (1,)), ((), ())), preferred_element_type=f32)
            e = jnp.exp2(t * (log2_e / sharpness))
            total = total + jnp.sum(e, axis=0, keepdims=True)
            eb = e.astype(bf16)
            e_ref[k * 128 : (k + 2) * 128] = eb
            part = lax.dot_general(v, eb, (((0,), (0,)), ((), ())), preferred_element_type=f32)
            pull = part if pull is None else pull + part
    for k in range(GROUP):
        u_ref[k] = pull[:, k * 128 : (k + 1) * 128].astype(bf16)
    for k in range(GROUP):
        for j in range(GROUP):
            s_ref[j, k : k + 1] = total[:, k * 128 : (k + 1) * 128]
    for j in range(GROUP):
        s_ref[j, 8:16] = pos_ref[...]


def row_sums(s_ref):
    total = s_ref[0]
    for j in range(1, GROUP):
        total = total + s_ref[j]
    return total


def weighted(e_ref, q_ref, r, k):
    rows = slice(k * 128, (k + 2) * 128)
    parts = [
        (e_ref[rows, j * 128 : (j + 1) * 128].astype(f32) * r[j : j + 1]).astype(bf16)
        for j in range(GROUP)
    ]
    p = jnp.concatenate(parts, axis=1)
    q = q_ref[...].reshape(q_ref.shape[0] * q_ref.shape[1], q_ref.shape[2])
    return jnp.dot(p, q, preferred_element_type=f32)


def give_body(e_ref, q_ref, s_ref, w_ref):
    sums = row_sums(s_ref)
    r = 1.0 / sums[:8]
    for k in range(0, GROUP, 2):
        w_ref[k * 128 : (k + 2) * 128] = weighted(e_ref, q_ref, r, k).astype(bf16)
    loss = jnp.sum(jnp.log(sums[:8])) - jnp.max(sums[8:9])
    high = jnp.full((8, 256), loss, f32).astype(bf16)
    low = (jnp.full((8, 256), loss, f32) - high.astype(f32)).astype(bf16)
    w_ref[1024:1040] = jnp.concatenate([high.astype(f32), low.astype(f32)], axis=0).astype(bf16)


def keep_body(e_ref, q_ref, s_ref, w_ref):
    r = 1.0 / row_sums(s_ref)[:8]
    for k in range(0, GROUP, 2):
        w_ref[k * 128 : (k + 2) * 128] = weighted(e_ref, q_ref, r, k)


def join_body(w_ref, got_ref, s_ref, out_ref):
    for k in range(GROUP):
        rows = slice(k * 128, (k + 1) * 128)
        out_ref[k, :128] = (w_ref[rows] + got_ref[rows].astype(f32)).astype(bf16)
    sums = row_sums(s_ref)
    loss = jnp.sum(jnp.log(sums[:8])) - jnp.max(sums[8:9])
    got = got_ref[1024:1040].astype(f32)
    both = got[:8] + got[8:] + loss
    high = both.astype(bf16)
    low = (both - high.astype(f32)).astype(bf16)
    tail = jnp.concatenate([high.astype(f32), low.astype(f32)], axis=0).astype(bf16)
    for k in range(GROUP):
        out_ref[k, 128:144] = tail


def slope(pull, hat, direction, length):
    grad = (pull - hat) / sharpness
    along = jnp.sum(direction * grad, axis=1, keepdims=True)
    return (grad - direction * along) / length


def final_body(high_ref, q_ref, v_ref, u_ref, w_ref, s_ref, loss_ref, qs_ref, vs_ref):
    q, q_len = unit(q_ref[...])
    v, v_len = unit(v_ref[...])
    q_hat, v_hat = q.astype(bf16).astype(f32), v.astype(bf16).astype(f32)
    ut = u_ref[0].astype(f32)
    w = w_ref[0, :128].astype(f32)
    tail = w_ref[0, 128:144].astype(f32)
    for k in range(1, GROUP):
        ut = ut + u_ref[k].astype(f32)
        w = w + w_ref[k, :128].astype(f32)
        tail = tail + w_ref[k, 128:144].astype(f32)
    sums = row_sums(s_ref)[:8]
    mine = lax.broadcasted_iota(jnp.int32, sums.shape, 0) == high_ref[0]
    own = jnp.sum(jnp.where(mine, sums, 0.0), axis=0, keepdims=True)
    u = (ut / own).T
    qs_ref[...] = slope(u, v_hat, q, q_len)
    vs_ref[...] = slope(w, q_hat, v, v_len)
    loss_ref[...] = (tail[:8] + tail[8:])[:, :128] / (128 * 128)


def high_index():
    bit = lambda a: (lax.axis_index(a) >= 2).astype(jnp.int32)
    return bit("z") * 4 + bit("y") * 2 + bit("x")


def per_device(queries, items):
    tile = (GROUP, 128, 256)
    qt, vt, pos = vmem_call(norm_body, [(tile, bf16), (tile, bf16), ((8, 128), f32)], "norm")(queries, items)
    own = exchange(vt, LOW)
    other = swap_cores(own)
    q = exchange(qt, HIGH)
    flops = 2 * 2048 * 1024 * 256
    e_own, e_oth, s, u = vmem_call(
        score_body,
        [((1024, 1024), bf16), ((1024, 1024), bf16), ((GROUP, 16, 128), f32), ((GROUP, 256, 128), bf16)],
        "score",
        2 * flops,
    )(own, other, q, pos)
    sums = exchange(s, HIGH)
    u = exchange(u, HIGH)
    (give,) = vmem_call(give_body, [((1040, 256), bf16)], "give", flops // 2)(e_oth, q, sums)
    got = swap_cores(give)
    (keep,) = vmem_call(keep_body, [((1024, 256), f32)], "keep", flops // 2)(e_own, q, sums)
    (w,) = vmem_call(join_body, [((GROUP, 144, 256), bf16)], "join")(keep, got, sums)
    w = exchange(w, LOW)
    loss, q_slope, v_slope = pl.pallas_call(
        final_body,
        in_specs=[pl.BlockSpec(memory_space=pltpu.SMEM)] + [pl.BlockSpec(memory_space=pltpu.VMEM)] * 5,
        out_specs=[pl.BlockSpec(memory_space=pltpu.VMEM)] * 3,
        out_shape=[
            jax.ShapeDtypeStruct((8, 128), f32),
            jax.ShapeDtypeStruct((128, 256), f32),
            jax.ShapeDtypeStruct((128, 256), f32),
        ],
        compiler_params=pltpu.CompilerParams(vmem_limit_bytes=24 * 2**20),
        name="final",
    )(high_index().reshape(1), queries, items, u, w, sums)
    return loss[0, 0], q_slope, v_slope


def solution(mesh):
    split = Mesh(mesh.devices.reshape(2, 4, 4, 4), AXES)
    rows = P(AXES, None)
    return jax.shard_map(
        per_device, mesh=split, in_specs=(rows, rows), out_specs=(P(), rows, rows), check_vma=False
    )
```

time: 586 us -> 90.6 us (0.15)
  the two profiles are of different devices: /device:TPU:1 before, /device:TPU:0 now
where the time goes in v1:
time: 90.6 us; the launch traced here: 90.1 us
  blocking collectives  48.7 us (54%)
  waiting for transfers between devices  22 us (24%)
  Pallas kernels  8.64 us (10%)
  starting transfers between devices  7.04 us (8%)
  local copies, waits for them, and re-layouts  2.99 us (3%)
    all_to_all x3, blocking collectives, exchange(): lax.all_to_all(pieces, AXES, 0, 0, tiled=True, axis_index_groups=groups)  48.7 us
    all_to_all x2, waiting for transfers between devices, exchange(): lax.all_to_all(pieces, AXES, 0, 0, tiled=True, axis_index_groups=groups)  22 us
    all_to_all x2, starting transfers between devices, exchange(): lax.all_to_all(pieces, AXES, 0, 0, tiled=True, axis_index_groups=groups)  7.03 us
    pallas_call x1, Pallas kernels, per_device(): vmem_call(score_body, [((1024, 1024), bf16), ((1024, 1024), bf16), ((GROU...  3.05 us
    unnamed x10, local copies, waits for them, and re-layouts  2.48 us
    pallas_call x1, Pallas kernels, per_device(): vmem_call(join_body, [((GROUP, 144, 256), bf16)], 'join')(keep, got, sums)  2.05 us
  transfers between devices with their start and end apart: 4, of which 2 were waited for; matrix products, arithmetic and copies ran while one was open for 0% of the time, Pallas kernels for 3%

profile of v1, /device:TPU:0, one launch (start us, length us, event | category | flops | bytes accessed | tf_op | source)
XLA Modules:
  0.0 90.1 jit_solution(6129239172439075450)
XLA Ops:
  0.6 0.0 copy-start.1
  0.6 0.8 copy-done.1
  1.5 0.0 copy-start.3
  1.5 0.8 copy-done.3
  2.3 0.3 norm.1
  2.6 15.1 %all_to_all.25.own_ref = bf16[8,128,256]{2,1,0:T(8,128)(2,1)S(1)} all-to-all(bf16[8,128,256]{2,1,0:T(8,128)(2,1)S(1)} %get-tuple-element.13), channel_id=1, replica_groups={{0,1,4,5,16,17,20,21},{3,2,7,6,19,18,23,22},{12,13,8,9,28,29,24,25},{15..., dimensions={0} | all-to-all | bytes 1048576 | tf_op jit(solution)/shard_map/all_to_all | solution.py:32
  17.7 0.0 collective-permute-start
  17.7 21.7 %all_to_all.26.q_ref = bf16[8,128,256]{2,1,0:T(8,128)(2,1)S(1)} all-to-all(bf16[8,128,256]{2,1,0:T(8,128)(2,1)S(1)} %get-tuple-element.14), channel_id=1, replica_groups={{0,3,12,15,48,51,60,63},{1,2,13,14,49,50,61,62},{4,7,8,11,52,55,56,59},..., dimensions={0} | all-to-all | bytes 1048576 | tf_op jit(solution)/shard_map/all_to_all | solution.py:32
  39.5 0.0 collective-permute-done.oth_ref
  39.5 3.1 %score.1 = (bf16[1024,1024]{1,0:T(8,128)(2,1)S(1)}, bf16[1024,1024]{1,0:T(8,128)(2,1)S(1)}, f32[8,16,128]{2,1,0:T(8,128)S(1)}, bf16[8,256,128]{2,1,0:T(8,128)(2,1)S(1)}) custom-call(bf16[8,128,256]{2,1,0:T(8,128)(2,1)S(1)} %all_to_all.25.own_ref, bf16[8,128,256]{2,1,0:T(8,128)(2,1)S(1)} %collective-permute-done.oth_ref, ...), custom_call_target="tpu_custom_call" | custom-call | flops 2147483648 | tf_op jit(solution)/shard_map/score/pallas_call | solution.py:178
  42.5 0.0 copy-start
  42.5 0.8 copy-done
  43.3 11.9 %all_to_all.27.s_ref = f32[8,16,128]{2,1,0:T(8,128)S(1)} all-to-all(f32[8,16,128]{2,1,0:T(8,128)S(1)} %get-tuple-element.18), channel_id=1, replica_groups={{0,3,12,15,48,51,60,63},{1,2,13,14,49,50,61,62},{4,7,8,11,52,55,56,59},..., dimensions={0} | all-to-all | bytes 131072 | tf_op jit(solution)/shard_map/all_to_all | solution.py:32
  55.2 1.5 %give.1 = bf16[1040,256]{1,0:T(8,128)(2,1)} custom-call(bf16[1024,1024]{1,0:T(8,128)(2,1)S(1)} %get-tuple-element.19.e_ref, bf16[8,128,256]{2,1,0:T(8,128)(2,1)S(1)} %all_to_all.26.q_ref, f32[8,16,128]{2,1,0:T(8,128)S(1)} %all_to_all.27.s_ref), custom_call_target="tpu_custom_call" | custom-call | flops 536870912 | tf_op jit(solution)/shard_map/give/pallas_call | solution.py:186
  56.8 0.0 collective-permute-start.1
  56.8 3.5 %all-to-all-start.2 = ((bf16[8,256,128]{2,1,0:T(8,128)(2,1)}), bf16[8,256,128]{2,1,0:T(8,128)(2,1)S(1)}, u32[]{:S(2)}, u32[]{:S(2)}) async-start(bf16[8,256,128]{2,1,0:T(8,128)(2,1)} %copy-done), calls=%async_computation.2 | async-start | bytes 1048576 | tf_op jit(solution)/shard_map/all_to_all | solution.py:32
  60.3 0.7 keep.1.w_ref
  61.0 0.0 copy-start.2
  61.0 0.0 copy-start.4
  61.0 0.0 collective-permute-done.1.got_ref
  61.0 2.0 %join.1 = bf16[8,144,256]{2,1,0:T(8,128)(2,1)} custom-call(f32[1024,256]{1,0:T(8,128)S(1)} %keep.1.w_ref, bf16[1040,256]{1,0:T(8,128)(2,1)} %collective-permute-done.1.got_ref, f32[8,16,128]{2,1,0:T(8,128)S(1)} %all_to_all.27.s_ref), custom_call_target="tpu_custom_call" | custom-call | tf_op jit(solution)/shard_map/join/pallas_call | solution.py:189
  63.1 11.9 %all-to-all-done.2.u_ref = bf16[8,256,128]{2,1,0:T(8,128)(2,1)S(1)} async-done(((bf16[8,256,128]{2,1,0:T(8,128)(2,1)}), bf16[8,256,128]{2,1,0:T(8,128)(2,1)S(1)}, u32[]{:S(2)}, u32[]{:S(2)}) %all-to-all-start.2) | async-done | bytes 524320 | tf_op jit(solution)/shard_map/all_to_all | solution.py:32
  74.9 3.5 %all-to-all-start.4 = ((bf16[8,144,256]{2,1,0:T(8,128)(2,1)}), bf16[8,144,256]{2,1,0:T(8,128)(2,1)S(1)}, u32[]{:S(2)}, u32[]{:S(2)}) async-start(bf16[8,144,256]{2,1,0:T(8,128)(2,1)} %join.1), calls=%async_computation.4 | async-start | bytes 1179648 | tf_op jit(solution)/shard_map/all_to_all | solution.py:32
  78.5 10.2 %all-to-all-done.4.w_ref = bf16[8,144,256]{2,1,0:T(8,128)(2,1)S(1)} async-done(((bf16[8,144,256]{2,1,0:T(8,128)(2,1)}), bf16[8,144,256]{2,1,0:T(8,128)(2,1)S(1)}, u32[]{:S(2)}, u32[]{:S(2)}) %all-to-all-start.4) | async-done | bytes 589856 | tf_op jit(solution)/shard_map/all_to_all | solution.py:32
  88.6 0.0 copy-done.2
  88.6 0.0 copy-done.4
  88.6 1.0 %final.1 = (f32[8,128]{1,0:T(8,128)S(1)}, f32[128,256]{1,0:T(8,128)}, f32[128,256]{1,0:T(8,128)}) custom-call(s32[1]{0:T(128)} %bitcast.high_ref, bf16[128,256]{1,0:T(8,128)(2,1)S(1)} %copy-done.2, bf16[128,256]{1,0:T(8,128)(2,1)S(1)} %copy-done.4, bf16[8,256,128]{2,1,0:T(8,128)(2,1)S(1)} %all-to-all-done.2.u_ref, ...), custom_call_target="tpu_custom_call" | custom-call | tf_op jit(solution)/shard_map/final/pallas_call | solution.py:191
  89.6 0.5 slice.3
Async XLA Ops:
  0.6 0.8 copy-start.1
  1.5 0.8 copy-start.3
  17.7 21.7 %collective-permute-start = (bf16[8,128,256]{2,1,0:T(8,128)(2,1)S(1)}, bf16[8,128,256]{2,1,0:T(8,128)(2,1)S(1)}, u32[]{:S(2)}, u32[]{:S(2)}) collective-permute-start(bf16[8,128,256]{2,1,0:T(8,128)(2,1)S(1)} %all_to_all.25.own_ref), channel_id=1, source_target_pairs={{0,64},{64,0},{1,65},{65,1},{2,66},{66,2},{3,67},{67,3},{4,68},{68... | collective-permute-start | bytes 1572872 | tf_op jit(solution)/shard_map/ppermute | solution.py:36
  42.5 0.8 copy-start
  56.8 4.2 %collective-permute-start.1 = (bf16[1040,256]{1,0:T(8,128)(2,1)}, bf16[1040,256]{1,0:T(8,128)(2,1)}, u32[]{:S(2)}, u32[]{:S(2)}) collective-permute-start(bf16[1040,256]{1,0:T(8,128)(2,1)} %give.1), channel_id=1, source_target_pairs={{0,64},{64,0},{1,65},{65,1},{2,66},{66,2},{3,67},{67,3},{4,68},{68... | collective-permute-start | bytes 1597448 | tf_op jit(solution)/shard_map/ppermute | solution.py:36
  56.8 18.2 %all-to-all-start.2 = ((bf16[8,256,128]{2,1,0:T(8,128)(2,1)}), bf16[8,256,128]{2,1,0:T(8,128)(2,1)S(1)}, u32[]{:S(2)}, u32[]{:S(2)}) async-start(bf16[8,256,128]{2,1,0:T(8,128)(2,1)} %copy-done), calls=%async_computation.2 | async-start | bytes 1048576 | tf_op jit(solution)/shard_map/all_to_all | solution.py:32
  61.0 27.7 %copy-start.2 = (bf16[128,256]{1,0:T(8,128)(2,1)S(1)}, bf16[128,256]{1,0:T(8,128)(2,1)}, u32[]{:S(2)}) copy-start(bf16[128,256]{1,0:T(8,128)(2,1)} %q_ref.3) | copy-start | bytes 196612
  61.0 27.7 %copy-start.4 = (bf16[128,256]{1,0:T(8,128)(2,1)S(1)}, bf16[128,256]{1,0:T(8,128)(2,1)}, u32[]{:S(2)}) copy-start(bf16[128,256]{1,0:T(8,128)(2,1)} %v_ref.3) | copy-start | bytes 196612
  74.9 13.7 %all-to-all-start.4 = ((bf16[8,144,256]{2,1,0:T(8,128)(2,1)}), bf16[8,144,256]{2,1,0:T(8,128)(2,1)S(1)}, u32[]{:S(2)}, u32[]{:S(2)}) async-start(bf16[8,144,256]{2,1,0:T(8,128)(2,1)} %join.1), calls=%async_computation.4 | async-start | bytes 1179648 | tf_op jit(solution)/shard_map/all_to_all | solution.py:32

commit v2 on v1

v2 whole, which is shorter than its diff:
```python
import math

import jax
import jax.numpy as jnp
from jax import lax
from jax.experimental import pallas as pl
from jax.experimental.pallas import tpu as pltpu
from jax.sharding import Mesh
from jax.sharding import PartitionSpec as P

AXES = ("blk", "z", "y", "x")
RING = {(0, 0): 0, (1, 0): 1, (1, 1): 2, (0, 1): 3}
BITS = [(a, b, c) for a in (0, 1) for b in (0, 1) for c in (0, 1)]
GROUP = 8
ROWS, D = 128, 256

sharpness = 0.05
tiny_square = 1e-12
log2_e = math.log2(math.e)
f32, bf16 = jnp.float32, jnp.bfloat16


def device_of(core, low, high):
    z, y, x = (RING[(l, h)] for l, h in zip(low, high))
    return ((core * 4 + z) * 4 + y) * 4 + x


def low_cubes(core):
    return [[device_of(core, low, high) for low in BITS] for high in BITS]


def high_cubes(core):
    return [[device_of(core, low, high) for high in BITS] for low in BITS]


BULK = low_cubes(0) + high_cubes(1)
HIGH = high_cubes(0) + high_cubes(1)


def exchange(pieces, groups):
    return lax.all_to_all(pieces, AXES, 0, 0, tiled=True, axis_index_groups=groups)


def swap_cores(value):
    return lax.ppermute(value, "blk", [(0, 1), (1, 0)])


def call(body, outs, name, flops=0, ins=None, scratch=()):
    spec = pl.BlockSpec(memory_space=pltpu.VMEM)
    return pl.pallas_call(
        body,
        out_shape=[jax.ShapeDtypeStruct(s, d) for s, d, *_ in outs],
        out_specs=[pl.BlockSpec(memory_space=o[2]) if len(o) > 2 else spec for o in outs],
        **({"in_specs": ins} if ins else {}),
        scratch_shapes=list(scratch),
        compiler_params=pltpu.CompilerParams(vmem_limit_bytes=24 * 2**20),
        cost_estimate=pl.CostEstimate(flops=flops, bytes_accessed=0, transcendentals=0),
        name=name,
    )


def unit(matrix):
    wide = matrix.astype(f32)
    length = jnp.sqrt(jnp.sum(wide * wide, axis=1, keepdims=True) + tiny_square)
    return wide / length, length


def norm_body(q_hbm, v_hbm, mine_ref, give_ref, pos_ref, q_ref, v_ref, sem):
    copies = [
        pltpu.make_async_copy(q_hbm, q_ref, sem.at[0]),
        pltpu.make_async_copy(v_hbm, v_ref, sem.at[1]),
    ]
    for c in copies:
        c.start()
    core = lax.axis_index("blk")
    copies[0].wait()
    q = unit(q_ref[...])[0].astype(bf16)
    copies[1].wait()
    v = unit(v_ref[...])[0].astype(bf16)
    total = jnp.sum(q.astype(f32) * v.astype(f32)) / sharpness
    pos_ref[...] = jnp.full((8, 128), total, f32)

    @pl.when(core == 0)
    def _():
        mine_ref[...] = v
        give_ref[...] = q

    @pl.when(core == 1)
    def _():
        mine_ref[...] = q
        give_ref[...] = v


def tile_body(mine_ref, got_ref, out_ref):
    core = lax.axis_index("blk")
    mine, got = mine_ref[...], got_ref[...]
    for k in range(GROUP):
        out_ref[k, core] = mine
        out_ref[k, 1 - core] = got


def score_body(mine_ref, got_ref, pos_ref, e_ref, q_ref, s_ref, u_ref, v_ref):
    core = lax.axis_index("blk")

    @pl.when(core == 0)
    def _():
        v_ref[...] = mine_ref[...]
        q_ref[...] = got_ref[:, 0]

    @pl.when(core == 1)
    def _():
        v_ref[...] = got_ref[...]
        q_ref[...] = mine_ref[:, 1]

    cols = GROUP * ROWS
    q = q_ref[...].reshape(cols, D)
    total = jnp.zeros((1, cols), f32)
    pull = None
    for k in range(GROUP):
        v = v_ref[k].reshape(2 * ROWS, D)
        t = lax.dot_general(v, q, (((1,), (1,)), ((), ())), preferred_element_type=f32)
        e = jnp.exp2(t * (log2_e / sharpness))
        total = total + jnp.sum(e, axis=0, keepdims=True)
        eb = e.astype(bf16)
        e_ref[k] = eb
        part = lax.dot_general(v, eb, (((0,), (0,)), ((), ())), preferred_element_type=f32)
        pull = part if pull is None else pull + part
    for k in range(GROUP):
        cut = slice(k * ROWS, (k + 1) * ROWS)
        u_ref[k, :, :ROWS] = pull[:ROWS, cut].astype(bf16)
        u_ref[k, :, ROWS:] = pull[ROWS:, cut].astype(bf16)
        for j in range(GROUP):
            s_ref[j, k : k + 1] = total[:, cut]
    for j in range(GROUP):
        s_ref[j, 8:16] = pos_ref[...]


def row_sums(s_ref):
    total = s_ref[0]
    for j in range(1, GROUP):
        total = total + s_ref[j]
    return total


def split(value):
    high = value.astype(bf16)
    low = (value - high.astype(f32)).astype(bf16)
    return jnp.concatenate([high.astype(f32), low.astype(f32)], axis=0).astype(bf16)


def weigh_body(e_ref, q_ref, s_ref, keep_ref, give_ref):
    sums = row_sums(s_ref)
    r = 1.0 / sums[:8]
    q = q_ref[...].reshape(GROUP * ROWS, D)
    for k in range(GROUP):
        parts = [
            (e_ref[k, :, j * ROWS : (j + 1) * ROWS].astype(f32) * r[j : j + 1]).astype(bf16)
            for j in range(GROUP)
        ]
        w = jnp.dot(jnp.concatenate(parts, axis=1), q, preferred_element_type=f32)
        keep_ref[k] = w
        give_ref[k * 256 : (k + 1) * 256] = w.astype(bf16)
    loss = jnp.sum(jnp.log(sums[:8])) - jnp.max(sums[8:9])
    give_ref[2048:2064] = split(jnp.full((8, D), loss, f32))


def join_body(keep_ref, got_ref, u_ref, got_u_ref, s_ref, out_ref):
    core = lax.axis_index("blk")

    @pl.when(core == 0)
    def _():
        for k in range(GROUP):
            out_ref[k, :256] = (keep_ref[k] + got_ref[k * 256 : (k + 1) * 256].astype(f32)).astype(bf16)

    @pl.when(core == 1)
    def _():
        for k in range(GROUP):
            out_ref[k, :128] = got_u_ref[k]
            out_ref[k, 128:256] = u_ref[k]

    sums = row_sums(s_ref)
    loss = jnp.sum(jnp.log(sums[:8])) - jnp.max(sums[8:9])
    got = got_ref[2048:2064].astype(f32)
    tail = split(got[:8] + got[8:] + loss)
    for k in range(GROUP):
        out_ref[k, 256:272] = tail


def sum_body(w_ref, keep_ref, give_ref):
    core = lax.axis_index("blk")

    def summed(first, rows):
        at = pl.ds(first, rows)
        total = w_ref[0, at].astype(f32)
        for k in range(1, GROUP):
            total = total + w_ref[k, at].astype(f32)
        return total

    tail = summed(256, 16)
    tail = tail[:8] + tail[8:]
    keep_ref[:128] = summed(pl.multiple_of(core * 128, 128), 128)
    give_ref[:128] = summed(pl.multiple_of((1 - core) * 128, 128), 128)
    keep_ref[128:136] = tail
    give_ref[128:136] = tail


def slope(pull, hat, direction, length):
    grad = (pull - hat) / sharpness
    along = jnp.sum(direction * grad, axis=1, keepdims=True)
    return (grad - direction * along) / length


def high_index():
    bit = lambda a: (lax.axis_index(a) >= 2).astype(jnp.int32)
    return bit("z") * 4 + bit("y") * 2 + bit("x")


def final_body(q_ref, v_ref, keep_ref, got_ref, s_ref, qs_ref, vs_ref, loss_ref):
    first = lax.axis_index("blk") == 0
    q, q_len = unit(q_ref[...])
    v, v_len = unit(v_ref[...])
    q_hat, v_hat = q.astype(bf16).astype(f32), v.astype(bf16).astype(f32)
    keep, got = keep_ref[...], got_ref[...]
    w = jnp.where(first, keep, got)
    u = jnp.where(first, got, keep)
    sums = row_sums(s_ref)[:8]
    mine = lax.broadcasted_iota(jnp.int32, sums.shape, 0) == high_index()
    own = jnp.sum(jnp.where(mine, sums, 0.0), axis=0, keepdims=True)
    u = jnp.concatenate([(u[:128, :128] / own).T, (u[:128, 128:] / own).T], axis=1)
    qs_ref[...] = slope(u, v_hat, q, q_len)
    vs_ref[...] = slope(w[:128], q_hat, v, v_len)
    loss_ref[0, 0] = jnp.max(w[128:136]) / (128 * 128)


def per_device(queries, items):
    anyspace = pl.BlockSpec(memory_space=pl.ANY)
    rows = (ROWS, D)
    mine, give, pos = call(
        norm_body,
        [(rows, bf16), (rows, bf16), ((8, 128), f32)],
        "norm",
        ins=[anyspace] * 2,
        scratch=[pltpu.VMEM(rows, bf16), pltpu.VMEM(rows, bf16), pltpu.SemaphoreType.DMA((2,))],
    )(queries, items)
    bulk = (GROUP, 2, ROWS, D)
    (tile,) = call(tile_body, [(bulk, bf16)], "tile")(mine, swap_cores(give))
    block = exchange(tile, BULK)
    flops = 2 * 2048 * 1024 * 256
    e, q, s, u = call(
        score_body,
        [
            ((GROUP, 256, 1024), bf16),
            ((GROUP, ROWS, D), bf16),
            ((GROUP, 16, 128), f32),
            ((GROUP, ROWS, D), bf16),
        ],
        "score",
        2 * flops,
        scratch=[pltpu.VMEM(bulk, bf16)],
    )(block, swap_cores(block), pos)
    got_u = swap_cores(u)
    sums = exchange(s, HIGH)
    keep, give = call(
        weigh_body, [((GROUP, 256, D), f32), ((2064, D), bf16)], "weigh", flops
    )(e, q, sums)
    (out,) = call(join_body, [((GROUP, 272, D), bf16)], "join")(keep, swap_cores(give), u, got_u, sums)
    out = exchange(out, BULK)
    keep, give = call(sum_body, [((136, D), f32), ((136, D), f32)], "sum")(out)
    q_slope, v_slope, loss = call(
        final_body, [(rows, f32), (rows, f32), ((1, 1), f32, pltpu.SMEM)], "final"
    )(queries, items, keep, swap_cores(give), sums)
    return loss.reshape(()), q_slope, v_slope


def solution(mesh):
    split = Mesh(mesh.devices.reshape(2, 4, 4, 4), AXES)
    rows = P(AXES, None)
    return jax.shard_map(
        per_device, mesh=split, in_specs=(rows, rows), out_specs=(P(), rows, rows), check_vma=False
    )
```

time: 90.6 us -> 70.4 us (0.78)
  the two profiles are of different devices: /device:TPU:0 before, /device:TPU:1 now
where the time goes in v2:
time: 70.4 us; the launch traced here: 70.1 us
  blocking collectives  50.5 us (72%)
  waiting for transfers between devices  7.86 us (11%)
  Pallas kernels  6.4 us (9%)
  starting transfers between devices  2.97 us (4%)
  local copies, waits for them, and re-layouts  1.68 us (2%)
    all_to_all x3, blocking collectives, exchange(): lax.all_to_all(pieces, AXES, 0, 0, tiled=True, axis_index_groups=groups)  50.5 us
    ppermute x5, waiting for transfers between devices, swap_cores(): return lax.ppermute(value, 'blk', [(0, 1), (1, 0)])  7.86 us
    pallas_call x1, Pallas kernels, per_device(): call(score_body, [((GROUP, 256, 1024), bf16), ((GROUP, ROWS, D), bf16), (...  3.16 us
    ppermute x5, starting transfers between devices, swap_cores(): return lax.ppermute(value, 'blk', [(0, 1), (1, 0)])  2.97 us
    unnamed x8, local copies, waits for them, and re-layouts  1.68 us
  transfers between devices with their start and end apart: 5, of which 4 were waited for; matrix products, arithmetic and copies ran while one was open for 0% of the time, Pallas kernels for 0%

profile of v2, /device:TPU:1, one launch (start us, length us, event | category | flops | bytes accessed | tf_op | source)
XLA Modules:
  0.0 70.1 jit_solution(1195603727560390803)
XLA Ops:
  0.6 0.0 copy-start
  0.6 0.8 %copy-done = bf16[128,256]{1,0:T(8,128)(2,1)S(1)} copy-done((bf16[128,256]{1,0:T(8,128)(2,1)S(1)}, bf16[128,256]{1,0:T(8,128)(2,1)}, u32[]{:S(2)}) %copy-start) | copy-done | bytes 65560
  1.5 0.0 copy-start.2
  1.5 0.8 %copy-done.2 = bf16[128,256]{1,0:T(8,128)(2,1)S(1)} copy-done((bf16[128,256]{1,0:T(8,128)(2,1)S(1)}, bf16[128,256]{1,0:T(8,128)(2,1)}, u32[]{:S(2)}) %copy-start.2) | copy-done | bytes 65560
  2.3 0.5 norm.1
  2.9 1.4 %collective-permute-start = (bf16[128,256]{1,0:T(8,128)(2,1)S(1)}, bf16[128,256]{1,0:T(8,128)(2,1)S(1)}, u32[]{:S(2)}, u32[]{:S(2)}) collective-permute-start(bf16[128,256]{1,0:T(8,128)(2,1)S(1)} %get-tuple-element.18), channel_id=1, source_target_pairs={{0,64},{64,0},{1,65},{65,1},{2,66},{66,2},{3,67},{67,3},{4,68},{68... | collective-permute-start | bytes 196616 | tf_op jit(solution)/shard_map/ppermute | solution.py:45
  4.3 0.9 %collective-permute-done.got_ref = bf16[128,256]{1,0:T(8,128)(2,1)S(1)} collective-permute-done((bf16[128,256]{1,0:T(8,128)(2,1)S(1)}, bf16[128,256]{1,0:T(8,128)(2,1)S(1)}, u32[]{:S(2)}, u32[]{:S(2)}) %collective-permute-start) | collective-permute-done | bytes 65568 | tf_op jit(solution)/shard_map/ppermute | solution.py:45
  5.2 0.1 tile.1
  5.3 23.3 %all_to_all.15.mine_ref = bf16[8,2,128,256]{3,2,1,0:T(8,128)(2,1)S(1)} all-to-all(bf16[8,2,128,256]{3,2,1,0:T(8,128)(2,1)S(1)} %tile.1), channel_id=1, replica_groups={{0,1,4,5,16,17,20,21},{3,2,7,6,19,18,23,22},{12,13,8,9,28,29,24,25},{15..., dimensions={0} | all-to-all | bytes 2097152 | tf_op jit(solution)/shard_map/all_to_all | solution.py:41
  28.6 0.0 collective-permute-start.1
  28.6 2.7 %collective-permute-done.1.got_ref = bf16[8,2,128,256]{3,2,1,0:T(8,128)(2,1)S(1)} collective-permute-done((bf16[8,2,128,256]{3,2,1,0:T(8,128)(2,1)S(1)}, bf16[8,2,128,256]{3,2,1,0:T(8,128)(2,1)S(1)}, u32[]{:S(2)}, u32[]{:S(2)}) %collective-permute-start.1) | collective-permute-done | bytes 1048608 | tf_op jit(solution)/shard_map/ppermute | solution.py:45
  31.2 3.2 %score.1 = (bf16[8,256,1024]{2,1,0:T(8,128)(2,1)S(1)}, bf16[8,128,256]{2,1,0:T(8,128)(2,1)S(1)}, f32[8,16,128]{2,1,0:T(8,128)S(1)}, bf16[8,128,256]{2,1,0:T(8,128)(2,1)S(1)}) custom-call(bf16[8,2,128,256]{3,2,1,0:T(8,128)(2,1)S(1)} %all_to_all.15.mine_ref, bf16[8,2,128,256]{3,2,1,0:T(8,128)(2,1)S(1)} %collective-permute-done.1.got_ref, ...), custom_call_target="tpu_custom_call" | custom-call | flops 2147483648 | tf_op jit(solution)/shard_map/score/pallas_call | solution.py:249
  34.4 10.8 %all_to_all.16.s_ref = f32[8,16,128]{2,1,0:T(8,128)S(1)} all-to-all(f32[8,16,128]{2,1,0:T(8,128)S(1)} %get-tuple-element.22), channel_id=1, replica_groups={{0,3,12,15,48,51,60,63},{1,2,13,14,49,50,61,62},{4,7,8,11,52,55,56,59},..., dimensions={0} | all-to-all | bytes 131072 | tf_op jit(solution)/shard_map/all_to_all | solution.py:41
  45.2 1.3 %weigh.1 = (f32[8,256,256]{2,1,0:T(8,128)S(1)}, bf16[2064,256]{1,0:T(8,128)(2,1)S(1)}) custom-call(bf16[8,256,1024]{2,1,0:T(8,128)(2,1)S(1)} %get-tuple-element.20.e_ref, bf16[8,128,256]{2,1,0:T(8,128)(2,1)S(1)} %get-tuple-element.21.q_ref, f32[8,16,128]{2,1,0:T(8,128)S(1)} %all_to_all.16.s_ref), custom_call_target="tpu_custom_call" | custom-call | flops 1073741824 | tf_op jit(solution)/shard_map/weigh/pallas_call | solution.py:263
  46.5 1.4 %collective-permute-start.2 = (bf16[2064,256]{1,0:T(8,128)(2,1)S(1)}, bf16[2064,256]{1,0:T(8,128)(2,1)S(1)}, u32[]{:S(2)}, u32[]{:S(2)}) collective-permute-start(bf16[2064,256]{1,0:T(8,128)(2,1)S(1)} %get-tuple-element.24), channel_id=1, source_target_pairs={{0,64},{64,0},{1,65},{65,1},{2,66},{66,2},{3,67},{67,3},{4,68},{68... | collective-permute-start | bytes 3170312 | tf_op jit(solution)/shard_map/ppermute | solution.py:45
  47.8 0.1 collective-permute-start.3
  47.9 3.0 %collective-permute-done.3.got_u_ref = bf16[8,128,256]{2,1,0:T(8,128)(2,1)S(1)} collective-permute-done((bf16[8,128,256]{2,1,0:T(8,128)(2,1)S(1)}, bf16[8,128,256]{2,1,0:T(8,128)(2,1)S(1)}, u32[]{:S(2)}, u32[]{:S(2)}) %collective-permute-start.3) | collective-permute-done | bytes 524320 | tf_op jit(solution)/shard_map/ppermute | solution.py:45
  50.9 0.0 collective-permute-done.2.got_ref
  50.9 0.2 join.1
  51.1 16.4 %all_to_all.17.w_ref = bf16[8,272,256]{2,1,0:T(8,128)(2,1)S(1)} all-to-all(bf16[8,272,256]{2,1,0:T(8,128)(2,1)S(1)} %join.1), channel_id=1, replica_groups={{0,1,4,5,16,17,20,21},{3,2,7,6,19,18,23,22},{12,13,8,9,28,29,24,25},{15..., dimensions={0} | all-to-all | bytes 2228224 | tf_op jit(solution)/shard_map/all_to_all | solution.py:41
  67.5 0.0 copy-start.1
  67.5 0.0 copy-start.3
  67.5 0.1 sum.1
  67.7 0.1 collective-permute-start.4
  67.8 1.3 %collective-permute-done.4.got_ref = f32[136,256]{1,0:T(8,128)S(1)} collective-permute-done((f32[136,256]{1,0:T(8,128)S(1)}, f32[136,256]{1,0:T(8,128)S(1)}, u32[]{:S(2)}, u32[]{:S(2)}) %collective-permute-start.4) | collective-permute-done | bytes 139296 | tf_op jit(solution)/shard_map/ppermute | solution.py:45
  69.1 0.0 copy-done.1
  69.1 0.0 copy-done.3
  69.1 1.0 %final.1 = (f32[128,256]{1,0:T(8,128)}, f32[128,256]{1,0:T(8,128)}, f32[1,1]{1,0:T(1,128)}) custom-call(bf16[128,256]{1,0:T(8,128)(2,1)S(1)} %copy-done.1, bf16[128,256]{1,0:T(8,128)(2,1)S(1)} %copy-done.3, f32[136,256]{1,0:T(8,128)S(1)} %get-tuple-element.26.keep_ref, f32[136,256]{1,0:T(8,128)S(1)} %collective-permute-done.4.got_ref, ...), custom_call_target="tpu_custom_call" | custom-call | tf_op jit(solution)/shard_map/final/pallas_call | solution.py:269
Async XLA Ops:
  0.6 0.8 %copy-start = (bf16[128,256]{1,0:T(8,128)(2,1)S(1)}, bf16[128,256]{1,0:T(8,128)(2,1)}, u32[]{:S(2)}) copy-start(bf16[128,256]{1,0:T(8,128)(2,1)} %q_ref.1) | copy-start | bytes 196612
  1.5 0.8 %copy-start.2 = (bf16[128,256]{1,0:T(8,128)(2,1)S(1)}, bf16[128,256]{1,0:T(8,128)(2,1)}, u32[]{:S(2)}) copy-start(bf16[128,256]{1,0:T(8,128)(2,1)} %v_ref.1) | copy-start | bytes 196612
  2.9 2.3 %collective-permute-start = (bf16[128,256]{1,0:T(8,128)(2,1)S(1)}, bf16[128,256]{1,0:T(8,128)(2,1)S(1)}, u32[]{:S(2)}, u32[]{:S(2)}) collective-permute-start(bf16[128,256]{1,0:T(8,128)(2,1)S(1)} %get-tuple-element.18), channel_id=1, source_target_pairs={{0,64},{64,0},{1,65},{65,1},{2,66},{66,2},{3,67},{67,3},{4,68},{68... | collective-permute-start | bytes 196616 | tf_op jit(solution)/shard_map/ppermute | solution.py:45
  28.6 2.7 %collective-permute-start.1 = (bf16[8,2,128,256]{3,2,1,0:T(8,128)(2,1)S(1)}, bf16[8,2,128,256]{3,2,1,0:T(8,128)(2,1)S(1)}, u32[]{:S(2)}, u32[]{:S(2)}) collective-permute-start(bf16[8,2,128,256]{3,2,1,0:T(8,128)(2,1)S(1)} %all_to_all.15.mine_ref), channel_id=1, source_target_pairs={{0,64},{64,0},{1,65},{65,1},{2,66},{66,2},{3,67},{67,3},{4,68},{68... | collective-permute-start | bytes 3145736 | tf_op jit(solution)/shard_map/ppermute | solution.py:45
  46.5 4.4 %collective-permute-start.2 = (bf16[2064,256]{1,0:T(8,128)(2,1)S(1)}, bf16[2064,256]{1,0:T(8,128)(2,1)S(1)}, u32[]{:S(2)}, u32[]{:S(2)}) collective-permute-start(bf16[2064,256]{1,0:T(8,128)(2,1)S(1)} %get-tuple-element.24), channel_id=1, source_target_pairs={{0,64},{64,0},{1,65},{65,1},{2,66},{66,2},{3,67},{67,3},{4,68},{68... | collective-permute-start | bytes 3170312 | tf_op jit(solution)/shard_map/ppermute | solution.py:45
  47.8 3.0 %collective-permute-start.3 = (bf16[8,128,256]{2,1,0:T(8,128)(2,1)S(1)}, bf16[8,128,256]{2,1,0:T(8,128)(2,1)S(1)}, u32[]{:S(2)}, u32[]{:S(2)}) collective-permute-start(bf16[8,128,256]{2,1,0:T(8,128)(2,1)S(1)} %get-tuple-element.25.u_ref), channel_id=1, source_target_pairs={{0,64},{64,0},{1,65},{65,1},{2,66},{66,2},{3,67},{67,3},{4,68},{68... | collective-permute-start | bytes 1572872 | tf_op jit(solution)/shard_map/ppermute | solution.py:45
  67.5 1.6 %copy-start.1 = (bf16[128,256]{1,0:T(8,128)(2,1)S(1)}, bf16[128,256]{1,0:T(8,128)(2,1)}, u32[]{:S(2)}) copy-start(bf16[128,256]{1,0:T(8,128)(2,1)} %q_ref.1) | copy-start | bytes 196612
  67.5 1.6 %copy-start.3 = (bf16[128,256]{1,0:T(8,128)(2,1)S(1)}, bf16[128,256]{1,0:T(8,128)(2,1)}, u32[]{:S(2)}) copy-start(bf16[128,256]{1,0:T(8,128)(2,1)} %v_ref.1) | copy-start | bytes 196612
  67.7 1.4 %collective-permute-start.4 = (f32[136,256]{1,0:T(8,128)S(1)}, f32[136,256]{1,0:T(8,128)S(1)}, u32[]{:S(2)}, u32[]{:S(2)}) collective-permute-start(f32[136,256]{1,0:T(8,128)S(1)} %get-tuple-element.27), channel_id=1, source_target_pairs={{0,64},{64,0},{1,65},{65,1},{2,66},{66,2},{3,67},{67,3},{4,68},{68... | collective-permute-start | bytes 417800 | tf_op jit(solution)/shard_map/ppermute | solution.py:45

commit v3 on v2

--- a/solution.py
+++ b/solution.py
@@ -1,3 +1,4 @@
+import functools
 import math
 
 import jax
@@ -127,8 +128,9 @@
         pull = part if pull is None else pull + part
     for k in range(GROUP):
         cut = slice(k * ROWS, (k + 1) * ROWS)
-        u_ref[k, :, :ROWS] = pull[:ROWS, cut].astype(bf16)
-        u_ref[k, :, ROWS:] = pull[ROWS:, cut].astype(bf16)
+        rows = slice(k * ROWS, (k + 1) * ROWS)
+        u_ref[rows, :ROWS] = pull[:ROWS, cut].astype(bf16)
+        u_ref[rows, ROWS:] = pull[ROWS:, cut].astype(bf16)
         for j in range(GROUP):
             s_ref[j, k : k + 1] = total[:, cut]
     for j in range(GROUP):
@@ -148,40 +150,51 @@
     return jnp.concatenate([high.astype(f32), low.astype(f32)], axis=0).astype(bf16)
 
 
-def weigh_body(e_ref, q_ref, s_ref, keep_ref, give_ref):
+def loss_part(sums):
+    return jnp.sum(jnp.log(sums[:8])) - jnp.max(sums[8:9])
+
+
+def weigh_body(first, *refs):
+    *u_ref, e_ref, q_ref, s_ref, keep_ref, give_ref = refs
+    core = lax.axis_index("blk")
     sums = row_sums(s_ref)
     r = 1.0 / sums[:8]
     q = q_ref[...].reshape(GROUP * ROWS, D)
-    for k in range(GROUP):
+    for k in range(GROUP // 2):
         parts = [
-            (e_ref[k, :, j * ROWS : (j + 1) * ROWS].astype(f32) * r[j : j + 1]).astype(bf16)
+            (e_ref[first + k, :, j * ROWS : (j + 1) * ROWS].astype(f32) * r[j : j + 1]).astype(bf16)
             for j in range(GROUP)
         ]
         w = jnp.dot(jnp.concatenate(parts, axis=1), q, preferred_element_type=f32)
         keep_ref[k] = w
         give_ref[k * 256 : (k + 1) * 256] = w.astype(bf16)
-    loss = jnp.sum(jnp.log(sums[:8])) - jnp.max(sums[8:9])
-    give_ref[2048:2064] = split(jnp.full((8, D), loss, f32))
-
-
-def join_body(keep_ref, got_ref, u_ref, got_u_ref, s_ref, out_ref):
+    if u_ref:
+        give_ref[1024:1040] = split(jnp.full((8, D), loss_part(sums), f32))
+
+        @pl.when(core == 0)
+        def _():
+            give_ref[:1024] = u_ref[0][...]
+
+
+def join_body(keep0_ref, keep1_ref, got0_ref, got1_ref, u_ref, s_ref, out_ref):
     core = lax.axis_index("blk")
 
     @pl.when(core == 0)
     def _():
         for k in range(GROUP):
-            out_ref[k, :256] = (keep_ref[k] + got_ref[k * 256 : (k + 1) * 256].astype(f32)).astype(bf16)
+            keep, got = (keep0_ref, got0_ref) if k < 4 else (keep1_ref, got1_ref)
+            i = k % 4
+            out_ref[k, :256] = (keep[i] + got[i * 256 : (i + 1) * 256].astype(f32)).astype(bf16)
 
     @pl.when(core == 1)
     def _():
         for k in range(GROUP):
-            out_ref[k, :128] = got_u_ref[k]
-            out_ref[k, 128:256] = u_ref[k]
-
-    sums = row_sums(s_ref)
-    loss = jnp.sum(jnp.log(sums[:8])) - jnp.max(sums[8:9])
-    got = got_ref[2048:2064].astype(f32)
-    tail = split(got[:8] + got[8:] + loss)
+            rows = slice(k * ROWS, (k + 1) * ROWS)
+            out_ref[k, :128] = got0_ref[rows]
+            out_ref[k, 128:256] = u_ref[rows]
+
+    got = got0_ref[1024:1040].astype(f32)
+    tail = split(got[:8] + got[8:] + loss_part(row_sums(s_ref)))
     for k in range(GROUP):
         out_ref[k, 256:272] = tail
 
@@ -233,7 +246,7 @@
 
 
 def per_device(queries, items):
-    anyspace = pl.BlockSpec(memory_space=pl.ANY)
+    anyspace = pl.BlockSpec(memory_space=pltpu.HBM)
     rows = (ROWS, D)
     mine, give, pos = call(
         norm_body,
@@ -241,7 +254,7 @@
         "norm",
         ins=[anyspace] * 2,
         scratch=[pltpu.VMEM(rows, bf16), pltpu.VMEM(rows, bf16), pltpu.SemaphoreType.DMA((2,))],
-    )(queries, items)
+    )(*(pltpu.with_memory_space_constraint(a, pltpu.HBM) for a in (queries, items)))
     bulk = (GROUP, 2, ROWS, D)
     (tile,) = call(tile_body, [(bulk, bf16)], "tile")(mine, swap_cores(give))
     block = exchange(tile, BULK)
@@ -252,18 +265,24 @@
             ((GROUP, 256, 1024), bf16),
             ((GROUP, ROWS, D), bf16),
             ((GROUP, 16, 128), f32),
-            ((GROUP, ROWS, D), bf16),
+            ((GROUP * ROWS, D), bf16),
         ],
         "score",
         2 * flops,
         scratch=[pltpu.VMEM(bulk, bf16)],
     )(block, swap_cores(block), pos)
-    got_u = swap_cores(u)
     sums = exchange(s, HIGH)
-    keep, give = call(
-        weigh_body, [((GROUP, 256, D), f32), ((2064, D), bf16)], "weigh", flops
-    )(e, q, sums)
-    (out,) = call(join_body, [((GROUP, 272, D), bf16)], "join")(keep, swap_cores(give), u, got_u, sums)
+    keep, got = [], []
+    for half in (0, 1):
+        k, g = call(
+            functools.partial(weigh_body, half * 4),
+            [((4, 256, D), f32), ((1040 - 16 * half, D), bf16)],
+            f"weigh{half}",
+            flops // 2,
+        )(*([u] if half == 0 else []), e, q, sums)
+        keep.append(k)
+        got.append(swap_cores(g))
+    (out,) = call(join_body, [((GROUP, 272, D), bf16)], "join")(*keep, *got, u, sums)
     out = exchange(out, BULK)
     keep, give = call(sum_body, [((136, D), f32), ((136, D), f32)], "sum")(out)
     q_slope, v_slope, loss = call(

time: 70.4 us -> 68.5 us (0.973)
  local copies, waits for them, and re-layouts: 1.68 us -> 0.01 us
  waiting for transfers between devices: 7.86 us -> 6.81 us
  Pallas kernels: 6.4 us -> 7.25 us
    unnamed x8 -> x4, local copies, waits for them, and re-layouts: 1.68 us -> 0.01 us
    ppermute x5, waiting for transfers between devices: 7.86 us -> 6.81 us  [swap_cores(): return lax.ppermute(value, 'blk', [(0, 1), (1, 0)])]
    pallas_call x2 -> x3, Pallas kernels: 1.5 us -> 1.65 us  [the longest x2 1.44 us: per_device(): call(functools.partial(weigh_body, half * 4), [((4, 256, D), f32), ((1040...]
  transfers between devices with their start and end apart: 5 -> 5, of which waited for: 4 -> 4; matrix products, arithmetic and copies ran while one was open for 0% -> 0% of each run, Pallas kernels for 0% -> 1%
where the time goes in v3:
time: 68.5 us; the launch traced here: 68.2 us
  blocking collectives  50.5 us (74%)
  Pallas kernels  7.25 us (11%)
  waiting for transfers between devices  6.81 us (10%)
  starting transfers between devices  3 us (4%)
    all_to_all x3, blocking collectives, exchange(): lax.all_to_all(pieces, AXES, 0, 0, tiled=True, axis_index_groups=groups)  50.5 us
    ppermute x5, waiting for transfers between devices, swap_cores(): return lax.ppermute(value, 'blk', [(0, 1), (1, 0)])  6.81 us
    pallas_call x1, Pallas kernels, per_device(): call(score_body, [((GROUP, 256, 1024), bf16), ((GROUP, ROWS, D), bf16), (...  3.16 us
    ppermute x5, starting transfers between devices, swap_cores(): return lax.ppermute(value, 'blk', [(0, 1), (1, 0)])  3 us
    pallas_call x2, Pallas kernels, per_device(): call(functools.partial(weigh_body, half * 4), [((4, 256, D), f32), ((1040...  1.44 us
  transfers between devices with their start and end apart: 5, of which 4 were waited for; matrix products, arithmetic and copies ran while one was open for 0% of the time, Pallas kernels for 1%

profile of v3, /device:TPU:1, one launch (start us, length us, event | category | flops | bytes accessed | tf_op | source)
XLA Modules:
  0.0 68.2 jit_solution(3551779744614678944)
XLA Ops:
  0.6 1.2 %norm.1 = (bf16[128,256]{1,0:T(8,128)(2,1)S(1)}, bf16[128,256]{1,0:T(8,128)(2,1)S(1)}, f32[8,128]{1,0:T(8,128)S(1)}) custom-call(bf16[128,256]{1,0:T(8,128)(2,1)} %q_ref.1, bf16[128,256]{1,0:T(8,128)(2,1)} %v_ref.1), custom_call_target="tpu_custom_call" | custom-call | tf_op jit(solution)/shard_map/norm/pallas_call | solution.py:251
  1.9 1.4 %collective-permute-start = (bf16[128,256]{1,0:T(8,128)(2,1)S(1)}, bf16[128,256]{1,0:T(8,128)(2,1)S(1)}, u32[]{:S(2)}, u32[]{:S(2)}) collective-permute-start(bf16[128,256]{1,0:T(8,128)(2,1)S(1)} %get-tuple-element.20), channel_id=1, source_target_pairs={{0,64},{64,0},{1,65},{65,1},{2,66},{66,2},{3,67},{67,3},{4,68},{68... | collective-permute-start | bytes 196616 | tf_op jit(solution)/shard_map/ppermute | solution.py:46
  3.3 0.9 %collective-permute-done.got_ref = bf16[128,256]{1,0:T(8,128)(2,1)S(1)} collective-permute-done((bf16[128,256]{1,0:T(8,128)(2,1)S(1)}, bf16[128,256]{1,0:T(8,128)(2,1)S(1)}, u32[]{:S(2)}, u32[]{:S(2)}) %collective-permute-start) | collective-permute-done | bytes 65568 | tf_op jit(solution)/shard_map/ppermute | solution.py:46
  4.2 0.1 tile.1
  4.3 23.3 %all_to_all.15.mine_ref = bf16[8,2,128,256]{3,2,1,0:T(8,128)(2,1)S(1)} all-to-all(bf16[8,2,128,256]{3,2,1,0:T(8,128)(2,1)S(1)} %tile.1), channel_id=1, replica_groups={{0,1,4,5,16,17,20,21},{3,2,7,6,19,18,23,22},{12,13,8,9,28,29,24,25},{15..., dimensions={0} | all-to-all | bytes 2097152 | tf_op jit(solution)/shard_map/all_to_all | solution.py:42
  27.6 0.0 collective-permute-start.1
  27.6 2.7 %collective-permute-done.1.got_ref = bf16[8,2,128,256]{3,2,1,0:T(8,128)(2,1)S(1)} collective-permute-done((bf16[8,2,128,256]{3,2,1,0:T(8,128)(2,1)S(1)}, bf16[8,2,128,256]{3,2,1,0:T(8,128)(2,1)S(1)}, u32[]{:S(2)}, u32[]{:S(2)}) %collective-permute-start.1) | collective-permute-done | bytes 1048608 | tf_op jit(solution)/shard_map/ppermute | solution.py:46
  30.2 3.2 %score.1 = (bf16[8,256,1024]{2,1,0:T(8,128)(2,1)S(1)}, bf16[8,128,256]{2,1,0:T(8,128)(2,1)S(1)}, f32[8,16,128]{2,1,0:T(8,128)S(1)}, bf16[1024,256]{1,0:T(8,128)(2,1)S(1)}) custom-call(bf16[8,2,128,256]{3,2,1,0:T(8,128)(2,1)S(1)} %all_to_all.15.mine_ref, bf16[8,2,128,256]{3,2,1,0:T(8,128)(2,1)S(1)} %collective-permute-done.1.got_ref, ...), custom_call_target="tpu_custom_call" | custom-call | flops 2147483648 | tf_op jit(solution)/shard_map/score/pallas_call | solution.py:262
  33.4 10.8 %all_to_all.16.refs_3_.refs_2_.s_ref = f32[8,16,128]{2,1,0:T(8,128)S(1)} all-to-all(f32[8,16,128]{2,1,0:T(8,128)S(1)} %get-tuple-element.25), channel_id=1, replica_groups={{0,3,12,15,48,51,60,63},{1,2,13,14,49,50,61,62},{4,7,8,11,52,55,56,59},..., dimensions={0} | all-to-all | bytes 131072 | tf_op jit(solution)/shard_map/all_to_all | solution.py:42
  44.2 0.7 %weigh0.1 = (f32[4,256,256]{2,1,0:T(8,128)S(1)}, bf16[1040,256]{1,0:T(8,128)(2,1)S(1)}) custom-call(bf16[1024,256]{1,0:T(8,128)(2,1)S(1)} %get-tuple-element.22.refs_0_.u_ref, bf16[8,256,1024]{2,1,0:T(8,128)(2,1)S(1)} %get-tuple-element.23.refs_1_.refs_0_, bf16[8,128,256]{2,1,0:T(8,128)(2,1)S(1)} %get-tuple-element.24.refs_2_.refs_1_, ...), custom_call_target="tpu_custom_call" | custom-call | flops 536870912 | tf_op jit(solution)/shard_map/weigh0/pallas_call | solution.py:277
  44.9 1.4 %collective-permute-start.2 = (bf16[1040,256]{1,0:T(8,128)(2,1)S(1)}, bf16[1040,256]{1,0:T(8,128)(2,1)S(1)}, u32[]{:S(2)}, u32[]{:S(2)}) collective-permute-start(bf16[1040,256]{1,0:T(8,128)(2,1)S(1)} %get-tuple-element.28), channel_id=1, source_target_pairs={{0,64},{64,0},{1,65},{65,1},{2,66},{66,2},{3,67},{67,3},{4,68},{68... | collective-permute-start | bytes 1597448 | tf_op jit(solution)/shard_map/ppermute | solution.py:46
  46.3 0.7 %weigh1.1 = (f32[4,256,256]{2,1,0:T(8,128)S(1)}, bf16[1024,256]{1,0:T(8,128)(2,1)S(1)}) custom-call(bf16[8,256,1024]{2,1,0:T(8,128)(2,1)S(1)} %get-tuple-element.23.refs_1_.refs_0_, bf16[8,128,256]{2,1,0:T(8,128)(2,1)S(1)} %get-tuple-element.24.refs_2_.refs_1_, f32[8,16,128]{2,1,0:T(8,128)S(1)} %all_to_all.16.refs_3_.refs_2_.s_ref), custom_call_target="tpu_custom_call" | custom-call | flops 536870912 | tf_op jit(solution)/shard_map/weigh1/pallas_call | solution.py:277
  47.0 0.1 collective-permute-start.3
  47.1 1.9 %collective-permute-done.3.got1_ref = bf16[1024,256]{1,0:T(8,128)(2,1)S(1)} collective-permute-done((bf16[1024,256]{1,0:T(8,128)(2,1)S(1)}, bf16[1024,256]{1,0:T(8,128)(2,1)S(1)}, u32[]{:S(2)}, u32[]{:S(2)}) %collective-permute-start.3) | collective-permute-done | bytes 524320 | tf_op jit(solution)/shard_map/ppermute | solution.py:46
  49.0 0.0 collective-permute-done.2.got0_ref
  49.0 0.2 join.1
  49.2 16.4 %all_to_all.17.w_ref = bf16[8,272,256]{2,1,0:T(8,128)(2,1)S(1)} all-to-all(bf16[8,272,256]{2,1,0:T(8,128)(2,1)S(1)} %join.1), channel_id=1, replica_groups={{0,1,4,5,16,17,20,21},{3,2,7,6,19,18,23,22},{12,13,8,9,28,29,24,25},{15..., dimensions={0} | all-to-all | bytes 2228224 | tf_op jit(solution)/shard_map/all_to_all | solution.py:42
  65.7 0.0 copy-start
  65.7 0.0 copy-start.1
  65.7 0.1 sum.1
  65.8 0.1 collective-permute-start.4
  65.9 1.3 %collective-permute-done.4.got_ref = f32[136,256]{1,0:T(8,128)S(1)} collective-permute-done((f32[136,256]{1,0:T(8,128)S(1)}, f32[136,256]{1,0:T(8,128)S(1)}, u32[]{:S(2)}, u32[]{:S(2)}) %collective-permute-start.4) | collective-permute-done | bytes 139296 | tf_op jit(solution)/shard_map/ppermute | solution.py:46
  67.3 0.0 copy-done
  67.3 0.0 copy-done.1
  67.3 1.0 %final.1 = (f32[128,256]{1,0:T(8,128)}, f32[128,256]{1,0:T(8,128)}, f32[1,1]{1,0:T(1,128)}) custom-call(bf16[128,256]{1,0:T(8,128)(2,1)S(1)} %copy-done, bf16[128,256]{1,0:T(8,128)(2,1)S(1)} %copy-done.1, f32[136,256]{1,0:T(8,128)S(1)} %get-tuple-element.30.keep_ref, f32[136,256]{1,0:T(8,128)S(1)} %collective-permute-done.4.got_ref, ...), custom_call_target="tpu_custom_call" | custom-call | tf_op jit(solution)/shard_map/final/pallas_call | solution.py:288
Async XLA Ops:
  1.9 2.3 %collective-permute-start = (bf16[128,256]{1,0:T(8,128)(2,1)S(1)}, bf16[128,256]{1,0:T(8,128)(2,1)S(1)}, u32[]{:S(2)}, u32[]{:S(2)}) collective-permute-start(bf16[128,256]{1,0:T(8,128)(2,1)S(1)} %get-tuple-element.20), channel_id=1, source_target_pairs={{0,64},{64,0},{1,65},{65,1},{2,66},{66,2},{3,67},{67,3},{4,68},{68... | collective-permute-start | bytes 196616 | tf_op jit(solution)/shard_map/ppermute | solution.py:46
  27.6 2.7 %collective-permute-start.1 = (bf16[8,2,128,256]{3,2,1,0:T(8,128)(2,1)S(1)}, bf16[8,2,128,256]{3,2,1,0:T(8,128)(2,1)S(1)}, u32[]{:S(2)}, u32[]{:S(2)}) collective-permute-start(bf16[8,2,128,256]{3,2,1,0:T(8,128)(2,1)S(1)} %all_to_all.15.mine_ref), channel_id=1, source_target_pairs={{0,64},{64,0},{1,65},{65,1},{2,66},{66,2},{3,67},{67,3},{4,68},{68... | collective-permute-start | bytes 3145736 | tf_op jit(solution)/shard_map/ppermute | solution.py:46
  44.9 4.1 %collective-permute-start.2 = (bf16[1040,256]{1,0:T(8,128)(2,1)S(1)}, bf16[1040,256]{1,0:T(8,128)(2,1)S(1)}, u32[]{:S(2)}, u32[]{:S(2)}) collective-permute-start(bf16[1040,256]{1,0:T(8,128)(2,1)S(1)} %get-tuple-element.28), channel_id=1, source_target_pairs={{0,64},{64,0},{1,65},{65,1},{2,66},{66,2},{3,67},{67,3},{4,68},{68... | collective-permute-start | bytes 1597448 | tf_op jit(solution)/shard_map/ppermute | solution.py:46
  47.0 2.0 %collective-permute-start.3 = (bf16[1024,256]{1,0:T(8,128)(2,1)S(1)}, bf16[1024,256]{1,0:T(8,128)(2,1)S(1)}, u32[]{:S(2)}, u32[]{:S(2)}) collective-permute-start(bf16[1024,256]{1,0:T(8,128)(2,1)S(1)} %get-tuple-element.29), channel_id=1, source_target_pairs={{0,64},{64,0},{1,65},{65,1},{2,66},{66,2},{3,67},{67,3},{4,68},{68... | collective-permute-start | bytes 1572872 | tf_op jit(solution)/shard_map/ppermute | solution.py:46
  65.7 1.6 %copy-start = (bf16[128,256]{1,0:T(8,128)(2,1)S(1)}, bf16[128,256]{1,0:T(8,128)(2,1)}, u32[]{:S(2)}) copy-start(bf16[128,256]{1,0:T(8,128)(2,1)} %q_ref.1) | copy-start | bytes 196612
  65.7 1.6 %copy-start.1 = (bf16[128,256]{1,0:T(8,128)(2,1)S(1)}, bf16[128,256]{1,0:T(8,128)(2,1)}, u32[]{:S(2)}) copy-start(bf16[128,256]{1,0:T(8,128)(2,1)} %v_ref.1) | copy-start | bytes 196612
  65.8 1.4 %collective-permute-start.4 = (f32[136,256]{1,0:T(8,128)S(1)}, f32[136,256]{1,0:T(8,128)S(1)}, u32[]{:S(2)}, u32[]{:S(2)}) collective-permute-start(f32[136,256]{1,0:T(8,128)S(1)} %get-tuple-element.31), channel_id=1, source_target_pairs={{0,64},{64,0},{1,65},{65,1},{2,66},{66,2},{3,67},{67,3},{4,68},{68... | collective-permute-start | bytes 417800 | tf_op jit(solution)/shard_map/ppermute | solution.py:46

commit v4 on v3

--- a/solution.py
+++ b/solution.py
@@ -34,8 +34,8 @@
     return [[device_of(core, low, high) for high in BITS] for low in BITS]
 
 
-BULK = low_cubes(0) + high_cubes(1)
-HIGH = high_cubes(0) + high_cubes(1)
+BULK = high_cubes(0) + low_cubes(1)
+LOW = low_cubes(0) + low_cubes(1)
 
 
 def exchange(pieces, groups):
@@ -223,9 +223,10 @@
     return (grad - direction * along) / length
 
 
-def high_index():
-    bit = lambda a: (lax.axis_index(a) >= 2).astype(jnp.int32)
-    return bit("z") * 4 + bit("y") * 2 + bit("x")
+def low_index():
+    at = [lax.axis_index(a) for a in "zyx"]
+    z, y, x = (((a == 1) | (a == 2)).astype(jnp.int32) for a in at)
+    return z * 4 + y * 2 + x
 
 
 def final_body(q_ref, v_ref, keep_ref, got_ref, s_ref, qs_ref, vs_ref, loss_ref):
@@ -237,7 +238,7 @@
     w = jnp.where(first, keep, got)
     u = jnp.where(first, got, keep)
     sums = row_sums(s_ref)[:8]
-    mine = lax.broadcasted_iota(jnp.int32, sums.shape, 0) == high_index()
+    mine = lax.broadcasted_iota(jnp.int32, sums.shape, 0) == low_index()
     own = jnp.sum(jnp.where(mine, sums, 0.0), axis=0, keepdims=True)
     u = jnp.concatenate([(u[:128, :128] / own).T, (u[:128, 128:] / own).T], axis=1)
     qs_ref[...] = slope(u, v_hat, q, q_len)
@@ -271,7 +272,7 @@
         2 * flops,
         scratch=[pltpu.VMEM(bulk, bf16)],
     )(block, swap_cores(block), pos)
-    sums = exchange(s, HIGH)
+    sums = exchange(s, LOW)
     keep, got = [], []
     for half in (0, 1):
         k, g = call(

time: 68.5 us -> 67.6 us (0.987)
  blocking collectives: 50.5 us -> 35.1 us
  starting transfers between devices: 3 us -> 18.2 us
  waiting for transfers between devices: 6.81 us -> 6.08 us
    all_to_all x3, blocking collectives: 50.5 us -> 35.1 us  [exchange(): lax.all_to_all(pieces, AXES, 0, 0, tiled=True, axis_index_groups=groups)]
    ppermute x5, starting transfers between devices: 3 us -> 18.2 us  [swap_cores(): return lax.ppermute(value, 'blk', [(0, 1), (1, 0)])]
    ppermute x5, waiting for transfers between devices: 6.81 us -> 6.08 us  [swap_cores(): return lax.ppermute(value, 'blk', [(0, 1), (1, 0)])]
where the time goes in v4:
time: 67.6 us; the launch traced here: 67.3 us
  blocking collectives  35.1 us (52%)
  starting transfers between devices  18.2 us (27%)
  Pallas kernels  7.24 us (11%)
  waiting for transfers between devices  6.08 us (9%)
  between operations  0.68 us (1%)
    all_to_all x3, blocking collectives, exchange(): lax.all_to_all(pieces, AXES, 0, 0, tiled=True, axis_index_groups=groups)  35.1 us
    ppermute x5, starting transfers between devices, swap_cores(): return lax.ppermute(value, 'blk', [(0, 1), (1, 0)])  18.2 us
    ppermute x5, waiting for transfers between devices, swap_cores(): return lax.ppermute(value, 'blk', [(0, 1), (1, 0)])  6.08 us
    pallas_call x1, Pallas kernels, per_device(): call(score_body, [((GROUP, 256, 1024), bf16), ((GROUP, ROWS, D), bf16), (...  3.15 us
    pallas_call x2, Pallas kernels, per_device(): call(functools.partial(weigh_body, half * 4), [((4, 256, D), f32), ((1040...  1.43 us
  transfers between devices with their start and end apart: 5, of which 4 were waited for; matrix products, arithmetic and copies ran while one was open for 0% of the time, Pallas kernels for 1%

profile of v4, /device:TPU:1, one launch (start us, length us, event | category | flops | bytes accessed | tf_op | source)
XLA Modules:
  0.0 67.3 jit_solution(13270386681875080874)
XLA Ops:
  0.6 1.2 %norm.1 = (bf16[128,256]{1,0:T(8,128)(2,1)S(1)}, bf16[128,256]{1,0:T(8,128)(2,1)S(1)}, f32[8,128]{1,0:T(8,128)S(1)}) custom-call(bf16[128,256]{1,0:T(8,128)(2,1)} %q_ref.1, bf16[128,256]{1,0:T(8,128)(2,1)} %v_ref.1), custom_call_target="tpu_custom_call" | custom-call | tf_op jit(solution)/shard_map/norm/pallas_call | solution.py:252
  1.9 1.4 %collective-permute-start = (bf16[128,256]{1,0:T(8,128)(2,1)S(1)}, bf16[128,256]{1,0:T(8,128)(2,1)S(1)}, u32[]{:S(2)}, u32[]{:S(2)}) collective-permute-start(bf16[128,256]{1,0:T(8,128)(2,1)S(1)} %get-tuple-element.20), channel_id=1, source_target_pairs={{0,64},{64,0},{1,65},{65,1},{2,66},{66,2},{3,67},{67,3},{4,68},{68... | collective-permute-start | bytes 196616 | tf_op jit(solution)/shard_map/ppermute | solution.py:46
  3.3 0.9 %collective-permute-done.got_ref = bf16[128,256]{1,0:T(8,128)(2,1)S(1)} collective-permute-done((bf16[128,256]{1,0:T(8,128)(2,1)S(1)}, bf16[128,256]{1,0:T(8,128)(2,1)S(1)}, u32[]{:S(2)}, u32[]{:S(2)}) %collective-permute-start) | collective-permute-done | bytes 65568 | tf_op jit(solution)/shard_map/ppermute | solution.py:46
  4.2 0.1 tile.1
  4.3 14.8 %all_to_all.15.mine_ref = bf16[8,2,128,256]{3,2,1,0:T(8,128)(2,1)S(1)} all-to-all(bf16[8,2,128,256]{3,2,1,0:T(8,128)(2,1)S(1)} %tile.1), channel_id=1, replica_groups={{0,3,12,15,48,51,60,63},{1,2,13,14,49,50,61,62},{4,7,8,11,52,55,56,59},..., dimensions={0} | all-to-all | bytes 2097152 | tf_op jit(solution)/shard_map/all_to_all | solution.py:42
  19.1 10.2 %collective-permute-start.1 = (bf16[8,2,128,256]{3,2,1,0:T(8,128)(2,1)S(1)}, bf16[8,2,128,256]{3,2,1,0:T(8,128)(2,1)S(1)}, u32[]{:S(2)}, u32[]{:S(2)}) collective-permute-start(bf16[8,2,128,256]{3,2,1,0:T(8,128)(2,1)S(1)} %all_to_all.15.mine_ref), channel_id=1, source_target_pairs={{0,64},{64,0},{1,65},{65,1},{2,66},{66,2},{3,67},{67,3},{4,68},{68... | collective-permute-start | bytes 3145736 | tf_op jit(solution)/shard_map/ppermute | solution.py:46
  29.4 2.3 %collective-permute-done.1.got_ref = bf16[8,2,128,256]{3,2,1,0:T(8,128)(2,1)S(1)} collective-permute-done((bf16[8,2,128,256]{3,2,1,0:T(8,128)(2,1)S(1)}, bf16[8,2,128,256]{3,2,1,0:T(8,128)(2,1)S(1)}, u32[]{:S(2)}, u32[]{:S(2)}) %collective-permute-start.1) | collective-permute-done | bytes 1048608 | tf_op jit(solution)/shard_map/ppermute | solution.py:46
  31.7 3.2 %score.1 = (bf16[8,256,1024]{2,1,0:T(8,128)(2,1)S(1)}, bf16[8,128,256]{2,1,0:T(8,128)(2,1)S(1)}, f32[8,16,128]{2,1,0:T(8,128)S(1)}, bf16[1024,256]{1,0:T(8,128)(2,1)S(1)}) custom-call(bf16[8,2,128,256]{3,2,1,0:T(8,128)(2,1)S(1)} %all_to_all.15.mine_ref, bf16[8,2,128,256]{3,2,1,0:T(8,128)(2,1)S(1)} %collective-permute-done.1.got_ref, ...), custom_call_target="tpu_custom_call" | custom-call | flops 2147483648 | tf_op jit(solution)/shard_map/score/pallas_call | solution.py:263
  34.8 7.2 %all_to_all.16.refs_3_.refs_2_.s_ref = f32[8,16,128]{2,1,0:T(8,128)S(1)} all-to-all(f32[8,16,128]{2,1,0:T(8,128)S(1)} %get-tuple-element.25), channel_id=1, replica_groups={{0,1,4,5,16,17,20,21},{3,2,7,6,19,18,23,22},{12,13,8,9,28,29,24,25},{15..., dimensions={0} | all-to-all | bytes 131072 | tf_op jit(solution)/shard_map/all_to_all | solution.py:42
  42.0 0.7 %weigh0.1 = (f32[4,256,256]{2,1,0:T(8,128)S(1)}, bf16[1040,256]{1,0:T(8,128)(2,1)S(1)}) custom-call(bf16[1024,256]{1,0:T(8,128)(2,1)S(1)} %get-tuple-element.22.refs_0_.u_ref, bf16[8,256,1024]{2,1,0:T(8,128)(2,1)S(1)} %get-tuple-element.23.refs_1_.refs_0_, bf16[8,128,256]{2,1,0:T(8,128)(2,1)S(1)} %get-tuple-element.24.refs_2_.refs_1_, ...), custom_call_target="tpu_custom_call" | custom-call | flops 536870912 | tf_op jit(solution)/shard_map/weigh0/pallas_call | solution.py:278
  42.7 1.6 %collective-permute-start.2 = (bf16[1040,256]{1,0:T(8,128)(2,1)S(1)}, bf16[1040,256]{1,0:T(8,128)(2,1)S(1)}, u32[]{:S(2)}, u32[]{:S(2)}) collective-permute-start(bf16[1040,256]{1,0:T(8,128)(2,1)S(1)} %get-tuple-element.28), channel_id=1, source_target_pairs={{0,64},{64,0},{1,65},{65,1},{2,66},{66,2},{3,67},{67,3},{4,68},{68... | collective-permute-start | bytes 1597448 | tf_op jit(solution)/shard_map/ppermute | solution.py:46
  44.3 0.7 %weigh1.1 = (f32[4,256,256]{2,1,0:T(8,128)S(1)}, bf16[1024,256]{1,0:T(8,128)(2,1)S(1)}) custom-call(bf16[8,256,1024]{2,1,0:T(8,128)(2,1)S(1)} %get-tuple-element.23.refs_1_.refs_0_, bf16[8,128,256]{2,1,0:T(8,128)(2,1)S(1)} %get-tuple-element.24.refs_2_.refs_1_, f32[8,16,128]{2,1,0:T(8,128)S(1)} %all_to_all.16.refs_3_.refs_2_.s_ref), custom_call_target="tpu_custom_call" | custom-call | flops 536870912 | tf_op jit(solution)/shard_map/weigh1/pallas_call | solution.py:278
  45.1 0.1 collective-permute-start.3
  45.2 1.9 %collective-permute-done.3.got1_ref = bf16[1024,256]{1,0:T(8,128)(2,1)S(1)} collective-permute-done((bf16[1024,256]{1,0:T(8,128)(2,1)S(1)}, bf16[1024,256]{1,0:T(8,128)(2,1)S(1)}, u32[]{:S(2)}, u32[]{:S(2)}) %collective-permute-start.3) | collective-permute-done | bytes 524320 | tf_op jit(solution)/shard_map/ppermute | solution.py:46
  47.0 0.0 collective-permute-done.2.got0_ref
  47.0 0.2 join.1
  47.3 13.1 %all_to_all.17.w_ref = bf16[8,272,256]{2,1,0:T(8,128)(2,1)S(1)} all-to-all(bf16[8,272,256]{2,1,0:T(8,128)(2,1)S(1)} %join.1), channel_id=1, replica_groups={{0,3,12,15,48,51,60,63},{1,2,13,14,49,50,61,62},{4,7,8,11,52,55,56,59},..., dimensions={0} | all-to-all | bytes 2228224 | tf_op jit(solution)/shard_map/all_to_all | solution.py:42
  60.4 0.0 copy-start
  60.4 0.0 copy-start.1
  60.4 0.1 sum.1
  60.5 4.8 %collective-permute-start.4 = (f32[136,256]{1,0:T(8,128)S(1)}, f32[136,256]{1,0:T(8,128)S(1)}, u32[]{:S(2)}, u32[]{:S(2)}) collective-permute-start(f32[136,256]{1,0:T(8,128)S(1)} %get-tuple-element.31), channel_id=1, source_target_pairs={{0,64},{64,0},{1,65},{65,1},{2,66},{66,2},{3,67},{67,3},{4,68},{68... | collective-permute-start | bytes 417800 | tf_op jit(solution)/shard_map/ppermute | solution.py:46
  65.3 1.0 %collective-permute-done.4.got_ref = f32[136,256]{1,0:T(8,128)S(1)} collective-permute-done((f32[136,256]{1,0:T(8,128)S(1)}, f32[136,256]{1,0:T(8,128)S(1)}, u32[]{:S(2)}, u32[]{:S(2)}) %collective-permute-start.4) | collective-permute-done | bytes 139296 | tf_op jit(solution)/shard_map/ppermute | solution.py:46
  66.3 0.0 copy-done
  66.3 0.0 copy-done.1
  66.3 1.0 %final.1 = (f32[128,256]{1,0:T(8,128)}, f32[128,256]{1,0:T(8,128)}, f32[1,1]{1,0:T(1,128)}) custom-call(bf16[128,256]{1,0:T(8,128)(2,1)S(1)} %copy-done, bf16[128,256]{1,0:T(8,128)(2,1)S(1)} %copy-done.1, f32[136,256]{1,0:T(8,128)S(1)} %get-tuple-element.30.keep_ref, f32[136,256]{1,0:T(8,128)S(1)} %collective-permute-done.4.got_ref, ...), custom_call_target="tpu_custom_call" | custom-call | tf_op jit(solution)/shard_map/final/pallas_call | solution.py:289
Async XLA Ops:
  1.9 2.3 %collective-permute-start = (bf16[128,256]{1,0:T(8,128)(2,1)S(1)}, bf16[128,256]{1,0:T(8,128)(2,1)S(1)}, u32[]{:S(2)}, u32[]{:S(2)}) collective-permute-start(bf16[128,256]{1,0:T(8,128)(2,1)S(1)} %get-tuple-element.20), channel_id=1, source_target_pairs={{0,64},{64,0},{1,65},{65,1},{2,66},{66,2},{3,67},{67,3},{4,68},{68... | collective-permute-start | bytes 196616 | tf_op jit(solution)/shard_map/ppermute | solution.py:46
  19.1 12.5 %collective-permute-start.1 = (bf16[8,2,128,256]{3,2,1,0:T(8,128)(2,1)S(1)}, bf16[8,2,128,256]{3,2,1,0:T(8,128)(2,1)S(1)}, u32[]{:S(2)}, u32[]{:S(2)}) collective-permute-start(bf16[8,2,128,256]{3,2,1,0:T(8,128)(2,1)S(1)} %all_to_all.15.mine_ref), channel_id=1, source_target_pairs={{0,64},{64,0},{1,65},{65,1},{2,66},{66,2},{3,67},{67,3},{4,68},{68... | collective-permute-start | bytes 3145736 | tf_op jit(solution)/shard_map/ppermute | solution.py:46
  42.7 4.4 %collective-permute-start.2 = (bf16[1040,256]{1,0:T(8,128)(2,1)S(1)}, bf16[1040,256]{1,0:T(8,128)(2,1)S(1)}, u32[]{:S(2)}, u32[]{:S(2)}) collective-permute-start(bf16[1040,256]{1,0:T(8,128)(2,1)S(1)} %get-tuple-element.28), channel_id=1, source_target_pairs={{0,64},{64,0},{1,65},{65,1},{2,66},{66,2},{3,67},{67,3},{4,68},{68... | collective-permute-start | bytes 1597448 | tf_op jit(solution)/shard_map/ppermute | solution.py:46
  45.1 2.0 %collective-permute-start.3 = (bf16[1024,256]{1,0:T(8,128)(2,1)S(1)}, bf16[1024,256]{1,0:T(8,128)(2,1)S(1)}, u32[]{:S(2)}, u32[]{:S(2)}) collective-permute-start(bf16[1024,256]{1,0:T(8,128)(2,1)S(1)} %get-tuple-element.29), channel_id=1, source_target_pairs={{0,64},{64,0},{1,65},{65,1},{2,66},{66,2},{3,67},{67,3},{4,68},{68... | collective-permute-start | bytes 1572872 | tf_op jit(solution)/shard_map/ppermute | solution.py:46
  60.4 6.0 %copy-start = (bf16[128,256]{1,0:T(8,128)(2,1)S(1)}, bf16[128,256]{1,0:T(8,128)(2,1)}, u32[]{:S(2)}) copy-start(bf16[128,256]{1,0:T(8,128)(2,1)} %q_ref.1) | copy-start | bytes 196612
  60.4 6.0 %copy-start.1 = (bf16[128,256]{1,0:T(8,128)(2,1)S(1)}, bf16[128,256]{1,0:T(8,128)(2,1)}, u32[]{:S(2)}) copy-start(bf16[128,256]{1,0:T(8,128)(2,1)} %v_ref.1) | copy-start | bytes 196612
  60.5 5.8 %collective-permute-start.4 = (f32[136,256]{1,0:T(8,128)S(1)}, f32[136,256]{1,0:T(8,128)S(1)}, u32[]{:S(2)}, u32[]{:S(2)}) collective-permute-start(f32[136,256]{1,0:T(8,128)S(1)} %get-tuple-element.31), channel_id=1, source_target_pairs={{0,64},{64,0},{1,65},{65,1},{2,66},{66,2},{3,67},{67,3},{4,68},{68... | collective-permute-start | bytes 417800 | tf_op jit(solution)/shard_map/ppermute | solution.py:46

commit v5 on v3

--- a/solution.py
+++ b/solution.py
@@ -10,10 +10,9 @@
 from jax.sharding import PartitionSpec as P
 
 AXES = ("blk", "z", "y", "x")
-RING = {(0, 0): 0, (1, 0): 1, (1, 1): 2, (0, 1): 3}
-BITS = [(a, b, c) for a in (0, 1) for b in (0, 1) for c in (0, 1)]
 GROUP = 8
 ROWS, D = 128, 256
+ITEM = 1
 
 sharpness = 0.05
 tiny_square = 1e-12
@@ -21,21 +20,24 @@
 f32, bf16 = jnp.float32, jnp.bfloat16
 
 
-def device_of(core, low, high):
-    z, y, x = (RING[(l, h)] for l, h in zip(low, high))
+def device_of(core, z, y, x):
     return ((core * 4 + z) * 4 + y) * 4 + x
 
 
-def low_cubes(core):
-    return [[device_of(core, low, high) for low in BITS] for high in BITS]
-
-
-def high_cubes(core):
-    return [[device_of(core, low, high) for high in BITS] for low in BITS]
-
-
-BULK = low_cubes(0) + high_cubes(1)
-HIGH = high_cubes(0) + high_cubes(1)
+def query_groups(core):
+    return [[device_of(core, z, y, x) for y in pair for x in range(4)] for z in range(4) for pair in ((0, 1), (2, 3))]
+
+
+def item_groups(core):
+    return [[device_of(core, z, y, x) for y in pair for z in range(4)] for x in range(4) for pair in ((1, 2), (3, 0))]
+
+
+def query_index():
+    return lax.axis_index("y") % 2 * 4 + lax.axis_index("x")
+
+
+BULK = item_groups(ITEM) + query_groups(1 - ITEM)
+QUERY = query_groups(0) + query_groups(1)
 
 
 def exchange(pieces, groups):
@@ -81,12 +83,12 @@
     total = jnp.sum(q.astype(f32) * v.astype(f32)) / sharpness
     pos_ref[...] = jnp.full((8, 128), total, f32)
 
-    @pl.when(core == 0)
+    @pl.when(core == ITEM)
     def _():
         mine_ref[...] = v
         give_ref[...] = q
 
-    @pl.when(core == 1)
+    @pl.when(core != ITEM)
     def _():
         mine_ref[...] = q
         give_ref[...] = v
@@ -103,15 +105,15 @@
 def score_body(mine_ref, got_ref, pos_ref, e_ref, q_ref, s_ref, u_ref, v_ref):
     core = lax.axis_index("blk")
 
-    @pl.when(core == 0)
+    @pl.when(core == ITEM)
     def _():
         v_ref[...] = mine_ref[...]
-        q_ref[...] = got_ref[:, 0]
-
-    @pl.when(core == 1)
+        q_ref[...] = got_ref[:, ITEM]
+
+    @pl.when(core != ITEM)
     def _():
         v_ref[...] = got_ref[...]
-        q_ref[...] = mine_ref[:, 1]
+        q_ref[...] = mine_ref[:, 1 - ITEM]
 
     cols = GROUP * ROWS
     q = q_ref[...].reshape(cols, D)
@@ -171,7 +173,7 @@
     if u_ref:
         give_ref[1024:1040] = split(jnp.full((8, D), loss_part(sums), f32))
 
-        @pl.when(core == 0)
+        @pl.when(core == ITEM)
         def _():
             give_ref[:1024] = u_ref[0][...]
 
@@ -179,19 +181,19 @@
 def join_body(keep0_ref, keep1_ref, got0_ref, got1_ref, u_ref, s_ref, out_ref):
     core = lax.axis_index("blk")
 
-    @pl.when(core == 0)
+    @pl.when(core == ITEM)
     def _():
         for k in range(GROUP):
             keep, got = (keep0_ref, got0_ref) if k < 4 else (keep1_ref, got1_ref)
             i = k % 4
             out_ref[k, :256] = (keep[i] + got[i * 256 : (i + 1) * 256].astype(f32)).astype(bf16)
 
-    @pl.when(core == 1)
+    @pl.when(core != ITEM)
     def _():
         for k in range(GROUP):
             rows = slice(k * ROWS, (k + 1) * ROWS)
-            out_ref[k, :128] = got0_ref[rows]
-            out_ref[k, 128:256] = u_ref[rows]
+            out_ref[k, (1 - ITEM) * 128 : (2 - ITEM) * 128] = u_ref[rows]
+            out_ref[k, ITEM * 128 : (ITEM + 1) * 128] = got0_ref[rows]
 
     got = got0_ref[1024:1040].astype(f32)
     tail = split(got[:8] + got[8:] + loss_part(row_sums(s_ref)))
@@ -223,13 +225,8 @@
     return (grad - direction * along) / length
 
 
-def high_index():
-    bit = lambda a: (lax.axis_index(a) >= 2).astype(jnp.int32)
-    return bit("z") * 4 + bit("y") * 2 + bit("x")
-
-
 def final_body(q_ref, v_ref, keep_ref, got_ref, s_ref, qs_ref, vs_ref, loss_ref):
-    first = lax.axis_index("blk") == 0
+    first = lax.axis_index("blk") == ITEM
     q, q_len = unit(q_ref[...])
     v, v_len = unit(v_ref[...])
     q_hat, v_hat = q.astype(bf16).astype(f32), v.astype(bf16).astype(f32)
@@ -237,7 +234,7 @@
     w = jnp.where(first, keep, got)
     u = jnp.where(first, got, keep)
     sums = row_sums(s_ref)[:8]
-    mine = lax.broadcasted_iota(jnp.int32, sums.shape, 0) == high_index()
+    mine = lax.broadcasted_iota(jnp.int32, sums.shape, 0) == query_index()
     own = jnp.sum(jnp.where(mine, sums, 0.0), axis=0, keepdims=True)
     u = jnp.concatenate([(u[:128, :128] / own).T, (u[:128, 128:] / own).T], axis=1)
     qs_ref[...] = slope(u, v_hat, q, q_len)
@@ -271,7 +268,7 @@
         2 * flops,
         scratch=[pltpu.VMEM(bulk, bf16)],
     )(block, swap_cores(block), pos)
-    sums = exchange(s, HIGH)
+    sums = exchange(s, QUERY)
     keep, got = [], []
     for half in (0, 1):
         k, g = call(

time: 68.5 us -> 59.7 us (0.87)
  blocking collectives: 50.5 us -> 41.3 us
    all_to_all x3, blocking collectives: 50.5 us -> 41.3 us  [exchange(): lax.all_to_all(pieces, AXES, 0, 0, tiled=True, axis_index_groups=groups)]
where the time goes in v5:
time: 59.7 us; the launch traced here: 59.4 us
  blocking collectives  41.3 us (69%)
  Pallas kernels  7.37 us (12%)
  waiting for transfers between devices  6.43 us (11%)
  starting transfers between devices  3.63 us (6%)
  between operations  0.68 us (1%)
    all_to_all x3, blocking collectives, exchange(): lax.all_to_all(pieces, AXES, 0, 0, tiled=True, axis_index_groups=groups)  41.3 us
    ppermute x5, waiting for transfers between devices, swap_cores(): return lax.ppermute(value, 'blk', [(0, 1), (1, 0)])  6.43 us
    ppermute x5, starting transfers between devices, swap_cores(): return lax.ppermute(value, 'blk', [(0, 1), (1, 0)])  3.63 us
    pallas_call x1, Pallas kernels, per_device(): call(score_body, [((GROUP, 256, 1024), bf16), ((GROUP, ROWS, D), bf16), (...  3.16 us
    pallas_call x2, Pallas kernels, per_device(): call(functools.partial(weigh_body, half * 4), [((4, 256, D), f32), ((1040...  1.46 us
    pallas_call x1, Pallas kernels, per_device(): call(norm_body, [(rows, bf16), (rows, bf16), ((8, 128), f32)], 'norm', in...  1.24 us
  transfers between devices with their start and end apart: 5, of which 4 were waited for; matrix products, arithmetic and copies ran while one was open for 0% of the time, Pallas kernels for 1%

profile of v5, /device:TPU:1, one launch (start us, length us, event | category | flops | bytes accessed | tf_op | source)
XLA Modules:
  0.0 59.4 jit_solution(2498739062351109886)
XLA Ops:
  0.6 1.2 %norm.1 = (bf16[128,256]{1,0:T(8,128)(2,1)S(1)}, bf16[128,256]{1,0:T(8,128)(2,1)S(1)}, f32[8,128]{1,0:T(8,128)S(1)}) custom-call(bf16[128,256]{1,0:T(8,128)(2,1)} %q_ref.1, bf16[128,256]{1,0:T(8,128)(2,1)} %v_ref.1), custom_call_target="tpu_custom_call" | custom-call | tf_op jit(solution)/shard_map/norm/pallas_call | solution.py:248
  1.9 1.4 %collective-permute-start = (bf16[128,256]{1,0:T(8,128)(2,1)S(1)}, bf16[128,256]{1,0:T(8,128)(2,1)S(1)}, u32[]{:S(2)}, u32[]{:S(2)}) collective-permute-start(bf16[128,256]{1,0:T(8,128)(2,1)S(1)} %get-tuple-element.20), channel_id=1, source_target_pairs={{0,64},{64,0},{1,65},{65,1},{2,66},{66,2},{3,67},{67,3},{4,68},{68... | collective-permute-start | bytes 196616 | tf_op jit(solution)/shard_map/ppermute | solution.py:48
  3.3 0.9 %collective-permute-done.got_ref = bf16[128,256]{1,0:T(8,128)(2,1)S(1)} collective-permute-done((bf16[128,256]{1,0:T(8,128)(2,1)S(1)}, bf16[128,256]{1,0:T(8,128)(2,1)S(1)}, u32[]{:S(2)}, u32[]{:S(2)}) %collective-permute-start) | collective-permute-done | bytes 65568 | tf_op jit(solution)/shard_map/ppermute | solution.py:48
  4.2 0.1 tile.1
  4.3 16.7 %all_to_all.15.mine_ref = bf16[8,2,128,256]{3,2,1,0:T(8,128)(2,1)S(1)} all-to-all(bf16[8,2,128,256]{3,2,1,0:T(8,128)(2,1)S(1)} %tile.1), channel_id=1, replica_groups={{68,84,100,116,72,88,104,120},{76,92,108,124,64,80,96,112},{69,85,101,1..., dimensions={0} | all-to-all | bytes 2097152 | tf_op jit(solution)/shard_map/all_to_all | solution.py:44
  21.0 0.4 collective-permute-start.1
  21.4 2.3 %collective-permute-done.1.got_ref = bf16[8,2,128,256]{3,2,1,0:T(8,128)(2,1)S(1)} collective-permute-done((bf16[8,2,128,256]{3,2,1,0:T(8,128)(2,1)S(1)}, bf16[8,2,128,256]{3,2,1,0:T(8,128)(2,1)S(1)}, u32[]{:S(2)}, u32[]{:S(2)}) %collective-permute-start.1) | collective-permute-done | bytes 1048608 | tf_op jit(solution)/shard_map/ppermute | solution.py:48
  23.7 3.2 %score.1 = (bf16[8,256,1024]{2,1,0:T(8,128)(2,1)S(1)}, bf16[8,128,256]{2,1,0:T(8,128)(2,1)S(1)}, f32[8,16,128]{2,1,0:T(8,128)S(1)}, bf16[1024,256]{1,0:T(8,128)(2,1)S(1)}) custom-call(bf16[8,2,128,256]{3,2,1,0:T(8,128)(2,1)S(1)} %all_to_all.15.mine_ref, bf16[8,2,128,256]{3,2,1,0:T(8,128)(2,1)S(1)} %collective-permute-done.1.got_ref, ...), custom_call_target="tpu_custom_call" | custom-call | flops 2147483648 | tf_op jit(solution)/shard_map/score/pallas_call | solution.py:259
  26.9 9.3 %all_to_all.16.refs_3_.refs_2_.s_ref = f32[8,16,128]{2,1,0:T(8,128)S(1)} all-to-all(f32[8,16,128]{2,1,0:T(8,128)S(1)} %get-tuple-element.25), channel_id=1, replica_groups={{0,1,2,3,4,5,6,7},{8,9,10,11,12,13,14,15},{16,17,18,19,20,21,22,23},{24..., dimensions={0} | all-to-all | bytes 131072 | tf_op jit(solution)/shard_map/all_to_all | solution.py:44
  36.1 0.8 %weigh0.1 = (f32[4,256,256]{2,1,0:T(8,128)S(1)}, bf16[1040,256]{1,0:T(8,128)(2,1)S(1)}) custom-call(bf16[1024,256]{1,0:T(8,128)(2,1)S(1)} %get-tuple-element.22.refs_0_.u_ref, bf16[8,256,1024]{2,1,0:T(8,128)(2,1)S(1)} %get-tuple-element.23.refs_1_.refs_0_, bf16[8,128,256]{2,1,0:T(8,128)(2,1)S(1)} %get-tuple-element.24.refs_2_.refs_1_, ...), custom_call_target="tpu_custom_call" | custom-call | flops 536870912 | tf_op jit(solution)/shard_map/weigh0/pallas_call | solution.py:274
  36.9 1.6 %collective-permute-start.2 = (bf16[1040,256]{1,0:T(8,128)(2,1)S(1)}, bf16[1040,256]{1,0:T(8,128)(2,1)S(1)}, u32[]{:S(2)}, u32[]{:S(2)}) collective-permute-start(bf16[1040,256]{1,0:T(8,128)(2,1)S(1)} %get-tuple-element.28), channel_id=1, source_target_pairs={{0,64},{64,0},{1,65},{65,1},{2,66},{66,2},{3,67},{67,3},{4,68},{68... | collective-permute-start | bytes 1597448 | tf_op jit(solution)/shard_map/ppermute | solution.py:48
  38.5 0.7 %weigh1.1 = (f32[4,256,256]{2,1,0:T(8,128)S(1)}, bf16[1024,256]{1,0:T(8,128)(2,1)S(1)}) custom-call(bf16[8,256,1024]{2,1,0:T(8,128)(2,1)S(1)} %get-tuple-element.23.refs_1_.refs_0_, bf16[8,128,256]{2,1,0:T(8,128)(2,1)S(1)} %get-tuple-element.24.refs_2_.refs_1_, f32[8,16,128]{2,1,0:T(8,128)S(1)} %all_to_all.16.refs_3_.refs_2_.s_ref), custom_call_target="tpu_custom_call" | custom-call | flops 536870912 | tf_op jit(solution)/shard_map/weigh1/pallas_call | solution.py:274
  39.2 0.1 collective-permute-start.3
  39.3 1.9 %collective-permute-done.3.got1_ref = bf16[1024,256]{1,0:T(8,128)(2,1)S(1)} collective-permute-done((bf16[1024,256]{1,0:T(8,128)(2,1)S(1)}, bf16[1024,256]{1,0:T(8,128)(2,1)S(1)}, u32[]{:S(2)}, u32[]{:S(2)}) %collective-permute-start.3) | collective-permute-done | bytes 524320 | tf_op jit(solution)/shard_map/ppermute | solution.py:48
  41.2 0.0 collective-permute-done.2.got0_ref
  41.2 0.3 join.1
  41.5 15.3 %all_to_all.17.w_ref = bf16[8,272,256]{2,1,0:T(8,128)(2,1)S(1)} all-to-all(bf16[8,272,256]{2,1,0:T(8,128)(2,1)S(1)} %join.1), channel_id=1, replica_groups={{68,84,100,116,72,88,104,120},{76,92,108,124,64,80,96,112},{69,85,101,1..., dimensions={0} | all-to-all | bytes 2228224 | tf_op jit(solution)/shard_map/all_to_all | solution.py:44
  56.8 0.0 copy-start
  56.8 0.0 copy-start.1
  56.8 0.1 sum.1
  57.0 0.1 collective-permute-start.4
  57.1 1.3 %collective-permute-done.4.got_ref = f32[136,256]{1,0:T(8,128)S(1)} collective-permute-done((f32[136,256]{1,0:T(8,128)S(1)}, f32[136,256]{1,0:T(8,128)S(1)}, u32[]{:S(2)}, u32[]{:S(2)}) %collective-permute-start.4) | collective-permute-done | bytes 139296 | tf_op jit(solution)/shard_map/ppermute | solution.py:48
  58.4 0.0 copy-done
  58.4 0.0 copy-done.1
  58.4 1.0 %final.1 = (f32[128,256]{1,0:T(8,128)}, f32[128,256]{1,0:T(8,128)}, f32[1,1]{1,0:T(1,128)}) custom-call(bf16[128,256]{1,0:T(8,128)(2,1)S(1)} %copy-done, bf16[128,256]{1,0:T(8,128)(2,1)S(1)} %copy-done.1, f32[136,256]{1,0:T(8,128)S(1)} %get-tuple-element.30.keep_ref, f32[136,256]{1,0:T(8,128)S(1)} %collective-permute-done.4.got_ref, ...), custom_call_target="tpu_custom_call" | custom-call | tf_op jit(solution)/shard_map/final/pallas_call | solution.py:285
Async XLA Ops:
  1.9 2.3 %collective-permute-start = (bf16[128,256]{1,0:T(8,128)(2,1)S(1)}, bf16[128,256]{1,0:T(8,128)(2,1)S(1)}, u32[]{:S(2)}, u32[]{:S(2)}) collective-permute-start(bf16[128,256]{1,0:T(8,128)(2,1)S(1)} %get-tuple-element.20), channel_id=1, source_target_pairs={{0,64},{64,0},{1,65},{65,1},{2,66},{66,2},{3,67},{67,3},{4,68},{68... | collective-permute-start | bytes 196616 | tf_op jit(solution)/shard_map/ppermute | solution.py:48
  21.0 2.7 %collective-permute-start.1 = (bf16[8,2,128,256]{3,2,1,0:T(8,128)(2,1)S(1)}, bf16[8,2,128,256]{3,2,1,0:T(8,128)(2,1)S(1)}, u32[]{:S(2)}, u32[]{:S(2)}) collective-permute-start(bf16[8,2,128,256]{3,2,1,0:T(8,128)(2,1)S(1)} %all_to_all.15.mine_ref), channel_id=1, source_target_pairs={{0,64},{64,0},{1,65},{65,1},{2,66},{66,2},{3,67},{67,3},{4,68},{68... | collective-permute-start | bytes 3145736 | tf_op jit(solution)/shard_map/ppermute | solution.py:48
  36.9 4.3 %collective-permute-start.2 = (bf16[1040,256]{1,0:T(8,128)(2,1)S(1)}, bf16[1040,256]{1,0:T(8,128)(2,1)S(1)}, u32[]{:S(2)}, u32[]{:S(2)}) collective-permute-start(bf16[1040,256]{1,0:T(8,128)(2,1)S(1)} %get-tuple-element.28), channel_id=1, source_target_pairs={{0,64},{64,0},{1,65},{65,1},{2,66},{66,2},{3,67},{67,3},{4,68},{68... | collective-permute-start | bytes 1597448 | tf_op jit(solution)/shard_map/ppermute | solution.py:48
  39.2 2.0 %collective-permute-start.3 = (bf16[1024,256]{1,0:T(8,128)(2,1)S(1)}, bf16[1024,256]{1,0:T(8,128)(2,1)S(1)}, u32[]{:S(2)}, u32[]{:S(2)}) collective-permute-start(bf16[1024,256]{1,0:T(8,128)(2,1)S(1)} %get-tuple-element.29), channel_id=1, source_target_pairs={{0,64},{64,0},{1,65},{65,1},{2,66},{66,2},{3,67},{67,3},{4,68},{68... | collective-permute-start | bytes 1572872 | tf_op jit(solution)/shard_map/ppermute | solution.py:48
  56.8 1.6 %copy-start = (bf16[128,256]{1,0:T(8,128)(2,1)S(1)}, bf16[128,256]{1,0:T(8,128)(2,1)}, u32[]{:S(2)}) copy-start(bf16[128,256]{1,0:T(8,128)(2,1)} %q_ref.1) | copy-start | bytes 196612
  56.8 1.6 %copy-start.1 = (bf16[128,256]{1,0:T(8,128)(2,1)S(1)}, bf16[128,256]{1,0:T(8,128)(2,1)}, u32[]{:S(2)}) copy-start(bf16[128,256]{1,0:T(8,128)(2,1)} %v_ref.1) | copy-start | bytes 196612
  57.0 1.4 %collective-permute-start.4 = (f32[136,256]{1,0:T(8,128)S(1)}, f32[136,256]{1,0:T(8,128)S(1)}, u32[]{:S(2)}, u32[]{:S(2)}) collective-permute-start(f32[136,256]{1,0:T(8,128)S(1)} %get-tuple-element.31), channel_id=1, source_target_pairs={{0,64},{64,0},{1,65},{65,1},{2,66},{66,2},{3,67},{67,3},{4,68},{68... | collective-permute-start | bytes 417800 | tf_op jit(solution)/shard_map/ppermute | solution.py:48

commit v6 on v5

--- a/solution.py
+++ b/solution.py
@@ -1,4 +1,3 @@
-import functools
 import math
 
 import jax
@@ -68,7 +67,11 @@
     return wide / length, length
 
 
-def norm_body(q_hbm, v_hbm, mine_ref, give_ref, pos_ref, q_ref, v_ref, sem):
+def hat(matrix):
+    return unit(matrix)[0].astype(bf16)
+
+
+def norm_body(q_hbm, v_hbm, mine_ref, pos_ref, q_ref, v_ref, sem):
     copies = [
         pltpu.make_async_copy(q_hbm, q_ref, sem.at[0]),
         pltpu.make_async_copy(v_hbm, v_ref, sem.at[1]),
@@ -76,33 +79,40 @@
     for c in copies:
         c.start()
     core = lax.axis_index("blk")
-    copies[0].wait()
-    q = unit(q_ref[...])[0].astype(bf16)
-    copies[1].wait()
-    v = unit(v_ref[...])[0].astype(bf16)
+    for c in copies:
+        c.wait()
+    q, v = hat(q_ref[...]), hat(v_ref[...])
     total = jnp.sum(q.astype(f32) * v.astype(f32)) / sharpness
     pos_ref[...] = jnp.full((8, 128), total, f32)
 
     @pl.when(core == ITEM)
     def _():
         mine_ref[...] = v
-        give_ref[...] = q
 
     @pl.when(core != ITEM)
     def _():
         mine_ref[...] = q
-        give_ref[...] = v
-
-
-def tile_body(mine_ref, got_ref, out_ref):
-    core = lax.axis_index("blk")
-    mine, got = mine_ref[...], got_ref[...]
-    for k in range(GROUP):
-        out_ref[k, core] = mine
-        out_ref[k, 1 - core] = got
-
-
-def score_body(mine_ref, got_ref, pos_ref, e_ref, q_ref, s_ref, u_ref, v_ref):
+
+
+def tile_body(mine_ref, got_q_ref, got_v_ref, out_ref):
+    core = lax.axis_index("blk")
+
+    def fill(got_ref):
+        mine, got = mine_ref[...], hat(got_ref[...])
+        for k in range(GROUP):
+            out_ref[k, core] = mine
+            out_ref[k, 1 - core] = got
+
+    @pl.when(core == ITEM)
+    def _():
+        fill(got_v_ref)
+
+    @pl.when(core != ITEM)
+    def _():
+        fill(got_q_ref)
+
+
+def score_body(mine_ref, got_ref, pos_ref, e_ref, q_ref, v_ref, s_ref):
     core = lax.axis_index("blk")
 
     @pl.when(core == ITEM)
@@ -118,23 +128,15 @@
     cols = GROUP * ROWS
     q = q_ref[...].reshape(cols, D)
     total = jnp.zeros((1, cols), f32)
-    pull = None
     for k in range(GROUP):
         v = v_ref[k].reshape(2 * ROWS, D)
         t = lax.dot_general(v, q, (((1,), (1,)), ((), ())), preferred_element_type=f32)
         e = jnp.exp2(t * (log2_e / sharpness))
         total = total + jnp.sum(e, axis=0, keepdims=True)
-        eb = e.astype(bf16)
-        e_ref[k] = eb
-        part = lax.dot_general(v, eb, (((0,), (0,)), ((), ())), preferred_element_type=f32)
-        pull = part if pull is None else pull + part
+        e_ref[k] = e.astype(bf16)
     for k in range(GROUP):
-        cut = slice(k * ROWS, (k + 1) * ROWS)
-        rows = slice(k * ROWS, (k + 1) * ROWS)
-        u_ref[rows, :ROWS] = pull[:ROWS, cut].astype(bf16)
-        u_ref[rows, ROWS:] = pull[ROWS:, cut].astype(bf16)
         for j in range(GROUP):
-            s_ref[j, k : k + 1] = total[:, cut]
+            s_ref[j, k : k + 1] = total[:, k * ROWS : (k + 1) * ROWS]
     for j in range(GROUP):
         s_ref[j, 8:16] = pos_ref[...]
 
@@ -156,26 +158,68 @@
     return jnp.sum(jnp.log(sums[:8])) - jnp.max(sums[8:9])
 
 
-def weigh_body(first, *refs):
-    *u_ref, e_ref, q_ref, s_ref, keep_ref, give_ref = refs
-    core = lax.axis_index("blk")
-    sums = row_sums(s_ref)
-    r = 1.0 / sums[:8]
+def weigh(e_ref, q_ref, r, first, store):
     q = q_ref[...].reshape(GROUP * ROWS, D)
     for k in range(GROUP // 2):
         parts = [
             (e_ref[first + k, :, j * ROWS : (j + 1) * ROWS].astype(f32) * r[j : j + 1]).astype(bf16)
             for j in range(GROUP)
         ]
-        w = jnp.dot(jnp.concatenate(parts, axis=1), q, preferred_element_type=f32)
+        store(k, jnp.dot(jnp.concatenate(parts, axis=1), q, preferred_element_type=f32))
+
+
+def pull(v_ref, e_ref, u_ref):
+    total = None
+    for k in range(0, GROUP, 2):
+        v = v_ref[k : k + 2].reshape(4 * ROWS, D)
+        e = e_ref[k : k + 2].reshape(4 * ROWS, GROUP * ROWS)
+        part = lax.dot_general(v, e, (((0,), (0,)), ((), ())), preferred_element_type=f32)
+        total = part if total is None else total + part
+    for k in range(GROUP):
+        rows = slice(k * ROWS, (k + 1) * ROWS)
+        u_ref[rows, :ROWS] = total[:ROWS, rows].astype(bf16)
+        u_ref[rows, ROWS:] = total[ROWS:, rows].astype(bf16)
+
+
+def first_body(e_ref, q_ref, s_ref, keep_ref, give_ref):
+    sums = row_sums(s_ref)
+
+    def store(k, w):
         keep_ref[k] = w
         give_ref[k * 256 : (k + 1) * 256] = w.astype(bf16)
-    if u_ref:
-        give_ref[1024:1040] = split(jnp.full((8, D), loss_part(sums), f32))
-
-        @pl.when(core == ITEM)
-        def _():
-            give_ref[:1024] = u_ref[0][...]
+
+    weigh(e_ref, q_ref, 1.0 / sums[:8], 0, store)
+    give_ref[1024:1040] = split(jnp.full((8, D), loss_part(sums), f32))
+
+
+def second_body(e_ref, q_ref, s_ref, v_ref, give_ref):
+    core = lax.axis_index("blk")
+
+    @pl.when(core == ITEM)
+    def _():
+        pull(v_ref, e_ref, give_ref)
+
+    @pl.when(core != ITEM)
+    def _():
+        def store(k, w):
+            give_ref[k * 256 : (k + 1) * 256] = w.astype(bf16)
+
+        weigh(e_ref, q_ref, 1.0 / row_sums(s_ref)[:8], 4, store)
+
+
+def third_body(e_ref, q_ref, s_ref, v_ref, keep_ref, u_ref):
+    core = lax.axis_index("blk")
+
+    @pl.when(core == ITEM)
+    def _():
+        def store(k, w):
+            keep_ref[k] = w
+
+        weigh(e_ref, q_ref, 1.0 / row_sums(s_ref)[:8], 4, store)
+
+    @pl.when(core != ITEM)
+    def _():
+        pull(v_ref, e_ref, u_ref)
 
 
 def join_body(keep0_ref, keep1_ref, got0_ref, got1_ref, u_ref, s_ref, out_ref):
@@ -193,7 +237,7 @@
         for k in range(GROUP):
             rows = slice(k * ROWS, (k + 1) * ROWS)
             out_ref[k, (1 - ITEM) * 128 : (2 - ITEM) * 128] = u_ref[rows]
-            out_ref[k, ITEM * 128 : (ITEM + 1) * 128] = got0_ref[rows]
+            out_ref[k, ITEM * 128 : (ITEM + 1) * 128] = got1_ref[rows]
 
     got = got0_ref[1024:1040].astype(f32)
     tail = split(got[:8] + got[8:] + loss_part(row_sums(s_ref)))
@@ -243,43 +287,39 @@
 
 
 def per_device(queries, items):
-    anyspace = pl.BlockSpec(memory_space=pltpu.HBM)
     rows = (ROWS, D)
-    mine, give, pos = call(
+    bulk = (GROUP, 2, ROWS, D)
+    in_hbm = [pltpu.with_memory_space_constraint(a, pltpu.HBM) for a in (queries, items)]
+    mine, pos = call(
         norm_body,
-        [(rows, bf16), (rows, bf16), ((8, 128), f32)],
+        [(rows, bf16), ((8, 128), f32)],
         "norm",
-        ins=[anyspace] * 2,
+        10**9,
+        ins=[pl.BlockSpec(memory_space=pltpu.HBM)] * 2,
         scratch=[pltpu.VMEM(rows, bf16), pltpu.VMEM(rows, bf16), pltpu.SemaphoreType.DMA((2,))],
-    )(*(pltpu.with_memory_space_constraint(a, pltpu.HBM) for a in (queries, items)))
-    bulk = (GROUP, 2, ROWS, D)
-    (tile,) = call(tile_body, [(bulk, bf16)], "tile")(mine, swap_cores(give))
+    )(*in_hbm)
+    (tile,) = call(tile_body, [(bulk, bf16)], "tile")(mine, swap_cores(queries), swap_cores(items))
     block = exchange(tile, BULK)
     flops = 2 * 2048 * 1024 * 256
-    e, q, s, u = call(
+    e, q, v, s = call(
         score_body,
         [
             ((GROUP, 256, 1024), bf16),
             ((GROUP, ROWS, D), bf16),
+            (bulk, bf16),
             ((GROUP, 16, 128), f32),
-            ((GROUP * ROWS, D), bf16),
         ],
         "score",
-        2 * flops,
-        scratch=[pltpu.VMEM(bulk, bf16)],
+        flops,
     )(block, swap_cores(block), pos)
     sums = exchange(s, QUERY)
-    keep, got = [], []
-    for half in (0, 1):
-        k, g = call(
-            functools.partial(weigh_body, half * 4),
-            [((4, 256, D), f32), ((1040 - 16 * half, D), bf16)],
-            f"weigh{half}",
-            flops // 2,
-        )(*([u] if half == 0 else []), e, q, sums)
-        keep.append(k)
-        got.append(swap_cores(g))
-    (out,) = call(join_body, [((GROUP, 272, D), bf16)], "join")(*keep, *got, u, sums)
+    half, pulled = (4, 256, D), (GROUP * ROWS, D)
+    keep0, give = call(first_body, [(half, f32), ((1040, D), bf16)], "first", flops)(e, q, sums)
+    got0 = swap_cores(give)
+    (give,) = call(second_body, [(pulled, bf16)], "second", flops)(e, q, sums, v)
+    got1 = swap_cores(give)
+    keep1, u = call(third_body, [(half, f32), (pulled, bf16)], "third", flops)(e, q, sums, v)
+    (out,) = call(join_body, [((GROUP, 272, D), bf16)], "join")(keep0, keep1, got0, got1, u, sums)
     out = exchange(out, BULK)
     keep, give = call(sum_body, [((136, D), f32), ((136, D), f32)], "sum")(out)
     q_slope, v_slope, loss = call(

time: 59.7 us -> 57.9 us (0.970)
  waiting for transfers between devices: 6.43 us -> 5.04 us
    pallas_call x1, Pallas kernels: 3.16 us -> 1.47 us  [per_device(): call(score_body, [((GROUP, 256, 1024), bf16), ((GROUP, ROWS, D), bf16), (...]
    ppermute x5 -> x6, waiting for transfers between devices: 6.43 us -> 5.04 us  [swap_cores(): return lax.ppermute(value, 'blk', [(0, 1), (1, 0)])]
    pallas_call x5 -> x6, Pallas kernels: 3.09 us -> 4.44 us  [the longest x1 1.28 us: per_device(): give, = call(second_body, [(pulled, bf16)], 'second', flops)(e, q, sums, v)]
    ppermute x5 -> x6, starting transfers between devices: 3.63 us -> 3.65 us  [swap_cores(): return lax.ppermute(value, 'blk', [(0, 1), (1, 0)])]
  transfers between devices with their start and end apart: 5 -> 6, of which waited for: 4 -> 4; matrix products, arithmetic and copies ran while one was open for 0% -> 0% of each run, Pallas kernels for 1% -> 6%
where the time goes in v6:
time: 57.9 us; the launch traced here: 57.6 us
  blocking collectives  41.2 us (71%)
  Pallas kernels  7.03 us (12%)
  waiting for transfers between devices  5.04 us (9%)
  starting transfers between devices  3.65 us (6%)
  between operations  0.71 us (1%)
    all_to_all x3, blocking collectives, exchange(): lax.all_to_all(pieces, AXES, 0, 0, tiled=True, axis_index_groups=groups)  41.2 us
    ppermute x6, waiting for transfers between devices, swap_cores(): return lax.ppermute(value, 'blk', [(0, 1), (1, 0)])  5.04 us
    ppermute x6, starting transfers between devices, swap_cores(): return lax.ppermute(value, 'blk', [(0, 1), (1, 0)])  3.65 us
    pallas_call x1, Pallas kernels, per_device(): call(score_body, [((GROUP, 256, 1024), bf16), ((GROUP, ROWS, D), bf16), (...  1.47 us
    pallas_call x1, Pallas kernels, per_device(): give, = call(second_body, [(pulled, bf16)], 'second', flops)(e, q, sums, v)  1.28 us
    pallas_call x1, Pallas kernels, per_device(): call(norm_body, [(rows, bf16), ((8, 128), f32)], 'norm', 10 ** 9, ins=[pl...  1.18 us
  transfers between devices with their start and end apart: 6, of which 4 were waited for; matrix products, arithmetic and copies ran while one was open for 0% of the time, Pallas kernels for 6%

profile of v6, /device:TPU:1, one launch (start us, length us, event | category | flops | bytes accessed | tf_op | source)
XLA Modules:
  0.0 57.6 jit_solution(11551943209134357477)
XLA Ops:
  0.6 1.4 %collective-permute-start = (bf16[128,256]{1,0:T(8,128)(2,1)}, bf16[128,256]{1,0:T(8,128)(2,1)S(1)}, u32[]{:S(2)}, u32[]{:S(2)}) collective-permute-start(bf16[128,256]{1,0:T(8,128)(2,1)} %q_ref.1), channel_id=1, source_target_pairs={{0,64},{64,0},{1,65},{65,1},{2,66},{66,2},{3,67},{67,3},{4,68},{68... | collective-permute-start | bytes 196616 | tf_op jit(solution)/shard_map/ppermute | solution.py:47
  2.1 0.1 collective-permute-start.1
  2.2 1.2 %norm.1 = (bf16[128,256]{1,0:T(8,128)(2,1)S(1)}, f32[8,128]{1,0:T(8,128)S(1)}) custom-call(bf16[128,256]{1,0:T(8,128)(2,1)} %q_ref.1, bf16[128,256]{1,0:T(8,128)(2,1)} %v_ref.1), custom_call_target="tpu_custom_call" | custom-call | flops 1000000000 | tf_op jit(solution)/shard_map/norm/pallas_call | solution.py:293
  3.3 0.0 collective-permute-done.got_q_ref
  3.4 0.2 collective-permute-done.1.got_v_ref
  3.5 0.2 tile.1
  3.7 16.7 %all_to_all.15.mine_ref = bf16[8,2,128,256]{3,2,1,0:T(8,128)(2,1)S(1)} all-to-all(bf16[8,2,128,256]{3,2,1,0:T(8,128)(2,1)S(1)} %tile.1), channel_id=1, replica_groups={{68,84,100,116,72,88,104,120},{76,92,108,124,64,80,96,112},{69,85,101,1..., dimensions={0} | all-to-all | bytes 2097152 | tf_op jit(solution)/shard_map/all_to_all | solution.py:43
  20.5 0.3 collective-permute-start.2
  20.8 2.4 %collective-permute-done.2.got_ref = bf16[8,2,128,256]{3,2,1,0:T(8,128)(2,1)S(1)} collective-permute-done((bf16[8,2,128,256]{3,2,1,0:T(8,128)(2,1)S(1)}, bf16[8,2,128,256]{3,2,1,0:T(8,128)(2,1)S(1)}, u32[]{:S(2)}, u32[]{:S(2)}) %collective-permute-start.2) | collective-permute-done | bytes 1048608 | tf_op jit(solution)/shard_map/ppermute | solution.py:47
  23.1 1.5 %score.1 = (bf16[8,256,1024]{2,1,0:T(8,128)(2,1)S(1)}, bf16[8,128,256]{2,1,0:T(8,128)(2,1)S(1)}, bf16[8,2,128,256]{3,2,1,0:T(8,128)(2,1)S(1)}, f32[8,16,128]{2,1,0:T(8,128)S(1)}) custom-call(bf16[8,2,128,256]{3,2,1,0:T(8,128)(2,1)S(1)} %all_to_all.15.mine_ref, bf16[8,2,128,256]{3,2,1,0:T(8,128)(2,1)S(1)} %collective-permute-done.2.got_ref, ...), custom_call_target="tpu_custom_call" | custom-call | flops 1073741824 | tf_op jit(solution)/shard_map/score/pallas_call | solution.py:304
  24.6 9.3 %all_to_all.16.s_ref = f32[8,16,128]{2,1,0:T(8,128)S(1)} all-to-all(f32[8,16,128]{2,1,0:T(8,128)S(1)} %get-tuple-element.22), channel_id=1, replica_groups={{0,1,2,3,4,5,6,7},{8,9,10,11,12,13,14,15},{16,17,18,19,20,21,22,23},{24..., dimensions={0} | all-to-all | bytes 131072 | tf_op jit(solution)/shard_map/all_to_all | solution.py:43
  33.9 0.7 %first.1 = (f32[4,256,256]{2,1,0:T(8,128)S(1)}, bf16[1040,256]{1,0:T(8,128)(2,1)S(1)}) custom-call(bf16[8,256,1024]{2,1,0:T(8,128)(2,1)S(1)} %get-tuple-element.20.e_ref, bf16[8,128,256]{2,1,0:T(8,128)(2,1)S(1)} %get-tuple-element.21.q_ref, f32[8,16,128]{2,1,0:T(8,128)S(1)} %all_to_all.16.s_ref), custom_call_target="tpu_custom_call" | custom-call | flops 1073741824 | tf_op jit(solution)/shard_map/first/pallas_call | solution.py:317
  34.6 1.6 %collective-permute-start.3 = (bf16[1040,256]{1,0:T(8,128)(2,1)S(1)}, bf16[1040,256]{1,0:T(8,128)(2,1)S(1)}, u32[]{:S(2)}, u32[]{:S(2)}) collective-permute-start(bf16[1040,256]{1,0:T(8,128)(2,1)S(1)} %get-tuple-element.26), channel_id=1, source_target_pairs={{0,64},{64,0},{1,65},{65,1},{2,66},{66,2},{3,67},{67,3},{4,68},{68... | collective-permute-start | bytes 1597448 | tf_op jit(solution)/shard_map/ppermute | solution.py:47
  36.3 1.3 %second.1 = bf16[1024,256]{1,0:T(8,128)(2,1)S(1)} custom-call(bf16[8,256,1024]{2,1,0:T(8,128)(2,1)S(1)} %get-tuple-element.20.e_ref, bf16[8,128,256]{2,1,0:T(8,128)(2,1)S(1)} %get-tuple-element.21.q_ref, f32[8,16,128]{2,1,0:T(8,128)S(1)} %all_to_all.16.s_ref, bf16[8,2,128,256]{3,2,1,0:T(8,128)(2,1)S(1)} %get-tuple-element.24.v_ref), custom_call_target="tpu_custom_call" | custom-call | flops 1073741824 | tf_op jit(solution)/shard_map/second/pallas_call | solution.py:319
  37.6 0.1 collective-permute-start.4
  37.6 0.7 %third.1 = (f32[4,256,256]{2,1,0:T(8,128)S(1)}, bf16[1024,256]{1,0:T(8,128)(2,1)S(1)}) custom-call(bf16[8,256,1024]{2,1,0:T(8,128)(2,1)S(1)} %get-tuple-element.20.e_ref, bf16[8,128,256]{2,1,0:T(8,128)(2,1)S(1)} %get-tuple-element.21.q_ref, f32[8,16,128]{2,1,0:T(8,128)S(1)} %all_to_all.16.s_ref, bf16[8,2,128,256]{3,2,1,0:T(8,128)(2,1)S(1)} %get-tuple-element.24.v_ref), custom_call_target="tpu_custom_call" | custom-call | flops 1073741824 | tf_op jit(solution)/shard_map/third/pallas_call | solution.py:321
  38.4 1.2 %collective-permute-done.4.got1_ref = bf16[1024,256]{1,0:T(8,128)(2,1)S(1)} collective-permute-done((bf16[1024,256]{1,0:T(8,128)(2,1)S(1)}, bf16[1024,256]{1,0:T(8,128)(2,1)S(1)}, u32[]{:S(2)}, u32[]{:S(2)}) %collective-permute-start.4) | collective-permute-done | bytes 524320 | tf_op jit(solution)/shard_map/ppermute | solution.py:47
  39.5 0.0 collective-permute-done.3.got0_ref
  39.5 0.3 join.1
  39.9 15.2 %all_to_all.17.w_ref = bf16[8,272,256]{2,1,0:T(8,128)(2,1)S(1)} all-to-all(bf16[8,272,256]{2,1,0:T(8,128)(2,1)S(1)} %join.1), channel_id=1, replica_groups={{68,84,100,116,72,88,104,120},{76,92,108,124,64,80,96,112},{69,85,101,1..., dimensions={0} | all-to-all | bytes 2228224 | tf_op jit(solution)/shard_map/all_to_all | solution.py:43
  55.1 0.0 copy-start
  55.1 0.0 copy-start.1
  55.1 0.1 sum.1
  55.2 0.1 collective-permute-start.5
  55.3 1.3 %collective-permute-done.5.got_ref = f32[136,256]{1,0:T(8,128)S(1)} collective-permute-done((f32[136,256]{1,0:T(8,128)S(1)}, f32[136,256]{1,0:T(8,128)S(1)}, u32[]{:S(2)}, u32[]{:S(2)}) %collective-permute-start.5) | collective-permute-done | bytes 139296 | tf_op jit(solution)/shard_map/ppermute | solution.py:47
  56.7 0.0 copy-done
  56.7 0.0 copy-done.1
  56.7 1.0 %final.1 = (f32[128,256]{1,0:T(8,128)}, f32[128,256]{1,0:T(8,128)}, f32[1,1]{1,0:T(1,128)}) custom-call(bf16[128,256]{1,0:T(8,128)(2,1)S(1)} %copy-done, bf16[128,256]{1,0:T(8,128)(2,1)S(1)} %copy-done.1, f32[136,256]{1,0:T(8,128)S(1)} %get-tuple-element.28.keep_ref, f32[136,256]{1,0:T(8,128)S(1)} %collective-permute-done.5.got_ref, ...), custom_call_target="tpu_custom_call" | custom-call | tf_op jit(solution)/shard_map/final/pallas_call | solution.py:325
Async XLA Ops:
  0.6 2.7 %collective-permute-start = (bf16[128,256]{1,0:T(8,128)(2,1)}, bf16[128,256]{1,0:T(8,128)(2,1)S(1)}, u32[]{:S(2)}, u32[]{:S(2)}) collective-permute-start(bf16[128,256]{1,0:T(8,128)(2,1)} %q_ref.1), channel_id=1, source_target_pairs={{0,64},{64,0},{1,65},{65,1},{2,66},{66,2},{3,67},{67,3},{4,68},{68... | collective-permute-start | bytes 196616 | tf_op jit(solution)/shard_map/ppermute | solution.py:47
  2.1 1.5 %collective-permute-start.1 = (bf16[128,256]{1,0:T(8,128)(2,1)}, bf16[128,256]{1,0:T(8,128)(2,1)S(1)}, u32[]{:S(2)}, u32[]{:S(2)}) collective-permute-start(bf16[128,256]{1,0:T(8,128)(2,1)} %v_ref.1), channel_id=1, source_target_pairs={{0,64},{64,0},{1,65},{65,1},{2,66},{66,2},{3,67},{67,3},{4,68},{68... | collective-permute-start | bytes 196616 | tf_op jit(solution)/shard_map/ppermute | solution.py:47
  20.5 2.7 %collective-permute-start.2 = (bf16[8,2,128,256]{3,2,1,0:T(8,128)(2,1)S(1)}, bf16[8,2,128,256]{3,2,1,0:T(8,128)(2,1)S(1)}, u32[]{:S(2)}, u32[]{:S(2)}) collective-permute-start(bf16[8,2,128,256]{3,2,1,0:T(8,128)(2,1)S(1)} %all_to_all.15.mine_ref), channel_id=1, source_target_pairs={{0,64},{64,0},{1,65},{65,1},{2,66},{66,2},{3,67},{67,3},{4,68},{68... | collective-permute-start | bytes 3145736 | tf_op jit(solution)/shard_map/ppermute | solution.py:47
  34.6 4.9 %collective-permute-start.3 = (bf16[1040,256]{1,0:T(8,128)(2,1)S(1)}, bf16[1040,256]{1,0:T(8,128)(2,1)S(1)}, u32[]{:S(2)}, u32[]{:S(2)}) collective-permute-start(bf16[1040,256]{1,0:T(8,128)(2,1)S(1)} %get-tuple-element.26), channel_id=1, source_target_pairs={{0,64},{64,0},{1,65},{65,1},{2,66},{66,2},{3,67},{67,3},{4,68},{68... | collective-permute-start | bytes 1597448 | tf_op jit(solution)/shard_map/ppermute | solution.py:47
  37.6 2.0 %collective-permute-start.4 = (bf16[1024,256]{1,0:T(8,128)(2,1)S(1)}, bf16[1024,256]{1,0:T(8,128)(2,1)S(1)}, u32[]{:S(2)}, u32[]{:S(2)}) collective-permute-start(bf16[1024,256]{1,0:T(8,128)(2,1)S(1)} %second.1), channel_id=1, source_target_pairs={{0,64},{64,0},{1,65},{65,1},{2,66},{66,2},{3,67},{67,3},{4,68},{68... | collective-permute-start | bytes 1572872 | tf_op jit(solution)/shard_map/ppermute | solution.py:47
  55.1 1.6 %copy-start = (bf16[128,256]{1,0:T(8,128)(2,1)S(1)}, bf16[128,256]{1,0:T(8,128)(2,1)}, u32[]{:S(2)}) copy-start(bf16[128,256]{1,0:T(8,128)(2,1)} %q_ref.1) | copy-start | bytes 196612
  55.1 1.6 %copy-start.1 = (bf16[128,256]{1,0:T(8,128)(2,1)S(1)}, bf16[128,256]{1,0:T(8,128)(2,1)}, u32[]{:S(2)}) copy-start(bf16[128,256]{1,0:T(8,128)(2,1)} %v_ref.1) | copy-start | bytes 196612
  55.2 1.4 %collective-permute-start.5 = (f32[136,256]{1,0:T(8,128)S(1)}, f32[136,256]{1,0:T(8,128)S(1)}, u32[]{:S(2)}, u32[]{:S(2)}) collective-permute-start(f32[136,256]{1,0:T(8,128)S(1)} %get-tuple-element.29), channel_id=1, source_target_pairs={{0,64},{64,0},{1,65},{65,1},{2,66},{66,2},{3,67},{67,3},{4,68},{68... | collective-permute-start | bytes 417800 | tf_op jit(solution)/shard_map/ppermute | solution.py:47

commit v7 on v6

--- a/solution.py
+++ b/solution.py
@@ -148,14 +148,18 @@
     return total
 
 
-def split(value):
-    high = value.astype(bf16)
-    low = (value - high.astype(f32)).astype(bf16)
-    return jnp.concatenate([high.astype(f32), low.astype(f32)], axis=0).astype(bf16)
-
-
 def loss_part(sums):
     return jnp.sum(jnp.log(sums[:8])) - jnp.max(sums[8:9])
+
+
+def split(value):
+    high = value.astype(bf16).astype(f32)
+    return jnp.concatenate([high, value - high], axis=1).astype(bf16)
+
+
+def joined(tail):
+    tail = tail.astype(f32)
+    return tail[:, :128] + tail[:, 128:]
 
 
 def weigh(e_ref, q_ref, r, first, store):
@@ -181,19 +185,10 @@
         u_ref[rows, ROWS:] = total[ROWS:, rows].astype(bf16)
 
 
-def first_body(e_ref, q_ref, s_ref, keep_ref, give_ref):
+def first_body(e_ref, q_ref, s_ref, v_ref, give_ref):
+    core = lax.axis_index("blk")
     sums = row_sums(s_ref)
-
-    def store(k, w):
-        keep_ref[k] = w
-        give_ref[k * 256 : (k + 1) * 256] = w.astype(bf16)
-
-    weigh(e_ref, q_ref, 1.0 / sums[:8], 0, store)
-    give_ref[1024:1040] = split(jnp.full((8, D), loss_part(sums), f32))
-
-
-def second_body(e_ref, q_ref, s_ref, v_ref, give_ref):
-    core = lax.axis_index("blk")
+    give_ref[1024:1032] = split(jnp.full((8, 128), loss_part(sums), f32))
 
     @pl.when(core == ITEM)
     def _():
@@ -204,7 +199,26 @@
         def store(k, w):
             give_ref[k * 256 : (k + 1) * 256] = w.astype(bf16)
 
-        weigh(e_ref, q_ref, 1.0 / row_sums(s_ref)[:8], 4, store)
+        weigh(e_ref, q_ref, 1.0 / sums[:8], 0, store)
+
+
+def second_body(e_ref, q_ref, s_ref, keep_ref, give_ref):
+    core = lax.axis_index("blk")
+    r = 1.0 / row_sums(s_ref)[:8]
+
+    @pl.when(core == ITEM)
+    def _():
+        def store(k, w):
+            keep_ref[k] = w
+
+        weigh(e_ref, q_ref, r, 0, store)
+
+    @pl.when(core != ITEM)
+    def _():
+        def store(k, w):
+            give_ref[k * 256 : (k + 1) * 256] = w.astype(bf16)
+
+        weigh(e_ref, q_ref, r, 4, store)
 
 
 def third_body(e_ref, q_ref, s_ref, v_ref, keep_ref, u_ref):
@@ -237,12 +251,11 @@
         for k in range(GROUP):
             rows = slice(k * ROWS, (k + 1) * ROWS)
             out_ref[k, (1 - ITEM) * 128 : (2 - ITEM) * 128] = u_ref[rows]
-            out_ref[k, ITEM * 128 : (ITEM + 1) * 128] = got1_ref[rows]
-
-    got = got0_ref[1024:1040].astype(f32)
-    tail = split(got[:8] + got[8:] + loss_part(row_sums(s_ref)))
+            out_ref[k, ITEM * 128 : (ITEM + 1) * 128] = got0_ref[rows]
+
+    tail = split(joined(got0_ref[1024:1032]) + loss_part(row_sums(s_ref)))
     for k in range(GROUP):
-        out_ref[k, 256:272] = tail
+        out_ref[k, 256:264] = tail
 
 
 def sum_body(w_ref, keep_ref, give_ref):
@@ -255,8 +268,7 @@
             total = total + w_ref[k, at].astype(f32)
         return total
 
-    tail = summed(256, 16)
-    tail = tail[:8] + tail[8:]
+    tail = jnp.concatenate([joined(summed(256, 8))] * 2, axis=1)
     keep_ref[:128] = summed(pl.multiple_of(core * 128, 128), 128)
     give_ref[:128] = summed(pl.multiple_of((1 - core) * 128, 128), 128)
     keep_ref[128:136] = tail
@@ -314,12 +326,12 @@
     )(block, swap_cores(block), pos)
     sums = exchange(s, QUERY)
     half, pulled = (4, 256, D), (GROUP * ROWS, D)
-    keep0, give = call(first_body, [(half, f32), ((1040, D), bf16)], "first", flops)(e, q, sums)
+    (give,) = call(first_body, [((1032, D), bf16)], "first", flops)(e, q, sums, v)
     got0 = swap_cores(give)
-    (give,) = call(second_body, [(pulled, bf16)], "second", flops)(e, q, sums, v)
+    keep0, give = call(second_body, [(half, f32), (pulled, bf16)], "second", flops)(e, q, sums)
     got1 = swap_cores(give)
     keep1, u = call(third_body, [(half, f32), (pulled, bf16)], "third", flops)(e, q, sums, v)
-    (out,) = call(join_body, [((GROUP, 272, D), bf16)], "join")(keep0, keep1, got0, got1, u, sums)
+    (out,) = call(join_body, [((GROUP, 264, D), bf16)], "join")(keep0, keep1, got0, got1, u, sums)
     out = exchange(out, BULK)
     keep, give = call(sum_body, [((136, D), f32), ((136, D), f32)], "sum")(out)
     q_slope, v_slope, loss = call(

time: 57.9 us -> 57.5 us (level)
  transfers between devices with their start and end apart: 6 -> 6, of which waited for: 4 -> 4; matrix products, arithmetic and copies ran while one was open for 0% -> 0% of each run, Pallas kernels for 6% -> 5%
where the time goes in v7:
time: 57.5 us; the launch traced here: 57.2 us
  blocking collectives  41.1 us (71%)
  Pallas kernels  7.22 us (13%)
  waiting for transfers between devices  5.03 us (9%)
  starting transfers between devices  3.1 us (5%)
  between operations  0.71 us (1%)
    all_to_all x3, blocking collectives, exchange(): lax.all_to_all(pieces, AXES, 0, 0, tiled=True, axis_index_groups=groups)  41.1 us
    ppermute x6, waiting for transfers between devices, swap_cores(): return lax.ppermute(value, 'blk', [(0, 1), (1, 0)])  5.03 us
    ppermute x6, starting transfers between devices, swap_cores(): return lax.ppermute(value, 'blk', [(0, 1), (1, 0)])  3.1 us
    pallas_call x1, Pallas kernels, per_device(): call(score_body, [((GROUP, 256, 1024), bf16), ((GROUP, ROWS, D), bf16), (...  1.47 us
    pallas_call x1, Pallas kernels, per_device(): give, = call(first_body, [((1032, D), bf16)], 'first', flops)(e, q, sums, v)  1.41 us
    pallas_call x1, Pallas kernels, per_device(): call(norm_body, [(rows, bf16), ((8, 128), f32)], 'norm', 10 ** 9, ins=[pl...  1.18 us
  transfers between devices with their start and end apart: 6, of which 4 were waited for; matrix products, arithmetic and copies ran while one was open for 0% of the time, Pallas kernels for 5%

profile of v7, /device:TPU:1, one launch (start us, length us, event | category | flops | bytes accessed | tf_op | source)
XLA Modules:
  0.0 57.2 jit_solution(8988767632472812102)
XLA Ops:
  0.6 1.4 %collective-permute-start = (bf16[128,256]{1,0:T(8,128)(2,1)}, bf16[128,256]{1,0:T(8,128)(2,1)S(1)}, u32[]{:S(2)}, u32[]{:S(2)}) collective-permute-start(bf16[128,256]{1,0:T(8,128)(2,1)} %q_ref.1), channel_id=1, source_target_pairs={{0,64},{64,0},{1,65},{65,1},{2,66},{66,2},{3,67},{67,3},{4,68},{68... | collective-permute-start | bytes 196616 | tf_op jit(solution)/shard_map/ppermute | solution.py:47
  2.1 0.1 collective-permute-start.1
  2.2 1.2 %norm.1 = (bf16[128,256]{1,0:T(8,128)(2,1)S(1)}, f32[8,128]{1,0:T(8,128)S(1)}) custom-call(bf16[128,256]{1,0:T(8,128)(2,1)} %q_ref.1, bf16[128,256]{1,0:T(8,128)(2,1)} %v_ref.1), custom_call_target="tpu_custom_call" | custom-call | flops 1000000000 | tf_op jit(solution)/shard_map/norm/pallas_call | solution.py:305
  3.3 0.0 collective-permute-done.got_q_ref
  3.4 0.2 collective-permute-done.1.got_v_ref
  3.5 0.2 tile.1
  3.7 16.7 %all_to_all.15.mine_ref = bf16[8,2,128,256]{3,2,1,0:T(8,128)(2,1)S(1)} all-to-all(bf16[8,2,128,256]{3,2,1,0:T(8,128)(2,1)S(1)} %tile.1), channel_id=1, replica_groups={{68,84,100,116,72,88,104,120},{76,92,108,124,64,80,96,112},{69,85,101,1..., dimensions={0} | all-to-all | bytes 2097152 | tf_op jit(solution)/shard_map/all_to_all | solution.py:43
  20.5 0.3 collective-permute-start.2
  20.8 2.4 %collective-permute-done.2.got_ref = bf16[8,2,128,256]{3,2,1,0:T(8,128)(2,1)S(1)} collective-permute-done((bf16[8,2,128,256]{3,2,1,0:T(8,128)(2,1)S(1)}, bf16[8,2,128,256]{3,2,1,0:T(8,128)(2,1)S(1)}, u32[]{:S(2)}, u32[]{:S(2)}) %collective-permute-start.2) | collective-permute-done | bytes 1048608 | tf_op jit(solution)/shard_map/ppermute | solution.py:47
  23.1 1.5 %score.1 = (bf16[8,256,1024]{2,1,0:T(8,128)(2,1)S(1)}, bf16[8,128,256]{2,1,0:T(8,128)(2,1)S(1)}, bf16[8,2,128,256]{3,2,1,0:T(8,128)(2,1)S(1)}, f32[8,16,128]{2,1,0:T(8,128)S(1)}) custom-call(bf16[8,2,128,256]{3,2,1,0:T(8,128)(2,1)S(1)} %all_to_all.15.mine_ref, bf16[8,2,128,256]{3,2,1,0:T(8,128)(2,1)S(1)} %collective-permute-done.2.got_ref, ...), custom_call_target="tpu_custom_call" | custom-call | flops 1073741824 | tf_op jit(solution)/shard_map/score/pallas_call | solution.py:316
  24.6 9.3 %all_to_all.16.s_ref = f32[8,16,128]{2,1,0:T(8,128)S(1)} all-to-all(f32[8,16,128]{2,1,0:T(8,128)S(1)} %get-tuple-element.22), channel_id=1, replica_groups={{0,1,2,3,4,5,6,7},{8,9,10,11,12,13,14,15},{16,17,18,19,20,21,22,23},{24..., dimensions={0} | all-to-all | bytes 131072 | tf_op jit(solution)/shard_map/all_to_all | solution.py:43
  33.9 1.4 %first.1 = bf16[1032,256]{1,0:T(8,128)(2,1)S(1)} custom-call(bf16[8,256,1024]{2,1,0:T(8,128)(2,1)S(1)} %get-tuple-element.20.e_ref, bf16[8,128,256]{2,1,0:T(8,128)(2,1)S(1)} %get-tuple-element.21.q_ref, f32[8,16,128]{2,1,0:T(8,128)S(1)} %all_to_all.16.s_ref, bf16[8,2,128,256]{3,2,1,0:T(8,128)(2,1)S(1)} %get-tuple-element.24.v_ref), custom_call_target="tpu_custom_call" | custom-call | flops 1073741824 | tf_op jit(solution)/shard_map/first/pallas_call | solution.py:329
  35.3 1.1 %collective-permute-start.3 = (bf16[1032,256]{1,0:T(8,128)(2,1)S(1)}, bf16[1032,256]{1,0:T(8,128)(2,1)S(1)}, u32[]{:S(2)}, u32[]{:S(2)}) collective-permute-start(bf16[1032,256]{1,0:T(8,128)(2,1)S(1)} %first.1), channel_id=1, source_target_pairs={{0,64},{64,0},{1,65},{65,1},{2,66},{66,2},{3,67},{67,3},{4,68},{68... | collective-permute-start | bytes 1585160 | tf_op jit(solution)/shard_map/ppermute | solution.py:47
  36.4 0.7 %second.1 = (f32[4,256,256]{2,1,0:T(8,128)S(1)}, bf16[1024,256]{1,0:T(8,128)(2,1)S(1)}) custom-call(bf16[8,256,1024]{2,1,0:T(8,128)(2,1)S(1)} %get-tuple-element.20.e_ref, bf16[8,128,256]{2,1,0:T(8,128)(2,1)S(1)} %get-tuple-element.21.q_ref, f32[8,16,128]{2,1,0:T(8,128)S(1)} %all_to_all.16.s_ref), custom_call_target="tpu_custom_call" | custom-call | flops 1073741824 | tf_op jit(solution)/shard_map/second/pallas_call | solution.py:331
  37.1 0.1 collective-permute-start.4
  37.2 0.7 %third.1 = (f32[4,256,256]{2,1,0:T(8,128)S(1)}, bf16[1024,256]{1,0:T(8,128)(2,1)S(1)}) custom-call(bf16[8,256,1024]{2,1,0:T(8,128)(2,1)S(1)} %get-tuple-element.20.e_ref, bf16[8,128,256]{2,1,0:T(8,128)(2,1)S(1)} %get-tuple-element.21.q_ref, f32[8,16,128]{2,1,0:T(8,128)S(1)} %all_to_all.16.s_ref, bf16[8,2,128,256]{3,2,1,0:T(8,128)(2,1)S(1)} %get-tuple-element.24.v_ref), custom_call_target="tpu_custom_call" | custom-call | flops 1073741824 | tf_op jit(solution)/shard_map/third/pallas_call | solution.py:333
  38.0 1.2 %collective-permute-done.4.got1_ref = bf16[1024,256]{1,0:T(8,128)(2,1)S(1)} collective-permute-done((bf16[1024,256]{1,0:T(8,128)(2,1)S(1)}, bf16[1024,256]{1,0:T(8,128)(2,1)S(1)}, u32[]{:S(2)}, u32[]{:S(2)}) %collective-permute-start.4) | collective-permute-done | bytes 524320 | tf_op jit(solution)/shard_map/ppermute | solution.py:47
  39.1 0.0 collective-permute-done.3.got0_ref
  39.1 0.4 join.1
  39.5 15.1 %all_to_all.17.w_ref = bf16[8,264,256]{2,1,0:T(8,128)(2,1)S(1)} all-to-all(bf16[8,264,256]{2,1,0:T(8,128)(2,1)S(1)} %join.1), channel_id=1, replica_groups={{68,84,100,116,72,88,104,120},{76,92,108,124,64,80,96,112},{69,85,101,1..., dimensions={0} | all-to-all | bytes 2162688 | tf_op jit(solution)/shard_map/all_to_all | solution.py:43
  54.6 0.0 copy-start
  54.6 0.0 copy-start.1
  54.6 0.1 sum.1
  54.8 0.1 collective-permute-start.5
  54.9 1.3 %collective-permute-done.5.got_ref = f32[136,256]{1,0:T(8,128)S(1)} collective-permute-done((f32[136,256]{1,0:T(8,128)S(1)}, f32[136,256]{1,0:T(8,128)S(1)}, u32[]{:S(2)}, u32[]{:S(2)}) %collective-permute-start.5) | collective-permute-done | bytes 139296 | tf_op jit(solution)/shard_map/ppermute | solution.py:47
  56.2 0.0 copy-done
  56.2 0.0 copy-done.1
  56.2 1.0 %final.1 = (f32[128,256]{1,0:T(8,128)}, f32[128,256]{1,0:T(8,128)}, f32[1,1]{1,0:T(1,128)}) custom-call(bf16[128,256]{1,0:T(8,128)(2,1)S(1)} %copy-done, bf16[128,256]{1,0:T(8,128)(2,1)S(1)} %copy-done.1, f32[136,256]{1,0:T(8,128)S(1)} %get-tuple-element.28.keep_ref, f32[136,256]{1,0:T(8,128)S(1)} %collective-permute-done.5.got_ref, ...), custom_call_target="tpu_custom_call" | custom-call | tf_op jit(solution)/shard_map/final/pallas_call | solution.py:337
Async XLA Ops:
  0.6 2.7 %collective-permute-start = (bf16[128,256]{1,0:T(8,128)(2,1)}, bf16[128,256]{1,0:T(8,128)(2,1)S(1)}, u32[]{:S(2)}, u32[]{:S(2)}) collective-permute-start(bf16[128,256]{1,0:T(8,128)(2,1)} %q_ref.1), channel_id=1, source_target_pairs={{0,64},{64,0},{1,65},{65,1},{2,66},{66,2},{3,67},{67,3},{4,68},{68... | collective-permute-start | bytes 196616 | tf_op jit(solution)/shard_map/ppermute | solution.py:47
  2.1 1.5 %collective-permute-start.1 = (bf16[128,256]{1,0:T(8,128)(2,1)}, bf16[128,256]{1,0:T(8,128)(2,1)S(1)}, u32[]{:S(2)}, u32[]{:S(2)}) collective-permute-start(bf16[128,256]{1,0:T(8,128)(2,1)} %v_ref.1), channel_id=1, source_target_pairs={{0,64},{64,0},{1,65},{65,1},{2,66},{66,2},{3,67},{67,3},{4,68},{68... | collective-permute-start | bytes 196616 | tf_op jit(solution)/shard_map/ppermute | solution.py:47
  20.5 2.7 %collective-permute-start.2 = (bf16[8,2,128,256]{3,2,1,0:T(8,128)(2,1)S(1)}, bf16[8,2,128,256]{3,2,1,0:T(8,128)(2,1)S(1)}, u32[]{:S(2)}, u32[]{:S(2)}) collective-permute-start(bf16[8,2,128,256]{3,2,1,0:T(8,128)(2,1)S(1)} %all_to_all.15.mine_ref), channel_id=1, source_target_pairs={{0,64},{64,0},{1,65},{65,1},{2,66},{66,2},{3,67},{67,3},{4,68},{68... | collective-permute-start | bytes 3145736 | tf_op jit(solution)/shard_map/ppermute | solution.py:47
  35.3 3.8 %collective-permute-start.3 = (bf16[1032,256]{1,0:T(8,128)(2,1)S(1)}, bf16[1032,256]{1,0:T(8,128)(2,1)S(1)}, u32[]{:S(2)}, u32[]{:S(2)}) collective-permute-start(bf16[1032,256]{1,0:T(8,128)(2,1)S(1)} %first.1), channel_id=1, source_target_pairs={{0,64},{64,0},{1,65},{65,1},{2,66},{66,2},{3,67},{67,3},{4,68},{68... | collective-permute-start | bytes 1585160 | tf_op jit(solution)/shard_map/ppermute | solution.py:47
  37.1 2.0 %collective-permute-start.4 = (bf16[1024,256]{1,0:T(8,128)(2,1)S(1)}, bf16[1024,256]{1,0:T(8,128)(2,1)S(1)}, u32[]{:S(2)}, u32[]{:S(2)}) collective-permute-start(bf16[1024,256]{1,0:T(8,128)(2,1)S(1)} %get-tuple-element.26), channel_id=1, source_target_pairs={{0,64},{64,0},{1,65},{65,1},{2,66},{66,2},{3,67},{67,3},{4,68},{68... | collective-permute-start | bytes 1572872 | tf_op jit(solution)/shard_map/ppermute | solution.py:47
  54.6 1.6 %copy-start = (bf16[128,256]{1,0:T(8,128)(2,1)S(1)}, bf16[128,256]{1,0:T(8,128)(2,1)}, u32[]{:S(2)}) copy-start(bf16[128,256]{1,0:T(8,128)(2,1)} %q_ref.1) | copy-start | bytes 196612
  54.6 1.6 %copy-start.1 = (bf16[128,256]{1,0:T(8,128)(2,1)S(1)}, bf16[128,256]{1,0:T(8,128)(2,1)}, u32[]{:S(2)}) copy-start(bf16[128,256]{1,0:T(8,128)(2,1)} %v_ref.1) | copy-start | bytes 196612
  54.8 1.4 %collective-permute-start.5 = (f32[136,256]{1,0:T(8,128)S(1)}, f32[136,256]{1,0:T(8,128)S(1)}, u32[]{:S(2)}, u32[]{:S(2)}) collective-permute-start(f32[136,256]{1,0:T(8,128)S(1)} %get-tuple-element.29), channel_id=1, source_target_pairs={{0,64},{64,0},{1,65},{65,1},{2,66},{66,2},{3,67},{67,3},{4,68},{68... | collective-permute-start | bytes 417800 | tf_op jit(solution)/shard_map/ppermute | solution.py:47

commit v8 on v7

v8 whole, which is shorter than its diff:
```python
import math

import jax
import jax.numpy as jnp
from jax import lax
from jax.experimental import pallas as pl
from jax.experimental.pallas import tpu as pltpu
from jax.sharding import Mesh
from jax.sharding import PartitionSpec as P

AXES = ("blk", "z", "y", "x")
GROUP = 8
ROWS, D = 128, 256
ITEM = 1

sharpness = 0.05
tiny_square = 1e-12
log2_e = math.log2(math.e)
f32, bf16 = jnp.float32, jnp.bfloat16


def device_of(core, z, y, x):
    return ((core * 4 + z) * 4 + y) * 4 + x


def query_groups(core):
    return [[device_of(core, z, y, x) for y in pair for x in range(4)] for z in range(4) for pair in ((0, 1), (2, 3))]


def item_groups(core):
    return [[device_of(core, z, y, x) for y in pair for z in range(4)] for x in range(4) for pair in ((1, 2), (3, 0))]


def query_index():
    return lax.axis_index("y") % 2 * 4 + lax.axis_index("x")


BULK = item_groups(ITEM) + query_groups(1 - ITEM)
QUERY = query_groups(0) + query_groups(1)


def exchange(pieces, groups):
    return lax.all_to_all(pieces, AXES, 0, 0, tiled=True, axis_index_groups=groups)


def swap_cores(value):
    return lax.ppermute(value, "blk", [(0, 1), (1, 0)])


def call(body, outs, name, flops=0, ins=None, scratch=()):
    spec = pl.BlockSpec(memory_space=pltpu.VMEM)
    return pl.pallas_call(
        body,
        out_shape=[jax.ShapeDtypeStruct(s, d) for s, d, *_ in outs],
        out_specs=[pl.BlockSpec(memory_space=o[2]) if len(o) > 2 else spec for o in outs],
        **({"in_specs": ins} if ins else {}),
        scratch_shapes=list(scratch),
        compiler_params=pltpu.CompilerParams(vmem_limit_bytes=24 * 2**20),
        cost_estimate=pl.CostEstimate(flops=flops, bytes_accessed=0, transcendentals=0),
        name=name,
    )


def unit(matrix):
    wide = matrix.astype(f32)
    length = jnp.sqrt(jnp.sum(wide * wide, axis=1, keepdims=True) + tiny_square)
    return wide / length, length


def hat(matrix):
    return unit(matrix)[0].astype(bf16)


def norm_body(q_hbm, v_hbm, mine_ref, pos_ref, q_ref, v_ref, sem):
    copies = [
        pltpu.make_async_copy(q_hbm, q_ref, sem.at[0]),
        pltpu.make_async_copy(v_hbm, v_ref, sem.at[1]),
    ]
    for c in copies:
        c.start()
    core = lax.axis_index("blk")
    for c in copies:
        c.wait()
    q, v = hat(q_ref[...]), hat(v_ref[...])
    total = jnp.sum(q.astype(f32) * v.astype(f32)) / sharpness
    pos_ref[...] = jnp.full((8, 128), total, f32)

    @pl.when(core == ITEM)
    def _():
        mine_ref[...] = v

    @pl.when(core != ITEM)
    def _():
        mine_ref[...] = q


def tile_body(mine_ref, got_q_ref, got_v_ref, out_ref):
    core = lax.axis_index("blk")

    def fill(got_ref):
        mine, got = mine_ref[...], hat(got_ref[...])
        for k in range(GROUP):
            out_ref[k, core] = mine
            out_ref[k, 1 - core] = got

    @pl.when(core == ITEM)
    def _():
        fill(got_v_ref)

    @pl.when(core != ITEM)
    def _():
        fill(got_q_ref)


def half_body(block_ref, out_ref):
    core = lax.axis_index("blk")

    @pl.when(core == ITEM)
    def _():
        out_ref[...] = block_ref[:4].reshape(GROUP, ROWS, D)

    @pl.when(core != ITEM)
    def _():
        out_ref[...] = block_ref[:, ITEM]


def rest_body(block_ref, out_ref):
    out_ref[...] = block_ref[4:].reshape(GROUP, ROWS, D)


def scores(v_ref, q_ref, e_ref):
    q = q_ref[...].reshape(GROUP * ROWS, D)
    total = jnp.zeros((1, GROUP * ROWS), f32)
    for k in range(4):
        v = v_ref[k].reshape(2 * ROWS, D)
        t = lax.dot_general(v, q, (((1,), (1,)), ((), ())), preferred_element_type=f32)
        e = jnp.exp2(t * (log2_e / sharpness))
        total = total + jnp.sum(e, axis=0, keepdims=True)
        e_ref[k] = e.astype(bf16)
    return total


def score0_body(block_ref, got_ref, e_ref, q_ref, v_ref, t_ref):
    core = lax.axis_index("blk")

    @pl.when(core == ITEM)
    def _():
        v_ref[...] = block_ref[:4]
        q_ref[...] = got_ref[...]

    @pl.when(core != ITEM)
    def _():
        v_ref[...] = got_ref[...].reshape(4, 2, ROWS, D)
        q_ref[...] = block_ref[:, 1 - ITEM]

    t_ref[...] = jnp.broadcast_to(scores(v_ref, q_ref, e_ref), t_ref.shape)


def score1_body(block_ref, got_ref, q_ref, t_ref, pos_ref, e_ref, v_ref, s_ref):
    core = lax.axis_index("blk")

    @pl.when(core == ITEM)
    def _():
        v_ref[...] = block_ref[4:]

    @pl.when(core != ITEM)
    def _():
        v_ref[...] = got_ref[...].reshape(4, 2, ROWS, D)

    total = t_ref[:1] + scores(v_ref, q_ref, e_ref)
    for k in range(GROUP):
        for j in range(GROUP):
            s_ref[j, k : k + 1] = total[:, k * ROWS : (k + 1) * ROWS]
    for j in range(GROUP):
        s_ref[j, 8:16] = pos_ref[...]


def row_sums(s_ref):
    total = s_ref[0]
    for j in range(1, GROUP):
        total = total + s_ref[j]
    return total


def loss_part(sums):
    return jnp.sum(jnp.log(sums[:8])) - jnp.max(sums[8:9])


def split(value):
    high = value.astype(bf16).astype(f32)
    return jnp.concatenate([high, value - high], axis=1).astype(bf16)


def joined(tail):
    tail = tail.astype(f32)
    return tail[:, :128] + tail[:, 128:]


def weigh(e_ref, q_ref, r, store):
    q = q_ref[...].reshape(GROUP * ROWS, D)
    for k in range(4):
        parts = [
            (e_ref[k, :, j * ROWS : (j + 1) * ROWS].astype(f32) * r[j : j + 1]).astype(bf16)
            for j in range(GROUP)
        ]
        store(k, jnp.dot(jnp.concatenate(parts, axis=1), q, preferred_element_type=f32))


def pull(v_refs, e_refs, u_ref):
    total = None
    for v_ref, e_ref in zip(v_refs, e_refs):
        for k in (0, 2):
            v = v_ref[k : k + 2].reshape(4 * ROWS, D)
            e = e_ref[k : k + 2].reshape(4 * ROWS, GROUP * ROWS)
            part = lax.dot_general(v, e, (((0,), (0,)), ((), ())), preferred_element_type=f32)
            total = part if total is None else total + part
    for k in range(GROUP):
        rows = slice(k * ROWS, (k + 1) * ROWS)
        u_ref[rows, :ROWS] = total[:ROWS, rows].astype(bf16)
        u_ref[rows, ROWS:] = total[ROWS:, rows].astype(bf16)


def into(ref):
    def store(k, w):
        ref[k * 256 : (k + 1) * 256] = w.astype(bf16)

    return store


def first_body(e0_ref, e1_ref, v0_ref, v1_ref, q_ref, s_ref, give_ref):
    core = lax.axis_index("blk")
    sums = row_sums(s_ref)
    give_ref[1024:1032] = split(jnp.full((8, 128), loss_part(sums), f32))

    @pl.when(core == ITEM)
    def _():
        pull((v0_ref, v1_ref), (e0_ref, e1_ref), give_ref)

    @pl.when(core != ITEM)
    def _():
        weigh(e0_ref, q_ref, 1.0 / sums[:8], into(give_ref))


def second_body(e1_ref, q_ref, s_ref, give_ref):
    @pl.when(lax.axis_index("blk") != ITEM)
    def _():
        weigh(e1_ref, q_ref, 1.0 / row_sums(s_ref)[:8], into(give_ref))


def third_body(e0_ref, e1_ref, v0_ref, v1_ref, q_ref, s_ref, keep_ref, u_ref):
    core = lax.axis_index("blk")

    @pl.when(core == ITEM)
    def _():
        r = 1.0 / row_sums(s_ref)[:8]
        for first, e_ref in ((0, e0_ref), (4, e1_ref)):

            def store(k, w):
                keep_ref[first + k] = w

            weigh(e_ref, q_ref, r, store)

    @pl.when(core != ITEM)
    def _():
        pull((v0_ref, v1_ref), (e0_ref, e1_ref), u_ref)


def merge_body(keep_ref, u_ref, got_ref, s_ref, out_ref):
    core = lax.axis_index("blk")

    @pl.when(core == ITEM)
    def _():
        for k in range(4):
            got = got_ref[k * 256 : (k + 1) * 256].astype(f32)
            out_ref[k, :256] = (keep_ref[k] + got).astype(bf16)

    @pl.when(core != ITEM)
    def _():
        for k in range(GROUP):
            rows = slice(k * ROWS, (k + 1) * ROWS)
            out_ref[k, (1 - ITEM) * 128 : (2 - ITEM) * 128] = u_ref[rows]
            out_ref[k, ITEM * 128 : (ITEM + 1) * 128] = got_ref[rows]

    tail = split(joined(got_ref[1024:1032]) + loss_part(row_sums(s_ref)))
    for k in range(GROUP):
        out_ref[k, 256:264] = tail


def join_body(part_ref, keep_ref, got_ref, out_ref):
    core = lax.axis_index("blk")
    out_ref[:4] = part_ref[:4]
    out_ref[4:, 256:264] = part_ref[4:, 256:264]

    @pl.when(core == ITEM)
    def _():
        for k in range(4):
            got = got_ref[k * 256 : (k + 1) * 256].astype(f32)
            out_ref[4 + k, :256] = (keep_ref[4 + k] + got).astype(bf16)

    @pl.when(core != ITEM)
    def _():
        out_ref[4:, :256] = part_ref[4:, :256]


def summed(w_ref, first, rows):
    at = pl.ds(first, rows)
    total = w_ref[0, at].astype(f32)
    for k in range(1, GROUP):
        total = total + w_ref[k, at].astype(f32)
    return total


def give_body(w_ref, give_ref):
    core = lax.axis_index("blk")
    give_ref[:128] = summed(w_ref, pl.multiple_of((1 - core) * 128, 128), 128)
    give_ref[128:136] = jnp.concatenate([joined(summed(w_ref, 256, 8))] * 2, axis=1)


def slope(pull, hat, direction, length):
    grad = (pull - hat) / sharpness
    along = jnp.sum(direction * grad, axis=1, keepdims=True)
    return (grad - direction * along) / length


def query_slope(u, q_ref, v_ref, s_ref):
    q, q_len = unit(q_ref[...])
    sums = row_sums(s_ref)[:8]
    mine = lax.broadcasted_iota(jnp.int32, sums.shape, 0) == query_index()
    own = jnp.sum(jnp.where(mine, sums, 0.0), axis=0, keepdims=True)
    u = jnp.concatenate([(u[:, :128] / own).T, (u[:, 128:] / own).T], axis=1)
    return slope(u, hat(v_ref[...]).astype(f32), q, q_len)


def item_slope(w, q_ref, v_ref):
    v, v_len = unit(v_ref[...])
    return slope(w, hat(q_ref[...]).astype(f32), v, v_len)


def own_body(w_ref, q_ref, v_ref, s_ref, own_ref):
    core = lax.axis_index("blk")
    own = summed(w_ref, pl.multiple_of(core * 128, 128), 128)

    @pl.when(core == ITEM)
    def _():
        own_ref[...] = item_slope(own, q_ref, v_ref)

    @pl.when(core != ITEM)
    def _():
        own_ref[...] = query_slope(own, q_ref, v_ref, s_ref)


def final_body(q_ref, v_ref, own_ref, give_ref, got_ref, s_ref, qs_ref, vs_ref, loss_ref):
    core = lax.axis_index("blk")

    @pl.when(core == ITEM)
    def _():
        vs_ref[...] = own_ref[...]
        qs_ref[...] = query_slope(got_ref[:128], q_ref, v_ref, s_ref)
        loss_ref[0, 0] = jnp.max(give_ref[128:136]) / (128 * 128)

    @pl.when(core != ITEM)
    def _():
        qs_ref[...] = own_ref[...]
        vs_ref[...] = item_slope(got_ref[:128], q_ref, v_ref)
        loss_ref[0, 0] = jnp.max(got_ref[128:136]) / (128 * 128)


def per_device(queries, items):
    rows = (ROWS, D)
    bulk = (GROUP, 2, ROWS, D)
    in_hbm = [pltpu.with_memory_space_constraint(a, pltpu.HBM) for a in (queries, items)]
    mine, pos = call(
        norm_body,
        [(rows, bf16), ((8, 128), f32)],
        "norm",
        10**9,
        ins=[pl.BlockSpec(memory_space=pltpu.HBM)] * 2,
        scratch=[pltpu.VMEM(rows, bf16), pltpu.VMEM(rows, bf16), pltpu.SemaphoreType.DMA((2,))],
    )(*in_hbm)
    (tile,) = call(tile_body, [(bulk, bf16)], "tile")(mine, swap_cores(queries), swap_cores(items))
    block = exchange(tile, BULK)
    flops = 2 * 2048 * 1024 * 256
    cut = (GROUP, ROWS, D)
    (a,) = call(half_body, [(cut, bf16)], "half")(block)
    got_a = swap_cores(a)
    (b,) = call(rest_body, [(cut, bf16)], "rest")(block)
    got_b = swap_cores(b)
    scored = ((4, 256, 1024), bf16)
    v_half = ((4, 2, ROWS, D), bf16)
    e0, q, v0, t = call(
        score0_body, [scored, (cut, bf16), v_half, ((8, GROUP * ROWS), f32)], "score0", flops
    )(block, got_a)
    e1, v1, s = call(
        score1_body, [scored, v_half, ((GROUP, 16, 128), f32)], "score1", flops
    )(block, got_b, q, t, pos)
    sums = exchange(s, QUERY)
    pulled = (GROUP * ROWS, D)
    (give,) = call(first_body, [((1032, D), bf16)], "first", flops)(e0, e1, v0, v1, q, sums)
    got0 = swap_cores(give)
    (give,) = call(second_body, [(pulled, bf16)], "second", flops)(e1, q, sums)
    got1 = swap_cores(give)
    keep, u = call(
        third_body, [((GROUP, 256, D), f32), (pulled, bf16)], "third", flops
    )(e0, e1, v0, v1, q, sums)
    packed = (GROUP, 264, D)
    (part,) = call(merge_body, [(packed, bf16)], "merge", flops)(keep, u, got0, sums)
    (out,) = call(join_body, [(packed, bf16)], "join")(part, keep, got1)
    out = exchange(out, BULK)
    (give,) = call(give_body, [((136, D), f32)], "give")(out)
    got = swap_cores(give)
    (own,) = call(own_body, [(rows, f32)], "own", flops)(out, queries, items, sums)
    q_slope, v_slope, loss = call(
        final_body, [(rows, f32), (rows, f32), ((1, 1), f32, pltpu.SMEM)], "final"
    )(queries, items, own, give, got, sums)
    return loss.reshape(()), q_slope, v_slope


def solution(mesh):
    split = Mesh(mesh.devices.reshape(2, 4, 4, 4), AXES)
    rows = P(AXES, None)
    return jax.shard_map(
        per_device, mesh=split, in_specs=(rows, rows), out_specs=(P(), rows, rows), check_vma=False
    )
```

time: 57.5 us -> 56.5 us (0.983)
  waiting for transfers between devices: 5.03 us -> 2.46 us
  starting transfers between devices: 3.1 us -> 4.2 us
    ppermute x6 -> x7, waiting for transfers between devices: 5.03 us -> 2.46 us  [swap_cores(): return lax.ppermute(value, 'blk', [(0, 1), (1, 0)])]
    ppermute x6 -> x7, starting transfers between devices: 3.1 us -> 4.2 us  [swap_cores(): return lax.ppermute(value, 'blk', [(0, 1), (1, 0)])]
    pallas_call x6 -> x11, Pallas kernels: 4.87 us -> 5.2 us  [the longest x1 1.41 us: per_device(): call(first_body, [((1032, D), bf16)], 'first', flops)]
  transfers between devices with their start and end apart: 6 -> 7, of which waited for: 4 -> 3; matrix products, arithmetic and copies ran while one was open for 0% -> 0% of each run, Pallas kernels for 5% -> 7%
where the time goes in v8:
time: 56.5 us; the launch traced here: 56.2 us
  blocking collectives  41.3 us (73%)
  Pallas kernels  7.54 us (13%)
  starting transfers between devices  4.2 us (7%)
  waiting for transfers between devices  2.46 us (4%)
  between operations  0.78 us (1%)
    all_to_all x3, blocking collectives, exchange(): lax.all_to_all(pieces, AXES, 0, 0, tiled=True, axis_index_groups=groups)  41.3 us
    ppermute x7, starting transfers between devices, swap_cores(): return lax.ppermute(value, 'blk', [(0, 1), (1, 0)])  4.2 us
    ppermute x7, waiting for transfers between devices, swap_cores(): return lax.ppermute(value, 'blk', [(0, 1), (1, 0)])  2.46 us
    pallas_call x1, Pallas kernels, per_device(): call(first_body, [((1032, D), bf16)], 'first', flops)  1.41 us
    pallas_call x1, Pallas kernels, per_device(): call(third_body, [((GROUP, 256, D), f32), (pulled, bf16)], 'third', flops)  1.25 us
    pallas_call x1, Pallas kernels, per_device(): call(norm_body, [(rows, bf16), ((8, 128), f32)], 'norm', 10 ** 9, ins=[pl...  1.18 us
  transfers between devices with their start and end apart: 7, of which 3 were waited for; matrix products, arithmetic and copies ran while one was open for 0% of the time, Pallas kernels for 7%

profile of v8, /device:TPU:1, one launch (start us, length us, event | category | flops | bytes accessed | tf_op | source)
XLA Modules:
  0.0 56.2 jit_solution(10665756675562828087)
XLA Ops:
  0.6 1.4 %collective-permute-start = (bf16[128,256]{1,0:T(8,128)(2,1)}, bf16[128,256]{1,0:T(8,128)(2,1)S(1)}, u32[]{:S(2)}, u32[]{:S(2)}) collective-permute-start(bf16[128,256]{1,0:T(8,128)(2,1)} %q_ref.3), channel_id=1, source_target_pairs={{0,64},{64,0},{1,65},{65,1},{2,66},{66,2},{3,67},{67,3},{4,68},{68... | collective-permute-start | bytes 196616 | tf_op jit(solution)/shard_map/ppermute | solution.py:47
  2.1 0.1 collective-permute-start.1
  2.2 1.2 %norm.1 = (bf16[128,256]{1,0:T(8,128)(2,1)S(1)}, f32[8,128]{1,0:T(8,128)S(1)}) custom-call(bf16[128,256]{1,0:T(8,128)(2,1)} %q_ref.3, bf16[128,256]{1,0:T(8,128)(2,1)} %v_ref.3), custom_call_target="tpu_custom_call" | custom-call | flops 1000000000 | tf_op jit(solution)/shard_map/norm/pallas_call | solution.py:372
  3.3 0.0 collective-permute-done.got_q_ref
  3.4 0.2 collective-permute-done.1.got_v_ref
  3.5 0.2 tile.1
  3.7 16.7 %all_to_all.15.block_ref = bf16[8,2,128,256]{3,2,1,0:T(8,128)(2,1)S(1)} all-to-all(bf16[8,2,128,256]{3,2,1,0:T(8,128)(2,1)S(1)} %tile.1), channel_id=1, replica_groups={{68,84,100,116,72,88,104,120},{76,92,108,124,64,80,96,112},{69,85,101,1..., dimensions={0} | all-to-all | bytes 2097152 | tf_op jit(solution)/shard_map/all_to_all | solution.py:43
  20.5 0.4 collective-permute-start.2
  20.9 0.3 collective-permute-start.3
  21.2 1.3 %collective-permute-done.2.got_ref = bf16[8,128,256]{2,1,0:T(8,128)(2,1)S(1)} collective-permute-done((bf16[8,128,256]{2,1,0:T(8,128)(2,1)S(1)}, bf16[8,128,256]{2,1,0:T(8,128)(2,1)S(1)}, u32[]{:S(2)}, u32[]{:S(2)}) %collective-permute-start.2) | collective-permute-done | bytes 524320 | tf_op jit(solution)/shard_map/ppermute | solution.py:47
  22.5 0.8 %score0.1 = (bf16[4,256,1024]{2,1,0:T(8,128)(2,1)S(1)}, bf16[8,128,256]{2,1,0:T(8,128)(2,1)S(1)}, bf16[4,2,128,256]{3,2,1,0:T(8,128)(2,1)S(1)}, f32[8,1024]{1,0:T(8,128)S(1)}) custom-call(bf16[8,2,128,256]{3,2,1,0:T(8,128)(2,1)S(1)} %all_to_all.15.block_ref, bf16[8,128,256]{2,1,0:T(8,128)(2,1)S(1)} %collective-permute-done.2.got_ref), custom_call_target="tpu_custom_call" | custom-call | flops 1073741824 | tf_op jit(solution)/shard_map/score0/pallas_call | solution.py:390
  23.3 0.0 collective-permute-done.3.got_ref
  23.3 0.8 %score1.1 = (bf16[4,256,1024]{2,1,0:T(8,128)(2,1)S(1)}, bf16[4,2,128,256]{3,2,1,0:T(8,128)(2,1)S(1)}, f32[8,16,128]{2,1,0:T(8,128)S(1)}) custom-call(bf16[8,2,128,256]{3,2,1,0:T(8,128)(2,1)S(1)} %all_to_all.15.block_ref, bf16[8,128,256]{2,1,0:T(8,128)(2,1)S(1)} %collective-permute-done.3.got_ref, bf16[8,128,256]{2,1,0:T(8,128)(2,1)S(1)} %get-tuple-element.19.q_ref, ...), custom_call_target="tpu_custom_call" | custom-call | flops 1073741824 | tf_op jit(solution)/shard_map/score1/pallas_call | solution.py:393
  24.2 9.3 %all_to_all.16.s_ref = f32[8,16,128]{2,1,0:T(8,128)S(1)} all-to-all(f32[8,16,128]{2,1,0:T(8,128)S(1)} %get-tuple-element.25), channel_id=1, replica_groups={{0,1,2,3,4,5,6,7},{8,9,10,11,12,13,14,15},{16,17,18,19,20,21,22,23},{24..., dimensions={0} | all-to-all | bytes 131072 | tf_op jit(solution)/shard_map/all_to_all | solution.py:43
  33.5 1.4 %first.1 = bf16[1032,256]{1,0:T(8,128)(2,1)S(1)} custom-call(bf16[4,256,1024]{2,1,0:T(8,128)(2,1)S(1)} %get-tuple-element.18.e0_ref, bf16[4,256,1024]{2,1,0:T(8,128)(2,1)S(1)} %get-tuple-element.22.e1_ref, bf16[4,2,128,256]{3,2,1,0:T(8,128)(2,1)S(1)} %get-tuple-element.23.v0_ref, bf16[4,2,128,256]{3,2,1,0:T(8,128)(2,1)S(1)} %get-tuple-element.24.v1_ref, ...), custom_call_target="tpu_custom_call" | custom-call | flops 1073741824 | tf_op jit(solution)/shard_map/first/pallas_call | solution.py:398
  34.9 1.1 %collective-permute-start.4 = (bf16[1032,256]{1,0:T(8,128)(2,1)S(1)}, bf16[1032,256]{1,0:T(8,128)(2,1)S(1)}, u32[]{:S(2)}, u32[]{:S(2)}) collective-permute-start(bf16[1032,256]{1,0:T(8,128)(2,1)S(1)} %first.1), channel_id=1, source_target_pairs={{0,64},{64,0},{1,65},{65,1},{2,66},{66,2},{3,67},{67,3},{4,68},{68... | collective-permute-start | bytes 1585160 | tf_op jit(solution)/shard_map/ppermute | solution.py:47
  36.0 0.8 %collective-permute-start.5 = (bf16[1024,256]{1,0:T(8,128)(2,1)S(1)}, bf16[1024,256]{1,0:T(8,128)(2,1)S(1)}, u32[]{:S(2)}, u32[]{:S(2)}) collective-permute-start(bf16[1024,256]{1,0:T(8,128)(2,1)S(1)} %second.1), channel_id=1, source_target_pairs={{0,64},{64,0},{1,65},{65,1},{2,66},{66,2},{3,67},{67,3},{4,68},{68... | collective-permute-start | bytes 1572872 | tf_op jit(solution)/shard_map/ppermute | solution.py:47
  36.8 1.2 %third.1 = (f32[8,256,256]{2,1,0:T(8,128)S(1)}, bf16[1024,256]{1,0:T(8,128)(2,1)S(1)}) custom-call(bf16[4,256,1024]{2,1,0:T(8,128)(2,1)S(1)} %get-tuple-element.18.e0_ref, bf16[4,256,1024]{2,1,0:T(8,128)(2,1)S(1)} %get-tuple-element.22.e1_ref, bf16[4,2,128,256]{3,2,1,0:T(8,128)(2,1)S(1)} %get-tuple-element.23.v0_ref, ...), custom_call_target="tpu_custom_call" | custom-call | flops 1073741824 | tf_op jit(solution)/shard_map/third/pallas_call | solution.py:402
  38.1 0.0 collective-permute-done.4.got_ref
  38.1 0.2 merge.1.part_ref
  38.3 0.0 collective-permute-done.5.got_ref
  38.4 0.1 join.1
  38.5 0.0 copy-start
  38.5 0.0 copy-start.1
  38.5 15.2 %all_to_all.17.w_ref = bf16[8,264,256]{2,1,0:T(8,128)(2,1)S(1)} all-to-all(bf16[8,264,256]{2,1,0:T(8,128)(2,1)S(1)} %join.1), channel_id=1, replica_groups={{68,84,100,116,72,88,104,120},{76,92,108,124,64,80,96,112},{69,85,101,1..., dimensions={0} | all-to-all | bytes 2162688 | tf_op jit(solution)/shard_map/all_to_all | solution.py:43
  53.8 0.1 give.1.give_ref
  53.8 0.1 collective-permute-start.6
  53.9 0.0 copy-done
  53.9 0.0 copy-done.1
  53.9 0.3 own.1.own_ref
  54.3 1.0 %collective-permute-done.6.got_ref = f32[136,256]{1,0:T(8,128)S(1)} collective-permute-done((f32[136,256]{1,0:T(8,128)S(1)}, f32[136,256]{1,0:T(8,128)S(1)}, u32[]{:S(2)}, u32[]{:S(2)}) %collective-permute-start.6) | collective-permute-done | bytes 139296 | tf_op jit(solution)/shard_map/ppermute | solution.py:47
  55.3 1.0 %final.1 = (f32[128,256]{1,0:T(8,128)}, f32[128,256]{1,0:T(8,128)}, f32[1,1]{1,0:T(1,128)}) custom-call(bf16[128,256]{1,0:T(8,128)(2,1)S(1)} %copy-done, bf16[128,256]{1,0:T(8,128)(2,1)S(1)} %copy-done.1, f32[128,256]{1,0:T(8,128)S(1)} %own.1.own_ref, f32[136,256]{1,0:T(8,128)S(1)} %give.1.give_ref, f32[136,256]{1,0:T(8,128)S(1)} %collective-permute-done.6.got_ref, ...), custom_call_target="tpu_custom_call" | custom-call | tf_op jit(solution)/shard_map/final/pallas_call | solution.py:412
  (3 shorter events, 0.1 us)
Async XLA Ops:
  0.6 2.7 %collective-permute-start = (bf16[128,256]{1,0:T(8,128)(2,1)}, bf16[128,256]{1,0:T(8,128)(2,1)S(1)}, u32[]{:S(2)}, u32[]{:S(2)}) collective-permute-start(bf16[128,256]{1,0:T(8,128)(2,1)} %q_ref.3), channel_id=1, source_target_pairs={{0,64},{64,0},{1,65},{65,1},{2,66},{66,2},{3,67},{67,3},{4,68},{68... | collective-permute-start | bytes 196616 | tf_op jit(solution)/shard_map/ppermute | solution.py:47
  2.1 1.5 %collective-permute-start.1 = (bf16[128,256]{1,0:T(8,128)(2,1)}, bf16[128,256]{1,0:T(8,128)(2,1)S(1)}, u32[]{:S(2)}, u32[]{:S(2)}) collective-permute-start(bf16[128,256]{1,0:T(8,128)(2,1)} %v_ref.3), channel_id=1, source_target_pairs={{0,64},{64,0},{1,65},{65,1},{2,66},{66,2},{3,67},{67,3},{4,68},{68... | collective-permute-start | bytes 196616 | tf_op jit(solution)/shard_map/ppermute | solution.py:47
  20.5 2.0 %collective-permute-start.2 = (bf16[8,128,256]{2,1,0:T(8,128)(2,1)S(1)}, bf16[8,128,256]{2,1,0:T(8,128)(2,1)S(1)}, u32[]{:S(2)}, u32[]{:S(2)}) collective-permute-start(bf16[8,128,256]{2,1,0:T(8,128)(2,1)S(1)} %half.1), channel_id=1, source_target_pairs={{0,64},{64,0},{1,65},{65,1},{2,66},{66,2},{3,67},{67,3},{4,68},{68... | collective-permute-start | bytes 1572872 | tf_op jit(solution)/shard_map/ppermute | solution.py:47
  20.9 2.4 %collective-permute-start.3 = (bf16[8,128,256]{2,1,0:T(8,128)(2,1)S(1)}, bf16[8,128,256]{2,1,0:T(8,128)(2,1)S(1)}, u32[]{:S(2)}, u32[]{:S(2)}) collective-permute-start(bf16[8,128,256]{2,1,0:T(8,128)(2,1)S(1)} %rest.1), channel_id=1, source_target_pairs={{0,64},{64,0},{1,65},{65,1},{2,66},{66,2},{3,67},{67,3},{4,68},{68... | collective-permute-start | bytes 1572872 | tf_op jit(solution)/shard_map/ppermute | solution.py:47
  34.9 3.2 %collective-permute-start.4 = (bf16[1032,256]{1,0:T(8,128)(2,1)S(1)}, bf16[1032,256]{1,0:T(8,128)(2,1)S(1)}, u32[]{:S(2)}, u32[]{:S(2)}) collective-permute-start(bf16[1032,256]{1,0:T(8,128)(2,1)S(1)} %first.1), channel_id=1, source_target_pairs={{0,64},{64,0},{1,65},{65,1},{2,66},{66,2},{3,67},{67,3},{4,68},{68... | collective-permute-start | bytes 1585160 | tf_op jit(solution)/shard_map/ppermute | solution.py:47
  36.0 2.4 %collective-permute-start.5 = (bf16[1024,256]{1,0:T(8,128)(2,1)S(1)}, bf16[1024,256]{1,0:T(8,128)(2,1)S(1)}, u32[]{:S(2)}, u32[]{:S(2)}) collective-permute-start(bf16[1024,256]{1,0:T(8,128)(2,1)S(1)} %second.1), channel_id=1, source_target_pairs={{0,64},{64,0},{1,65},{65,1},{2,66},{66,2},{3,67},{67,3},{4,68},{68... | collective-permute-start | bytes 1572872 | tf_op jit(solution)/shard_map/ppermute | solution.py:47
  38.5 15.4 %copy-start = (bf16[128,256]{1,0:T(8,128)(2,1)S(1)}, bf16[128,256]{1,0:T(8,128)(2,1)}, u32[]{:S(2)}) copy-start(bf16[128,256]{1,0:T(8,128)(2,1)} %q_ref.3) | copy-start | bytes 196612
  38.5 15.4 %copy-start.1 = (bf16[128,256]{1,0:T(8,128)(2,1)S(1)}, bf16[128,256]{1,0:T(8,128)(2,1)}, u32[]{:S(2)}) copy-start(bf16[128,256]{1,0:T(8,128)(2,1)} %v_ref.3) | copy-start | bytes 196612
  53.8 1.4 %collective-permute-start.6 = (f32[136,256]{1,0:T(8,128)S(1)}, f32[136,256]{1,0:T(8,128)S(1)}, u32[]{:S(2)}, u32[]{:S(2)}) collective-permute-start(f32[136,256]{1,0:T(8,128)S(1)} %give.1.give_ref), channel_id=1, source_target_pairs={{0,64},{64,0},{1,65},{65,1},{2,66},{66,2},{3,67},{67,3},{4,68},{68... | collective-permute-start | bytes 417800 | tf_op jit(solution)/shard_map/ppermute | solution.py:47

commit v9 on v8

--- a/solution.py
+++ b/solution.py
@@ -128,49 +128,62 @@
     out_ref[...] = block_ref[4:].reshape(GROUP, ROWS, D)
 
 
-def scores(v_ref, q_ref, e_ref):
-    q = q_ref[...].reshape(GROUP * ROWS, D)
+def by_role(item, query):
+    core = lax.axis_index("blk")
+    pl.when(core == ITEM)(item)
+    pl.when(core != ITEM)(query)
+
+
+def rows_of(ref):
+    return ref[...].reshape(-1, D)
+
+
+def own_queries(block_ref):
+    return block_ref[:, 1 - ITEM].reshape(GROUP * ROWS, D)
+
+
+def item_parts(block_ref):
+    return [lambda k=k: block_ref[k].reshape(2 * ROWS, D) for k in range(GROUP)]
+
+
+def got_parts(*refs):
+    return [lambda ref=ref, k=k: ref[2 * k : 2 * k + 2].reshape(2 * ROWS, D) for ref in refs for k in range(4)]
+
+
+def scores(parts, q, e_ref):
     total = jnp.zeros((1, GROUP * ROWS), f32)
-    for k in range(4):
-        v = v_ref[k].reshape(2 * ROWS, D)
-        t = lax.dot_general(v, q, (((1,), (1,)), ((), ())), preferred_element_type=f32)
+    for k, part in enumerate(parts):
+        t = lax.dot_general(part(), q, (((1,), (1,)), ((), ())), preferred_element_type=f32)
         e = jnp.exp2(t * (log2_e / sharpness))
         total = total + jnp.sum(e, axis=0, keepdims=True)
         e_ref[k] = e.astype(bf16)
     return total
 
 
-def score0_body(block_ref, got_ref, e_ref, q_ref, v_ref, t_ref):
-    core = lax.axis_index("blk")
-
-    @pl.when(core == ITEM)
-    def _():
-        v_ref[...] = block_ref[:4]
-        q_ref[...] = got_ref[...]
-
-    @pl.when(core != ITEM)
-    def _():
-        v_ref[...] = got_ref[...].reshape(4, 2, ROWS, D)
-        q_ref[...] = block_ref[:, 1 - ITEM]
-
-    t_ref[...] = jnp.broadcast_to(scores(v_ref, q_ref, e_ref), t_ref.shape)
-
-
-def score1_body(block_ref, got_ref, q_ref, t_ref, pos_ref, e_ref, v_ref, s_ref):
-    core = lax.axis_index("blk")
-
-    @pl.when(core == ITEM)
-    def _():
-        v_ref[...] = block_ref[4:]
-
-    @pl.when(core != ITEM)
-    def _():
-        v_ref[...] = got_ref[...].reshape(4, 2, ROWS, D)
-
-    total = t_ref[:1] + scores(v_ref, q_ref, e_ref)
-    for k in range(GROUP):
+def score0_body(block_ref, got_ref, e_ref, t_ref):
+    def item():
+        t_ref[:1] = scores(item_parts(block_ref)[:4], rows_of(got_ref), e_ref)
+
+    def query():
+        t_ref[:1] = scores(got_parts(got_ref), own_queries(block_ref), e_ref)
+
+    by_role(item, query)
+
+
+def score1_body(block_ref, got_a_ref, got_b_ref, t_ref, pos_ref, e_ref, s_ref):
+    def send(total):
+        total = total + t_ref[:1]
+        total = jnp.concatenate([total[:, k * ROWS : (k + 1) * ROWS] for k in range(GROUP)], axis=0)
         for j in range(GROUP):
-            s_ref[j, k : k + 1] = total[:, k * ROWS : (k + 1) * ROWS]
+            s_ref[j, :8] = total
+
+    def item():
+        send(scores(item_parts(block_ref)[4:], rows_of(got_a_ref), e_ref))
+
+    def query():
+        send(scores(got_parts(got_b_ref), own_queries(block_ref), e_ref))
+
+    by_role(item, query)
     for j in range(GROUP):
         s_ref[j, 8:16] = pos_ref[...]
 
@@ -182,8 +195,8 @@
     return total
 
 
-def loss_part(sums):
-    return jnp.sum(jnp.log(sums[:8])) - jnp.max(sums[8:9])
+def loss_part(sums, pos):
+    return jnp.sum(jnp.log(sums)) - jnp.max(pos[:1])
 
 
 def split(value):
@@ -196,9 +209,8 @@
     return tail[:, :128] + tail[:, 128:]
 
 
-def weigh(e_ref, q_ref, r, store):
-    q = q_ref[...].reshape(GROUP * ROWS, D)
-    for k in range(4):
+def weigh(e_ref, q, r, store, ks=range(4)):
+    for k in ks:
         parts = [
             (e_ref[k, :, j * ROWS : (j + 1) * ROWS].astype(f32) * r[j : j + 1]).astype(bf16)
             for j in range(GROUP)
@@ -206,14 +218,14 @@
         store(k, jnp.dot(jnp.concatenate(parts, axis=1), q, preferred_element_type=f32))
 
 
-def pull(v_refs, e_refs, u_ref):
+def pull(parts, e_refs, u_ref):
     total = None
-    for v_ref, e_ref in zip(v_refs, e_refs):
-        for k in (0, 2):
-            v = v_ref[k : k + 2].reshape(4 * ROWS, D)
-            e = e_ref[k : k + 2].reshape(4 * ROWS, GROUP * ROWS)
-            part = lax.dot_general(v, e, (((0,), (0,)), ((), ())), preferred_element_type=f32)
-            total = part if total is None else total + part
+    for i in range(0, GROUP, 2):
+        v = jnp.concatenate([parts[i](), parts[i + 1]()], axis=0)
+        k = i % 4
+        e = e_refs[i // 4][k : k + 2].reshape(4 * ROWS, GROUP * ROWS)
+        part = lax.dot_general(v, e, (((0,), (0,)), ((), ())), preferred_element_type=f32)
+        total = part if total is None else total + part
     for k in range(GROUP):
         rows = slice(k * ROWS, (k + 1) * ROWS)
         u_ref[rows, :ROWS] = total[:ROWS, rows].astype(bf16)
@@ -227,79 +239,87 @@
     return store
 
 
-def first_body(e0_ref, e1_ref, v0_ref, v1_ref, q_ref, s_ref, give_ref):
-    core = lax.axis_index("blk")
+def keeping(ref):
+    def store(k, w):
+        ref[k] = w
+
+    return store
+
+
+def first_body(e0_ref, e1_ref, block_ref, s_ref, give_ref):
     sums = row_sums(s_ref)
-    give_ref[1024:1032] = split(jnp.full((8, 128), loss_part(sums), f32))
-
-    @pl.when(core == ITEM)
-    def _():
-        pull((v0_ref, v1_ref), (e0_ref, e1_ref), give_ref)
-
-    @pl.when(core != ITEM)
-    def _():
-        weigh(e0_ref, q_ref, 1.0 / sums[:8], into(give_ref))
-
-
-def second_body(e1_ref, q_ref, s_ref, give_ref):
-    @pl.when(lax.axis_index("blk") != ITEM)
-    def _():
-        weigh(e1_ref, q_ref, 1.0 / row_sums(s_ref)[:8], into(give_ref))
-
-
-def third_body(e0_ref, e1_ref, v0_ref, v1_ref, q_ref, s_ref, keep_ref, u_ref):
-    core = lax.axis_index("blk")
-
-    @pl.when(core == ITEM)
-    def _():
-        r = 1.0 / row_sums(s_ref)[:8]
-        for first, e_ref in ((0, e0_ref), (4, e1_ref)):
-
-            def store(k, w):
-                keep_ref[first + k] = w
-
-            weigh(e_ref, q_ref, r, store)
-
-    @pl.when(core != ITEM)
-    def _():
-        pull((v0_ref, v1_ref), (e0_ref, e1_ref), u_ref)
-
-
-def merge_body(keep_ref, u_ref, got_ref, s_ref, out_ref):
-    core = lax.axis_index("blk")
-
-    @pl.when(core == ITEM)
-    def _():
+    give_ref[1024:1032] = split(sums[:8])
+    give_ref[1032:1040] = split(sums[8:])
+
+    def item():
+        pull(item_parts(block_ref), (e0_ref, e1_ref), give_ref)
+
+    def query():
+        weigh(e0_ref, own_queries(block_ref), 1.0 / sums[:8], into(give_ref))
+
+    by_role(item, query)
+
+
+def second_body(e0_ref, e1_ref, block_ref, got_a_ref, s_ref, keep_ref, give_ref):
+    r = 1.0 / row_sums(s_ref)[:8]
+
+    def item():
+        weigh(e0_ref, rows_of(got_a_ref), r, keeping(keep_ref), range(2))
+
+    def query():
+        weigh(e1_ref, own_queries(block_ref), r, into(give_ref))
+
+    by_role(item, query)
+
+
+def third_body(e0_ref, e1_ref, got_a_ref, got_b_ref, s_ref, keep0_ref, keep1_ref, u_ref):
+    def item():
+        r, q = 1.0 / row_sums(s_ref)[:8], rows_of(got_a_ref)
+        weigh(e0_ref, q, r, lambda k, w: keeping(keep0_ref)(k - 2, w), range(2, 4))
+        weigh(e1_ref, q, r, keeping(keep1_ref))
+
+    def query():
+        pull(got_parts(got_a_ref, got_b_ref), (e0_ref, e1_ref), u_ref)
+
+    by_role(item, query)
+
+
+def merge_body(keep0_ref, keep1_ref, u_ref, got_ref, s_ref, out_ref):
+    def item():
         for k in range(4):
+            keep = keep0_ref[k] if k < 2 else keep1_ref[k - 2]
             got = got_ref[k * 256 : (k + 1) * 256].astype(f32)
-            out_ref[k, :256] = (keep_ref[k] + got).astype(bf16)
-
-    @pl.when(core != ITEM)
-    def _():
+            out_ref[k, :256] = (keep + got).astype(bf16)
+        sums = row_sums(s_ref)
+        loss = loss_part(sums[:8], sums[8:])
+        loss = loss + loss_part(joined(got_ref[1024:1032]), joined(got_ref[1032:1040]))
+        tail = split(jnp.full((8, 128), loss, f32))
+        for k in range(GROUP):
+            out_ref[k, 256:264] = tail
+
+    def query():
         for k in range(GROUP):
             rows = slice(k * ROWS, (k + 1) * ROWS)
             out_ref[k, (1 - ITEM) * 128 : (2 - ITEM) * 128] = u_ref[rows]
             out_ref[k, ITEM * 128 : (ITEM + 1) * 128] = got_ref[rows]
-
-    tail = split(joined(got_ref[1024:1032]) + loss_part(row_sums(s_ref)))
-    for k in range(GROUP):
-        out_ref[k, 256:264] = tail
+            out_ref[k, 256:264] = jnp.zeros((8, D), bf16)
+
+    by_role(item, query)
 
 
 def join_body(part_ref, keep_ref, got_ref, out_ref):
-    core = lax.axis_index("blk")
     out_ref[:4] = part_ref[:4]
     out_ref[4:, 256:264] = part_ref[4:, 256:264]
 
-    @pl.when(core == ITEM)
-    def _():
+    def item():
         for k in range(4):
             got = got_ref[k * 256 : (k + 1) * 256].astype(f32)
-            out_ref[4 + k, :256] = (keep_ref[4 + k] + got).astype(bf16)
-
-    @pl.when(core != ITEM)
-    def _():
+            out_ref[4 + k, :256] = (keep_ref[k] + got).astype(bf16)
+
+    def query():
         out_ref[4:, :256] = part_ref[4:, :256]
+
+    by_role(item, query)
 
 
 def summed(w_ref, first, rows):
@@ -386,25 +406,24 @@
     (b,) = call(rest_body, [(cut, bf16)], "rest")(block)
     got_b = swap_cores(b)
     scored = ((4, 256, 1024), bf16)
-    v_half = ((4, 2, ROWS, D), bf16)
-    e0, q, v0, t = call(
-        score0_body, [scored, (cut, bf16), v_half, ((8, GROUP * ROWS), f32)], "score0", flops
-    )(block, got_a)
-    e1, v1, s = call(
-        score1_body, [scored, v_half, ((GROUP, 16, 128), f32)], "score1", flops
-    )(block, got_b, q, t, pos)
+    e0, t = call(score0_body, [scored, ((8, GROUP * ROWS), f32)], "score0", flops)(block, got_a)
+    e1, s = call(
+        score1_body, [scored, ((GROUP, 16, 128), f32)], "score1", flops
+    )(block, got_a, got_b, t, pos)
     sums = exchange(s, QUERY)
     pulled = (GROUP * ROWS, D)
-    (give,) = call(first_body, [((1032, D), bf16)], "first", flops)(e0, e1, v0, v1, q, sums)
+    (give,) = call(first_body, [((1040, D), bf16)], "first", flops)(e0, e1, block, sums)
     got0 = swap_cores(give)
-    (give,) = call(second_body, [(pulled, bf16)], "second", flops)(e1, q, sums)
+    keep0, give = call(
+        second_body, [((2, 256, D), f32), (pulled, bf16)], "second", flops
+    )(e0, e1, block, got_a, sums)
     got1 = swap_cores(give)
-    keep, u = call(
-        third_body, [((GROUP, 256, D), f32), (pulled, bf16)], "third", flops
-    )(e0, e1, v0, v1, q, sums)
+    keep1, keep2, u = call(
+        third_body, [((2, 256, D), f32), ((4, 256, D), f32), (pulled, bf16)], "third", flops
+    )(e0, e1, got_a, got_b, sums)
     packed = (GROUP, 264, D)
-    (part,) = call(merge_body, [(packed, bf16)], "merge", flops)(keep, u, got0, sums)
-    (out,) = call(join_body, [(packed, bf16)], "join")(part, keep, got1)
+    (part,) = call(merge_body, [(packed, bf16)], "merge", flops)(keep0, keep1, u, got0, sums)
+    (out,) = call(join_body, [(packed, bf16)], "join")(part, keep2, got1)
     out = exchange(out, BULK)
     (give,) = call(give_body, [((136, D), f32)], "give")(out)
     got = swap_cores(give)

time: 56.5 us -> 56.2 us (level)
  local copies, waits for them, and re-layouts: 0.01 us -> 0.7 us
    unnamed x4, local copies, waits for them, and re-layouts: 0.01 us -> 0.7 us
  transfers between devices with their start and end apart: 7 -> 7, of which waited for: 3 -> 4; matrix products, arithmetic and copies ran while one was open for 0% -> 0% of each run, Pallas kernels for 7% -> 7%
where the time goes in v9:
time: 56.2 us; the launch traced here: 56 us
  blocking collectives  41.1 us (73%)
  Pallas kernels  7.44 us (13%)
  starting transfers between devices  3.75 us (7%)
  waiting for transfers between devices  2.19 us (4%)
  between operations  0.76 us (1%)
  local copies, waits for them, and re-layouts  0.7 us (1%)
    all_to_all x3, blocking collectives, exchange(): lax.all_to_all(pieces, AXES, 0, 0, tiled=True, axis_index_groups=groups)  41.1 us
    ppermute x7, starting transfers between devices, swap_cores(): return lax.ppermute(value, 'blk', [(0, 1), (1, 0)])  3.75 us
    ppermute x7, waiting for transfers between devices, swap_cores(): return lax.ppermute(value, 'blk', [(0, 1), (1, 0)])  2.19 us
    pallas_call x1, Pallas kernels, per_device(): call(first_body, [((1040, D), bf16)], 'first', flops)(e0, e1, block, sums)  1.28 us
    pallas_call x1, Pallas kernels, per_device(): call(norm_body, [(rows, bf16), ((8, 128), f32)], 'norm', 10 ** 9, ins=[pl...  1.18 us
  transfers between devices with their start and end apart: 7, of which 4 were waited for; matrix products, arithmetic and copies ran while one was open for 0% of the time, Pallas kernels for 7%

profile of v9, /device:TPU:1, one launch (start us, length us, event | category | flops | bytes accessed | tf_op | source)
XLA Modules:
  0.0 56.0 jit_solution(10569879187195648005)
XLA Ops:
  0.6 1.4 %collective-permute-start = (bf16[128,256]{1,0:T(8,128)(2,1)}, bf16[128,256]{1,0:T(8,128)(2,1)S(1)}, u32[]{:S(2)}, u32[]{:S(2)}) collective-permute-start(bf16[128,256]{1,0:T(8,128)(2,1)} %q_ref.3), channel_id=1, source_target_pairs={{0,64},{64,0},{1,65},{65,1},{2,66},{66,2},{3,67},{67,3},{4,68},{68... | collective-permute-start | bytes 196616 | tf_op jit(solution)/shard_map/ppermute | solution.py:47
  2.1 0.1 collective-permute-start.1
  2.2 1.2 %norm.1 = (bf16[128,256]{1,0:T(8,128)(2,1)S(1)}, f32[8,128]{1,0:T(8,128)S(1)}) custom-call(bf16[128,256]{1,0:T(8,128)(2,1)} %q_ref.3, bf16[128,256]{1,0:T(8,128)(2,1)} %v_ref.3), custom_call_target="tpu_custom_call" | custom-call | flops 1000000000 | tf_op jit(solution)/shard_map/norm/pallas_call | solution.py:392
  3.3 0.0 collective-permute-done.got_q_ref
  3.4 0.2 collective-permute-done.1.got_v_ref
  3.5 0.2 tile.1
  3.7 16.7 %all_to_all.15.block_ref = bf16[8,2,128,256]{3,2,1,0:T(8,128)(2,1)S(1)} all-to-all(bf16[8,2,128,256]{3,2,1,0:T(8,128)(2,1)S(1)} %tile.1), channel_id=1, replica_groups={{68,84,100,116,72,88,104,120},{76,92,108,124,64,80,96,112},{69,85,101,1..., dimensions={0} | all-to-all | bytes 2097152 | tf_op jit(solution)/shard_map/all_to_all | solution.py:43
  20.5 0.4 collective-permute-start.2
  20.9 0.3 collective-permute-start.3
  21.2 1.3 %collective-permute-done.2.got_ref.got_a_ref = bf16[8,128,256]{2,1,0:T(8,128)(2,1)S(1)} collective-permute-done((bf16[8,128,256]{2,1,0:T(8,128)(2,1)S(1)}, bf16[8,128,256]{2,1,0:T(8,128)(2,1)S(1)}, u32[]{:S(2)}, u32[]{:S(2)}) %collective-permute-start.2) | collective-permute-done | bytes 524320 | tf_op jit(solution)/shard_map/ppermute | solution.py:47
  22.5 0.8 %score0.1 = (bf16[4,256,1024]{2,1,0:T(8,128)(2,1)S(1)}, f32[8,1024]{1,0:T(8,128)S(1)}) custom-call(bf16[8,2,128,256]{3,2,1,0:T(8,128)(2,1)S(1)} %all_to_all.15.block_ref, bf16[8,128,256]{2,1,0:T(8,128)(2,1)S(1)} %collective-permute-done.2.got_ref.got_a_ref), custom_call_target="tpu_custom_call" | custom-call | flops 1073741824 | tf_op jit(solution)/shard_map/score0/pallas_call | solution.py:409
  23.3 0.0 collective-permute-done.3.got_b_ref
  23.3 0.8 %score1.1 = (bf16[4,256,1024]{2,1,0:T(8,128)(2,1)S(1)}, f32[8,16,128]{2,1,0:T(8,128)S(1)}) custom-call(bf16[8,2,128,256]{3,2,1,0:T(8,128)(2,1)S(1)} %all_to_all.15.block_ref, bf16[8,128,256]{2,1,0:T(8,128)(2,1)S(1)} %collective-permute-done.2.got_ref.got_a_ref, bf16[8,128,256]{2,1,0:T(8,128)(2,1)S(1)} %collective-permute-done.3.got_b_ref, ...), custom_call_target="tpu_custom_call" | custom-call | flops 1073741824 | tf_op jit(solution)/shard_map/score1/pallas_call | solution.py:410
  24.1 9.3 %all_to_all.16.s_ref = f32[8,16,128]{2,1,0:T(8,128)S(1)} all-to-all(f32[8,16,128]{2,1,0:T(8,128)S(1)} %get-tuple-element.22), channel_id=1, replica_groups={{0,1,2,3,4,5,6,7},{8,9,10,11,12,13,14,15},{16,17,18,19,20,21,22,23},{24..., dimensions={0} | all-to-all | bytes 131072 | tf_op jit(solution)/shard_map/all_to_all | solution.py:43
  33.4 1.3 %first.1 = bf16[1040,256]{1,0:T(8,128)(2,1)S(1)} custom-call(bf16[4,256,1024]{2,1,0:T(8,128)(2,1)S(1)} %get-tuple-element.18.e0_ref, bf16[4,256,1024]{2,1,0:T(8,128)(2,1)S(1)} %get-tuple-element.21.e1_ref, bf16[8,2,128,256]{3,2,1,0:T(8,128)(2,1)S(1)} %all_to_all.15.block_ref, f32[8,16,128]{2,1,0:T(8,128)S(1)} %all_to_all.16.s_ref), custom_call_target="tpu_custom_call" | custom-call | flops 1073741824 | tf_op jit(solution)/shard_map/first/pallas_call | solution.py:415
  34.7 1.1 %collective-permute-start.4 = (bf16[1040,256]{1,0:T(8,128)(2,1)S(1)}, bf16[1040,256]{1,0:T(8,128)(2,1)S(1)}, u32[]{:S(2)}, u32[]{:S(2)}) collective-permute-start(bf16[1040,256]{1,0:T(8,128)(2,1)S(1)} %first.1), channel_id=1, source_target_pairs={{0,64},{64,0},{1,65},{65,1},{2,66},{66,2},{3,67},{67,3},{4,68},{68... | collective-permute-start | bytes 1597448 | tf_op jit(solution)/shard_map/ppermute | solution.py:47
  35.8 0.5 second.1
  36.2 0.4 collective-permute-start.5
  36.6 1.0 %third.1 = (f32[2,256,256]{2,1,0:T(8,128)S(1)}, f32[4,256,256]{2,1,0:T(8,128)S(1)}, bf16[1024,256]{1,0:T(8,128)(2,1)S(1)}) custom-call(bf16[4,256,1024]{2,1,0:T(8,128)(2,1)S(1)} %get-tuple-element.18.e0_ref, bf16[4,256,1024]{2,1,0:T(8,128)(2,1)S(1)} %get-tuple-element.21.e1_ref, bf16[8,128,256]{2,1,0:T(8,128)(2,1)S(1)} %collective-permute-done.2.got_ref.got_a_ref, ...), custom_call_target="tpu_custom_call" | custom-call | flops 1073741824 | tf_op jit(solution)/shard_map/third/pallas_call | solution.py:421
  37.6 0.0 collective-permute-done.4.got_ref
  37.6 0.2 merge.1.part_ref
  37.8 0.4 collective-permute-done.5.got_ref
  38.2 0.1 join.1
  38.4 15.1 %all_to_all.17.w_ref = bf16[8,264,256]{2,1,0:T(8,128)(2,1)S(1)} all-to-all(bf16[8,264,256]{2,1,0:T(8,128)(2,1)S(1)} %join.1), channel_id=1, replica_groups={{68,84,100,116,72,88,104,120},{76,92,108,124,64,80,96,112},{69,85,101,1..., dimensions={0} | all-to-all | bytes 2162688 | tf_op jit(solution)/shard_map/all_to_all | solution.py:43
  53.5 0.0 copy-start
  53.5 0.0 copy-start.1
  53.5 0.1 give.1.give_ref
  53.5 0.1 collective-permute-start.6
  53.6 0.7 %copy-done = bf16[128,256]{1,0:T(8,128)(2,1)S(1)} copy-done((bf16[128,256]{1,0:T(8,128)(2,1)S(1)}, bf16[128,256]{1,0:T(8,128)(2,1)}, u32[]{:S(2)}) %copy-start) | copy-done | bytes 65560
  54.3 0.0 copy-done.1
  54.3 0.3 own.1.own_ref
  54.7 0.3 collective-permute-done.6.got_ref
  55.0 1.0 %final.1 = (f32[128,256]{1,0:T(8,128)}, f32[128,256]{1,0:T(8,128)}, f32[1,1]{1,0:T(1,128)}) custom-call(bf16[128,256]{1,0:T(8,128)(2,1)S(1)} %copy-done, bf16[128,256]{1,0:T(8,128)(2,1)S(1)} %copy-done.1, f32[128,256]{1,0:T(8,128)S(1)} %own.1.own_ref, f32[136,256]{1,0:T(8,128)S(1)} %give.1.give_ref, f32[136,256]{1,0:T(8,128)S(1)} %collective-permute-done.6.got_ref, ...), custom_call_target="tpu_custom_call" | custom-call | tf_op jit(solution)/shard_map/final/pallas_call | solution.py:431
  (2 shorter events, 0.1 us)
Async XLA Ops:
  0.6 2.7 %collective-permute-start = (bf16[128,256]{1,0:T(8,128)(2,1)}, bf16[128,256]{1,0:T(8,128)(2,1)S(1)}, u32[]{:S(2)}, u32[]{:S(2)}) collective-permute-start(bf16[128,256]{1,0:T(8,128)(2,1)} %q_ref.3), channel_id=1, source_target_pairs={{0,64},{64,0},{1,65},{65,1},{2,66},{66,2},{3,67},{67,3},{4,68},{68... | collective-permute-start | bytes 196616 | tf_op jit(solution)/shard_map/ppermute | solution.py:47
  2.1 1.5 %collective-permute-start.1 = (bf16[128,256]{1,0:T(8,128)(2,1)}, bf16[128,256]{1,0:T(8,128)(2,1)S(1)}, u32[]{:S(2)}, u32[]{:S(2)}) collective-permute-start(bf16[128,256]{1,0:T(8,128)(2,1)} %v_ref.3), channel_id=1, source_target_pairs={{0,64},{64,0},{1,65},{65,1},{2,66},{66,2},{3,67},{67,3},{4,68},{68... | collective-permute-start | bytes 196616 | tf_op jit(solution)/shard_map/ppermute | solution.py:47
  20.5 2.0 %collective-permute-start.2 = (bf16[8,128,256]{2,1,0:T(8,128)(2,1)S(1)}, bf16[8,128,256]{2,1,0:T(8,128)(2,1)S(1)}, u32[]{:S(2)}, u32[]{:S(2)}) collective-permute-start(bf16[8,128,256]{2,1,0:T(8,128)(2,1)S(1)} %half.1), channel_id=1, source_target_pairs={{0,64},{64,0},{1,65},{65,1},{2,66},{66,2},{3,67},{67,3},{4,68},{68... | collective-permute-start | bytes 1572872 | tf_op jit(solution)/shard_map/ppermute | solution.py:47
  20.9 2.4 %collective-permute-start.3 = (bf16[8,128,256]{2,1,0:T(8,128)(2,1)S(1)}, bf16[8,128,256]{2,1,0:T(8,128)(2,1)S(1)}, u32[]{:S(2)}, u32[]{:S(2)}) collective-permute-start(bf16[8,128,256]{2,1,0:T(8,128)(2,1)S(1)} %rest.1), channel_id=1, source_target_pairs={{0,64},{64,0},{1,65},{65,1},{2,66},{66,2},{3,67},{67,3},{4,68},{68... | collective-permute-start | bytes 1572872 | tf_op jit(solution)/shard_map/ppermute | solution.py:47
  34.7 2.9 %collective-permute-start.4 = (bf16[1040,256]{1,0:T(8,128)(2,1)S(1)}, bf16[1040,256]{1,0:T(8,128)(2,1)S(1)}, u32[]{:S(2)}, u32[]{:S(2)}) collective-permute-start(bf16[1040,256]{1,0:T(8,128)(2,1)S(1)} %first.1), channel_id=1, source_target_pairs={{0,64},{64,0},{1,65},{65,1},{2,66},{66,2},{3,67},{67,3},{4,68},{68... | collective-permute-start | bytes 1597448 | tf_op jit(solution)/shard_map/ppermute | solution.py:47
  36.2 2.0 %collective-permute-start.5 = (bf16[1024,256]{1,0:T(8,128)(2,1)S(1)}, bf16[1024,256]{1,0:T(8,128)(2,1)S(1)}, u32[]{:S(2)}, u32[]{:S(2)}) collective-permute-start(bf16[1024,256]{1,0:T(8,128)(2,1)S(1)} %get-tuple-element.27), channel_id=1, source_target_pairs={{0,64},{64,0},{1,65},{65,1},{2,66},{66,2},{3,67},{67,3},{4,68},{68... | collective-permute-start | bytes 1572872 | tf_op jit(solution)/shard_map/ppermute | solution.py:47
  53.5 0.8 %copy-start = (bf16[128,256]{1,0:T(8,128)(2,1)S(1)}, bf16[128,256]{1,0:T(8,128)(2,1)}, u32[]{:S(2)}) copy-start(bf16[128,256]{1,0:T(8,128)(2,1)} %q_ref.3) | copy-start | bytes 196612
  53.5 0.9 %copy-start.1 = (bf16[128,256]{1,0:T(8,128)(2,1)S(1)}, bf16[128,256]{1,0:T(8,128)(2,1)}, u32[]{:S(2)}) copy-start(bf16[128,256]{1,0:T(8,128)(2,1)} %v_ref.3) | copy-start | bytes 196612
  53.5 1.4 %collective-permute-start.6 = (f32[136,256]{1,0:T(8,128)S(1)}, f32[136,256]{1,0:T(8,128)S(1)}, u32[]{:S(2)}, u32[]{:S(2)}) collective-permute-start(f32[136,256]{1,0:T(8,128)S(1)} %give.1.give_ref), channel_id=1, source_target_pairs={{0,64},{64,0},{1,65},{65,1},{2,66},{66,2},{3,67},{67,3},{4,68},{68... | collective-permute-start | bytes 417800 | tf_op jit(solution)/shard_map/ppermute | solution.py:47

commit v10 on v9

--- a/solution.py
+++ b/solution.py
@@ -369,33 +369,37 @@
         own_ref[...] = query_slope(own, q_ref, v_ref, s_ref)
 
 
-def final_body(q_ref, v_ref, own_ref, give_ref, got_ref, s_ref, qs_ref, vs_ref, loss_ref):
-    core = lax.axis_index("blk")
-
-    @pl.when(core == ITEM)
-    def _():
-        vs_ref[...] = own_ref[...]
-        qs_ref[...] = query_slope(got_ref[:128], q_ref, v_ref, s_ref)
-        loss_ref[0, 0] = jnp.max(give_ref[128:136]) / (128 * 128)
-
-    @pl.when(core != ITEM)
-    def _():
-        qs_ref[...] = own_ref[...]
-        vs_ref[...] = item_slope(got_ref[:128], q_ref, v_ref)
-        loss_ref[0, 0] = jnp.max(got_ref[128:136]) / (128 * 128)
+def final_body(q_ref, v_ref, own_ref, give_ref, got_ref, s_ref, qs_hbm, vs_hbm, loss_ref, new_ref, sem):
+    def finish(own_hbm, other_hbm, other, total):
+        first = pltpu.make_async_copy(own_ref, own_hbm, sem.at[0])
+        first.start()
+        new_ref[...] = other()
+        second = pltpu.make_async_copy(new_ref, other_hbm, sem.at[1])
+        second.start()
+        loss_ref[0, 0] = jnp.max(total[128:136]) / (128 * 128)
+        first.wait()
+        second.wait()
+
+    def item():
+        finish(vs_hbm, qs_hbm, lambda: query_slope(got_ref[:128], q_ref, v_ref, s_ref), give_ref)
+
+    def query():
+        finish(qs_hbm, vs_hbm, lambda: item_slope(got_ref[:128], q_ref, v_ref), got_ref)
+
+    by_role(item, query)
 
 
 def per_device(queries, items):
     rows = (ROWS, D)
     bulk = (GROUP, 2, ROWS, D)
     in_hbm = [pltpu.with_memory_space_constraint(a, pltpu.HBM) for a in (queries, items)]
-    mine, pos = call(
+    mine, pos, q_raw, v_raw = call(
         norm_body,
-        [(rows, bf16), ((8, 128), f32)],
+        [(rows, bf16), ((8, 128), f32), (rows, bf16), (rows, bf16)],
         "norm",
         10**9,
         ins=[pl.BlockSpec(memory_space=pltpu.HBM)] * 2,
-        scratch=[pltpu.VMEM(rows, bf16), pltpu.VMEM(rows, bf16), pltpu.SemaphoreType.DMA((2,))],
+        scratch=[pltpu.SemaphoreType.DMA((2,))],
     )(*in_hbm)
     (tile,) = call(tile_body, [(bulk, bf16)], "tile")(mine, swap_cores(queries), swap_cores(items))
     block = exchange(tile, BULK)
@@ -427,10 +431,13 @@
     out = exchange(out, BULK)
     (give,) = call(give_body, [((136, D), f32)], "give")(out)
     got = swap_cores(give)
-    (own,) = call(own_body, [(rows, f32)], "own", flops)(out, queries, items, sums)
+    (own,) = call(own_body, [(rows, f32)], "own", flops)(out, q_raw, v_raw, sums)
     q_slope, v_slope, loss = call(
-        final_body, [(rows, f32), (rows, f32), ((1, 1), f32, pltpu.SMEM)], "final"
-    )(queries, items, own, give, got, sums)
+        final_body,
+        [(rows, f32, pltpu.HBM), (rows, f32, pltpu.HBM), ((1, 1), f32, pltpu.SMEM)],
+        "final",
+        scratch=[pltpu.VMEM(rows, f32), pltpu.SemaphoreType.DMA((2,))],
+    )(q_raw, v_raw, own, give, got, sums)
     return loss.reshape(()), q_slope, v_slope
 
 

time: 56.2 us -> 56.7 us (level)
  local copies, waits for them, and re-layouts: 0.7 us -> 0 us
  waiting for transfers between devices: 2.19 us -> 2.88 us
    unnamed x4 -> x0, local copies, waits for them, and re-layouts: 0.7 us -> none
    ppermute x7, waiting for transfers between devices: 2.19 us -> 2.88 us  [swap_cores(): return lax.ppermute(value, 'blk', [(0, 1), (1, 0)])]
where the time goes in v10:
time: 56.7 us; the launch traced here: 56.4 us
  blocking collectives  41.1 us (72%)
  Pallas kernels  7.93 us (14%)
  starting transfers between devices  3.74 us (7%)
  waiting for transfers between devices  2.88 us (5%)
  between operations  0.76 us (1%)
    all_to_all x3, blocking collectives, exchange(): lax.all_to_all(pieces, AXES, 0, 0, tiled=True, axis_index_groups=groups)  41.1 us
    ppermute x7, starting transfers between devices, swap_cores(): return lax.ppermute(value, 'blk', [(0, 1), (1, 0)])  3.74 us
    ppermute x7, waiting for transfers between devices, swap_cores(): return lax.ppermute(value, 'blk', [(0, 1), (1, 0)])  2.88 us
    pallas_call x1, Pallas kernels, per_device(): call(final_body, [(rows, f32, pltpu.HBM), (rows, f32, pltpu.HBM), ((1, 1)...  1.45 us
    pallas_call x1, Pallas kernels, per_device(): call(first_body, [((1040, D), bf16)], 'first', flops)(e0, e1, block, sums)  1.28 us
    pallas_call x1, Pallas kernels, per_device(): call(norm_body, [(rows, bf16), ((8, 128), f32), (rows, bf16), (rows, bf16...  1.18 us
  transfers between devices with their start and end apart: 7, of which 4 were waited for; matrix products, arithmetic and copies ran while one was open for 0% of the time, Pallas kernels for 7%

profile of v10, /device:TPU:1, one launch (start us, length us, event | category | flops | bytes accessed | tf_op | source)
XLA Modules:
  0.0 56.4 jit_solution(10345505818721045043)
XLA Ops:
  0.6 1.4 %collective-permute-start = (bf16[128,256]{1,0:T(8,128)(2,1)}, bf16[128,256]{1,0:T(8,128)(2,1)S(1)}, u32[]{:S(2)}, u32[]{:S(2)}) collective-permute-start(bf16[128,256]{1,0:T(8,128)(2,1)} %q_hbm.1), channel_id=1, source_target_pairs={{0,64},{64,0},{1,65},{65,1},{2,66},{66,2},{3,67},{67,3},{4,68},{68... | collective-permute-start | bytes 196616 | tf_op jit(solution)/shard_map/ppermute | solution.py:47
  2.1 0.1 collective-permute-start.1
  2.2 1.2 %norm.1 = (bf16[128,256]{1,0:T(8,128)(2,1)S(1)}, f32[8,128]{1,0:T(8,128)S(1)}, bf16[128,256]{1,0:T(8,128)(2,1)S(1)}, bf16[128,256]{1,0:T(8,128)(2,1)S(1)}) custom-call(bf16[128,256]{1,0:T(8,128)(2,1)} %q_hbm.1, bf16[128,256]{1,0:T(8,128)(2,1)} %v_hbm.1), custom_call_target="tpu_custom_call" | custom-call | flops 1000000000 | tf_op jit(solution)/shard_map/norm/pallas_call | solution.py:396
  3.3 0.0 collective-permute-done.got_q_ref
  3.4 0.2 collective-permute-done.1.got_v_ref
  3.5 0.2 tile.1
  3.7 16.7 %all_to_all.15.block_ref = bf16[8,2,128,256]{3,2,1,0:T(8,128)(2,1)S(1)} all-to-all(bf16[8,2,128,256]{3,2,1,0:T(8,128)(2,1)S(1)} %tile.1), channel_id=1, replica_groups={{68,84,100,116,72,88,104,120},{76,92,108,124,64,80,96,112},{69,85,101,1..., dimensions={0} | all-to-all | bytes 2097152 | tf_op jit(solution)/shard_map/all_to_all | solution.py:43
  20.5 0.4 collective-permute-start.2
  20.9 0.3 collective-permute-start.3
  21.2 1.3 %collective-permute-done.2.got_ref.got_a_ref = bf16[8,128,256]{2,1,0:T(8,128)(2,1)S(1)} collective-permute-done((bf16[8,128,256]{2,1,0:T(8,128)(2,1)S(1)}, bf16[8,128,256]{2,1,0:T(8,128)(2,1)S(1)}, u32[]{:S(2)}, u32[]{:S(2)}) %collective-permute-start.2) | collective-permute-done | bytes 524320 | tf_op jit(solution)/shard_map/ppermute | solution.py:47
  22.5 0.8 %score0.1 = (bf16[4,256,1024]{2,1,0:T(8,128)(2,1)S(1)}, f32[8,1024]{1,0:T(8,128)S(1)}) custom-call(bf16[8,2,128,256]{3,2,1,0:T(8,128)(2,1)S(1)} %all_to_all.15.block_ref, bf16[8,128,256]{2,1,0:T(8,128)(2,1)S(1)} %collective-permute-done.2.got_ref.got_a_ref), custom_call_target="tpu_custom_call" | custom-call | flops 1073741824 | tf_op jit(solution)/shard_map/score0/pallas_call | solution.py:413
  23.3 0.0 collective-permute-done.3.got_b_ref
  23.3 0.8 %score1.1 = (bf16[4,256,1024]{2,1,0:T(8,128)(2,1)S(1)}, f32[8,16,128]{2,1,0:T(8,128)S(1)}) custom-call(bf16[8,2,128,256]{3,2,1,0:T(8,128)(2,1)S(1)} %all_to_all.15.block_ref, bf16[8,128,256]{2,1,0:T(8,128)(2,1)S(1)} %collective-permute-done.2.got_ref.got_a_ref, bf16[8,128,256]{2,1,0:T(8,128)(2,1)S(1)} %collective-permute-done.3.got_b_ref, ...), custom_call_target="tpu_custom_call" | custom-call | flops 1073741824 | tf_op jit(solution)/shard_map/score1/pallas_call | solution.py:414
  24.1 9.3 %all_to_all.16.s_ref = f32[8,16,128]{2,1,0:T(8,128)S(1)} all-to-all(f32[8,16,128]{2,1,0:T(8,128)S(1)} %get-tuple-element.26), channel_id=1, replica_groups={{0,1,2,3,4,5,6,7},{8,9,10,11,12,13,14,15},{16,17,18,19,20,21,22,23},{24..., dimensions={0} | all-to-all | bytes 131072 | tf_op jit(solution)/shard_map/all_to_all | solution.py:43
  33.4 1.3 %first.1 = bf16[1040,256]{1,0:T(8,128)(2,1)S(1)} custom-call(bf16[4,256,1024]{2,1,0:T(8,128)(2,1)S(1)} %get-tuple-element.22.e0_ref, bf16[4,256,1024]{2,1,0:T(8,128)(2,1)S(1)} %get-tuple-element.25.e1_ref, bf16[8,2,128,256]{3,2,1,0:T(8,128)(2,1)S(1)} %all_to_all.15.block_ref, f32[8,16,128]{2,1,0:T(8,128)S(1)} %all_to_all.16.s_ref), custom_call_target="tpu_custom_call" | custom-call | flops 1073741824 | tf_op jit(solution)/shard_map/first/pallas_call | solution.py:419
  34.7 1.1 %collective-permute-start.4 = (bf16[1040,256]{1,0:T(8,128)(2,1)S(1)}, bf16[1040,256]{1,0:T(8,128)(2,1)S(1)}, u32[]{:S(2)}, u32[]{:S(2)}) collective-permute-start(bf16[1040,256]{1,0:T(8,128)(2,1)S(1)} %first.1), channel_id=1, source_target_pairs={{0,64},{64,0},{1,65},{65,1},{2,66},{66,2},{3,67},{67,3},{4,68},{68... | collective-permute-start | bytes 1597448 | tf_op jit(solution)/shard_map/ppermute | solution.py:47
  35.8 0.5 second.1
  36.2 0.4 collective-permute-start.5
  36.6 1.0 %third.1 = (f32[2,256,256]{2,1,0:T(8,128)S(1)}, f32[4,256,256]{2,1,0:T(8,128)S(1)}, bf16[1024,256]{1,0:T(8,128)(2,1)S(1)}) custom-call(bf16[4,256,1024]{2,1,0:T(8,128)(2,1)S(1)} %get-tuple-element.22.e0_ref, bf16[4,256,1024]{2,1,0:T(8,128)(2,1)S(1)} %get-tuple-element.25.e1_ref, bf16[8,128,256]{2,1,0:T(8,128)(2,1)S(1)} %collective-permute-done.2.got_ref.got_a_ref, ...), custom_call_target="tpu_custom_call" | custom-call | flops 1073741824 | tf_op jit(solution)/shard_map/third/pallas_call | solution.py:425
  37.6 0.0 collective-permute-done.4.got_ref
  37.6 0.2 merge.1.part_ref
  37.8 0.4 collective-permute-done.5.got_ref
  38.2 0.1 join.1
  38.4 15.1 %all_to_all.17.w_ref = bf16[8,264,256]{2,1,0:T(8,128)(2,1)S(1)} all-to-all(bf16[8,264,256]{2,1,0:T(8,128)(2,1)S(1)} %join.1), channel_id=1, replica_groups={{68,84,100,116,72,88,104,120},{76,92,108,124,64,80,96,112},{69,85,101,1..., dimensions={0} | all-to-all | bytes 2162688 | tf_op jit(solution)/shard_map/all_to_all | solution.py:43
  53.5 0.1 give.1.give_ref
  53.5 0.1 collective-permute-start.6
  53.6 0.3 own.1.own_ref
  54.0 1.0 %collective-permute-done.6.got_ref = f32[136,256]{1,0:T(8,128)S(1)} collective-permute-done((f32[136,256]{1,0:T(8,128)S(1)}, f32[136,256]{1,0:T(8,128)S(1)}, u32[]{:S(2)}, u32[]{:S(2)}) %collective-permute-start.6) | collective-permute-done | bytes 139296 | tf_op jit(solution)/shard_map/ppermute | solution.py:47
  55.0 1.5 %final.1 = (f32[128,256]{1,0:T(8,128)}, f32[128,256]{1,0:T(8,128)}, f32[1,1]{1,0:T(1,128)}) custom-call(bf16[128,256]{1,0:T(8,128)(2,1)S(1)} %get-tuple-element.19.q_ref, bf16[128,256]{1,0:T(8,128)(2,1)S(1)} %get-tuple-element.20.v_ref, f32[128,256]{1,0:T(8,128)S(1)} %own.1.own_ref, f32[136,256]{1,0:T(8,128)S(1)} %give.1.give_ref, ...), custom_call_target="tpu_custom_call" | custom-call | tf_op jit(solution)/shard_map/final/pallas_call | solution.py:435
  (2 shorter events, 0.1 us)
Async XLA Ops:
  0.6 2.7 %collective-permute-start = (bf16[128,256]{1,0:T(8,128)(2,1)}, bf16[128,256]{1,0:T(8,128)(2,1)S(1)}, u32[]{:S(2)}, u32[]{:S(2)}) collective-permute-start(bf16[128,256]{1,0:T(8,128)(2,1)} %q_hbm.1), channel_id=1, source_target_pairs={{0,64},{64,0},{1,65},{65,1},{2,66},{66,2},{3,67},{67,3},{4,68},{68... | collective-permute-start | bytes 196616 | tf_op jit(solution)/shard_map/ppermute | solution.py:47
  2.1 1.5 %collective-permute-start.1 = (bf16[128,256]{1,0:T(8,128)(2,1)}, bf16[128,256]{1,0:T(8,128)(2,1)S(1)}, u32[]{:S(2)}, u32[]{:S(2)}) collective-permute-start(bf16[128,256]{1,0:T(8,128)(2,1)} %v_hbm.1), channel_id=1, source_target_pairs={{0,64},{64,0},{1,65},{65,1},{2,66},{66,2},{3,67},{67,3},{4,68},{68... | collective-permute-start | bytes 196616 | tf_op jit(solution)/shard_map/ppermute | solution.py:47
  20.5 2.0 %collective-permute-start.2 = (bf16[8,128,256]{2,1,0:T(8,128)(2,1)S(1)}, bf16[8,128,256]{2,1,0:T(8,128)(2,1)S(1)}, u32[]{:S(2)}, u32[]{:S(2)}) collective-permute-start(bf16[8,128,256]{2,1,0:T(8,128)(2,1)S(1)} %half.1), channel_id=1, source_target_pairs={{0,64},{64,0},{1,65},{65,1},{2,66},{66,2},{3,67},{67,3},{4,68},{68... | collective-permute-start | bytes 1572872 | tf_op jit(solution)/shard_map/ppermute | solution.py:47
  20.9 2.4 %collective-permute-start.3 = (bf16[8,128,256]{2,1,0:T(8,128)(2,1)S(1)}, bf16[8,128,256]{2,1,0:T(8,128)(2,1)S(1)}, u32[]{:S(2)}, u32[]{:S(2)}) collective-permute-start(bf16[8,128,256]{2,1,0:T(8,128)(2,1)S(1)} %rest.1), channel_id=1, source_target_pairs={{0,64},{64,0},{1,65},{65,1},{2,66},{66,2},{3,67},{67,3},{4,68},{68... | collective-permute-start | bytes 1572872 | tf_op jit(solution)/shard_map/ppermute | solution.py:47
  34.7 2.9 %collective-permute-start.4 = (bf16[1040,256]{1,0:T(8,128)(2,1)S(1)}, bf16[1040,256]{1,0:T(8,128)(2,1)S(1)}, u32[]{:S(2)}, u32[]{:S(2)}) collective-permute-start(bf16[1040,256]{1,0:T(8,128)(2,1)S(1)} %first.1), channel_id=1, source_target_pairs={{0,64},{64,0},{1,65},{65,1},{2,66},{66,2},{3,67},{67,3},{4,68},{68... | collective-permute-start | bytes 1597448 | tf_op jit(solution)/shard_map/ppermute | solution.py:47
  36.2 2.0 %collective-permute-start.5 = (bf16[1024,256]{1,0:T(8,128)(2,1)S(1)}, bf16[1024,256]{1,0:T(8,128)(2,1)S(1)}, u32[]{:S(2)}, u32[]{:S(2)}) collective-permute-start(bf16[1024,256]{1,0:T(8,128)(2,1)S(1)} %get-tuple-element.31), channel_id=1, source_target_pairs={{0,64},{64,0},{1,65},{65,1},{2,66},{66,2},{3,67},{67,3},{4,68},{68... | collective-permute-start | bytes 1572872 | tf_op jit(solution)/shard_map/ppermute | solution.py:47
  53.5 1.4 %collective-permute-start.6 = (f32[136,256]{1,0:T(8,128)S(1)}, f32[136,256]{1,0:T(8,128)S(1)}, u32[]{:S(2)}, u32[]{:S(2)}) collective-permute-start(f32[136,256]{1,0:T(8,128)S(1)} %give.1.give_ref), channel_id=1, source_target_pairs={{0,64},{64,0},{1,65},{65,1},{2,66},{66,2},{3,67},{67,3},{4,68},{68... | collective-permute-start | bytes 417800 | tf_op jit(solution)/shard_map/ppermute | solution.py:47

commit v11 on v9

--- a/solution.py
+++ b/solution.py
@@ -12,6 +12,8 @@
 GROUP = 8
 ROWS, D = 128, 256
 ITEM = 1
+RING_Q, RING_V, PAIR = "z", "y", "x"
+NEAR, CROSS = ((0, 1), (2, 3)), ((1, 2), (3, 0))
 
 sharpness = 0.05
 tiny_square = 1e-12
@@ -19,24 +21,29 @@
 f32, bf16 = jnp.float32, jnp.bfloat16
 
 
-def device_of(core, z, y, x):
-    return ((core * 4 + z) * 4 + y) * 4 + x
-
-
-def query_groups(core):
-    return [[device_of(core, z, y, x) for y in pair for x in range(4)] for z in range(4) for pair in ((0, 1), (2, 3))]
-
-
-def item_groups(core):
-    return [[device_of(core, z, y, x) for y in pair for z in range(4)] for x in range(4) for pair in ((1, 2), (3, 0))]
+def groups(core, ring, pairs, fixed, order):
+    def device(at):
+        return ((core * 4 + at["z"]) * 4 + at["y"]) * 4 + at["x"]
+
+    return [
+        [device({fixed: f, PAIR: p, ring: r}) for p in pair for r in order] for f in range(4) for pair in pairs
+    ]
+
+
+def query_groups(core, order):
+    return groups(core, RING_Q, NEAR, RING_V, order)
+
+
+def item_groups(core, order):
+    return groups(core, RING_V, CROSS, RING_Q, order)
 
 
 def query_index():
-    return lax.axis_index("y") % 2 * 4 + lax.axis_index("x")
-
-
-BULK = item_groups(ITEM) + query_groups(1 - ITEM)
-QUERY = query_groups(0) + query_groups(1)
+    return lax.axis_index(PAIR) % 2 * 4 + 3 - lax.axis_index(RING_Q)
+
+
+BULK = item_groups(ITEM, (2, 1, 0, 3)) + query_groups(1 - ITEM, (3, 2, 1, 0))
+QUERY = query_groups(0, (3, 1, 0, 2)) + query_groups(1, (3, 1, 0, 2))
 
 
 def exchange(pieces, groups):
@@ -389,13 +396,13 @@
     rows = (ROWS, D)
     bulk = (GROUP, 2, ROWS, D)
     in_hbm = [pltpu.with_memory_space_constraint(a, pltpu.HBM) for a in (queries, items)]
-    mine, pos = call(
+    mine, pos, q_raw, v_raw = call(
         norm_body,
-        [(rows, bf16), ((8, 128), f32)],
+        [(rows, bf16), ((8, 128), f32), (rows, bf16), (rows, bf16)],
         "norm",
         10**9,
         ins=[pl.BlockSpec(memory_space=pltpu.HBM)] * 2,
-        scratch=[pltpu.VMEM(rows, bf16), pltpu.VMEM(rows, bf16), pltpu.SemaphoreType.DMA((2,))],
+        scratch=[pltpu.SemaphoreType.DMA((2,))],
     )(*in_hbm)
     (tile,) = call(tile_body, [(bulk, bf16)], "tile")(mine, swap_cores(queries), swap_cores(items))
     block = exchange(tile, BULK)
@@ -427,10 +434,10 @@
     out = exchange(out, BULK)
     (give,) = call(give_body, [((136, D), f32)], "give")(out)
     got = swap_cores(give)
-    (own,) = call(own_body, [(rows, f32)], "own", flops)(out, queries, items, sums)
+    (own,) = call(own_body, [(rows, f32)], "own", flops)(out, q_raw, v_raw, sums)
     q_slope, v_slope, loss = call(
         final_body, [(rows, f32), (rows, f32), ((1, 1), f32, pltpu.SMEM)], "final"
-    )(queries, items, own, give, got, sums)
+    )(q_raw, v_raw, own, give, got, sums)
     return loss.reshape(()), q_slope, v_slope
 
 

time: 56.2 us -> 53.2 us (0.947)
  blocking collectives: 41.1 us -> 37.6 us
  local copies, waits for them, and re-layouts: 0.7 us -> 0 us
  starting transfers between devices: 3.75 us -> 4.37 us
    all_to_all x3, blocking collectives: 41.1 us -> 37.6 us  [exchange(): lax.all_to_all(pieces, AXES, 0, 0, tiled=True, axis_index_groups=groups)]
    unnamed x4 -> x0, local copies, waits for them, and re-layouts: 0.7 us -> none
    ppermute x7, starting transfers between devices: 3.75 us -> 4.37 us  [swap_cores(): return lax.ppermute(value, 'blk', [(0, 1), (1, 0)])]
where the time goes in v11:
time: 53.2 us; the launch traced here: 52.9 us
  blocking collectives  37.6 us (71%)
  Pallas kernels  7.43 us (14%)
  starting transfers between devices  4.37 us (8%)
  waiting for transfers between devices  2.68 us (5%)
  between operations  0.75 us (1%)
    all_to_all x3, blocking collectives, exchange(): lax.all_to_all(pieces, AXES, 0, 0, tiled=True, axis_index_groups=groups)  37.6 us
    ppermute x7, starting transfers between devices, swap_cores(): return lax.ppermute(value, 'blk', [(0, 1), (1, 0)])  4.37 us
    ppermute x7, waiting for transfers between devices, swap_cores(): return lax.ppermute(value, 'blk', [(0, 1), (1, 0)])  2.68 us
    pallas_call x1, Pallas kernels, per_device(): call(first_body, [((1040, D), bf16)], 'first', flops)(e0, e1, block, sums)  1.28 us
    pallas_call x1, Pallas kernels, per_device(): call(norm_body, [(rows, bf16), ((8, 128), f32), (rows, bf16), (rows, bf16...  1.18 us
  transfers between devices with their start and end apart: 7, of which 4 were waited for; matrix products, arithmetic and copies ran while one was open for 0% of the time, Pallas kernels for 7%

profile of v11, /device:TPU:1, one launch (start us, length us, event | category | flops | bytes accessed | tf_op | source)
XLA Modules:
  0.0 52.9 jit_solution(6541270379383844101)
XLA Ops:
  0.6 1.4 %collective-permute-start = (bf16[128,256]{1,0:T(8,128)(2,1)}, bf16[128,256]{1,0:T(8,128)(2,1)S(1)}, u32[]{:S(2)}, u32[]{:S(2)}) collective-permute-start(bf16[128,256]{1,0:T(8,128)(2,1)} %q_hbm.1), channel_id=1, source_target_pairs={{0,64},{64,0},{1,65},{65,1},{2,66},{66,2},{3,67},{67,3},{4,68},{68... | collective-permute-start | bytes 196616 | tf_op jit(solution)/shard_map/ppermute | solution.py:54
  2.1 0.1 collective-permute-start.1
  2.2 1.2 %norm.1 = (bf16[128,256]{1,0:T(8,128)(2,1)S(1)}, f32[8,128]{1,0:T(8,128)S(1)}, bf16[128,256]{1,0:T(8,128)(2,1)S(1)}, bf16[128,256]{1,0:T(8,128)(2,1)S(1)}) custom-call(bf16[128,256]{1,0:T(8,128)(2,1)} %q_hbm.1, bf16[128,256]{1,0:T(8,128)(2,1)} %v_hbm.1), custom_call_target="tpu_custom_call" | custom-call | flops 1000000000 | tf_op jit(solution)/shard_map/norm/pallas_call | solution.py:399
  3.3 0.0 collective-permute-done.got_q_ref
  3.4 0.2 collective-permute-done.1.got_v_ref
  3.5 0.2 tile.1
  3.7 15.0 %all_to_all.15.block_ref = bf16[8,2,128,256]{3,2,1,0:T(8,128)(2,1)S(1)} all-to-all(bf16[8,2,128,256]{3,2,1,0:T(8,128)(2,1)S(1)} %tile.1), channel_id=1, replica_groups={{73,69,65,77,74,70,66,78},{75,71,67,79,72,68,64,76},{89,85,81,93,90,86,..., dimensions={0} | all-to-all | bytes 2097152 | tf_op jit(solution)/shard_map/all_to_all | solution.py:50
  18.8 1.1 %collective-permute-start.2 = (bf16[8,128,256]{2,1,0:T(8,128)(2,1)S(1)}, bf16[8,128,256]{2,1,0:T(8,128)(2,1)S(1)}, u32[]{:S(2)}, u32[]{:S(2)}) collective-permute-start(bf16[8,128,256]{2,1,0:T(8,128)(2,1)S(1)} %half.1), channel_id=1, source_target_pairs={{0,64},{64,0},{1,65},{65,1},{2,66},{66,2},{3,67},{67,3},{4,68},{68... | collective-permute-start | bytes 1572872 | tf_op jit(solution)/shard_map/ppermute | solution.py:54
  19.9 0.1 collective-permute-start.3
  20.0 1.4 %collective-permute-done.2.got_ref.got_a_ref = bf16[8,128,256]{2,1,0:T(8,128)(2,1)S(1)} collective-permute-done((bf16[8,128,256]{2,1,0:T(8,128)(2,1)S(1)}, bf16[8,128,256]{2,1,0:T(8,128)(2,1)S(1)}, u32[]{:S(2)}, u32[]{:S(2)}) %collective-permute-start.2) | collective-permute-done | bytes 524320 | tf_op jit(solution)/shard_map/ppermute | solution.py:54
  21.4 0.8 %score0.1 = (bf16[4,256,1024]{2,1,0:T(8,128)(2,1)S(1)}, f32[8,1024]{1,0:T(8,128)S(1)}) custom-call(bf16[8,2,128,256]{3,2,1,0:T(8,128)(2,1)S(1)} %all_to_all.15.block_ref, bf16[8,128,256]{2,1,0:T(8,128)(2,1)S(1)} %collective-permute-done.2.got_ref.got_a_ref), custom_call_target="tpu_custom_call" | custom-call | flops 1073741824 | tf_op jit(solution)/shard_map/score0/pallas_call | solution.py:416
  22.2 0.0 collective-permute-done.3.got_b_ref
  22.2 0.8 %score1.1 = (bf16[4,256,1024]{2,1,0:T(8,128)(2,1)S(1)}, f32[8,16,128]{2,1,0:T(8,128)S(1)}) custom-call(bf16[8,2,128,256]{3,2,1,0:T(8,128)(2,1)S(1)} %all_to_all.15.block_ref, bf16[8,128,256]{2,1,0:T(8,128)(2,1)S(1)} %collective-permute-done.2.got_ref.got_a_ref, bf16[8,128,256]{2,1,0:T(8,128)(2,1)S(1)} %collective-permute-done.3.got_b_ref, ...), custom_call_target="tpu_custom_call" | custom-call | flops 1073741824 | tf_op jit(solution)/shard_map/score1/pallas_call | solution.py:417
  23.0 8.5 %all_to_all.16.s_ref = f32[8,16,128]{2,1,0:T(8,128)S(1)} all-to-all(f32[8,16,128]{2,1,0:T(8,128)S(1)} %get-tuple-element.26), channel_id=1, replica_groups={{48,16,0,32,49,17,1,33},{50,18,2,34,51,19,3,35},{52,20,4,36,53,21,5,37}..., dimensions={0} | all-to-all | bytes 131072 | tf_op jit(solution)/shard_map/all_to_all | solution.py:50
  31.6 1.3 %first.1 = bf16[1040,256]{1,0:T(8,128)(2,1)S(1)} custom-call(bf16[4,256,1024]{2,1,0:T(8,128)(2,1)S(1)} %get-tuple-element.22.e0_ref, bf16[4,256,1024]{2,1,0:T(8,128)(2,1)S(1)} %get-tuple-element.25.e1_ref, bf16[8,2,128,256]{3,2,1,0:T(8,128)(2,1)S(1)} %all_to_all.15.block_ref, f32[8,16,128]{2,1,0:T(8,128)S(1)} %all_to_all.16.s_ref), custom_call_target="tpu_custom_call" | custom-call | flops 1073741824 | tf_op jit(solution)/shard_map/first/pallas_call | solution.py:422
  32.8 0.8 %collective-permute-start.4 = (bf16[1040,256]{1,0:T(8,128)(2,1)S(1)}, bf16[1040,256]{1,0:T(8,128)(2,1)S(1)}, u32[]{:S(2)}, u32[]{:S(2)}) collective-permute-start(bf16[1040,256]{1,0:T(8,128)(2,1)S(1)} %first.1), channel_id=1, source_target_pairs={{0,64},{64,0},{1,65},{65,1},{2,66},{66,2},{3,67},{67,3},{4,68},{68... | collective-permute-start | bytes 1597448 | tf_op jit(solution)/shard_map/ppermute | solution.py:54
  33.7 0.5 second.1
  34.1 0.4 collective-permute-start.5
  34.5 1.0 %third.1 = (f32[2,256,256]{2,1,0:T(8,128)S(1)}, f32[4,256,256]{2,1,0:T(8,128)S(1)}, bf16[1024,256]{1,0:T(8,128)(2,1)S(1)}) custom-call(bf16[4,256,1024]{2,1,0:T(8,128)(2,1)S(1)} %get-tuple-element.22.e0_ref, bf16[4,256,1024]{2,1,0:T(8,128)(2,1)S(1)} %get-tuple-element.25.e1_ref, bf16[8,128,256]{2,1,0:T(8,128)(2,1)S(1)} %collective-permute-done.2.got_ref.got_a_ref, ...), custom_call_target="tpu_custom_call" | custom-call | flops 1073741824 | tf_op jit(solution)/shard_map/third/pallas_call | solution.py:428
  35.5 0.0 collective-permute-done.4.got_ref
  35.5 0.2 merge.1.part_ref
  35.7 0.4 collective-permute-done.5.got_ref
  36.1 0.1 join.1
  36.3 14.1 %all_to_all.17.w_ref = bf16[8,264,256]{2,1,0:T(8,128)(2,1)S(1)} all-to-all(bf16[8,264,256]{2,1,0:T(8,128)(2,1)S(1)} %join.1), channel_id=1, replica_groups={{73,69,65,77,74,70,66,78},{75,71,67,79,72,68,64,76},{89,85,81,93,90,86,..., dimensions={0} | all-to-all | bytes 2162688 | tf_op jit(solution)/shard_map/all_to_all | solution.py:50
  50.4 0.1 give.1.give_ref
  50.4 0.5 collective-permute-start.6
  50.9 0.3 own.1.own_ref
  51.2 0.7 %collective-permute-done.6.got_ref = f32[136,256]{1,0:T(8,128)S(1)} collective-permute-done((f32[136,256]{1,0:T(8,128)S(1)}, f32[136,256]{1,0:T(8,128)S(1)}, u32[]{:S(2)}, u32[]{:S(2)}) %collective-permute-start.6) | collective-permute-done | bytes 139296 | tf_op jit(solution)/shard_map/ppermute | solution.py:54
  51.9 1.0 %final.1 = (f32[128,256]{1,0:T(8,128)}, f32[128,256]{1,0:T(8,128)}, f32[1,1]{1,0:T(1,128)}) custom-call(bf16[128,256]{1,0:T(8,128)(2,1)S(1)} %get-tuple-element.19.q_ref, bf16[128,256]{1,0:T(8,128)(2,1)S(1)} %get-tuple-element.20.v_ref, f32[128,256]{1,0:T(8,128)S(1)} %own.1.own_ref, f32[136,256]{1,0:T(8,128)S(1)} %give.1.give_ref, ...), custom_call_target="tpu_custom_call" | custom-call | tf_op jit(solution)/shard_map/final/pallas_call | solution.py:438
  (2 shorter events, 0.1 us)
Async XLA Ops:
  0.6 2.7 %collective-permute-start = (bf16[128,256]{1,0:T(8,128)(2,1)}, bf16[128,256]{1,0:T(8,128)(2,1)S(1)}, u32[]{:S(2)}, u32[]{:S(2)}) collective-permute-start(bf16[128,256]{1,0:T(8,128)(2,1)} %q_hbm.1), channel_id=1, source_target_pairs={{0,64},{64,0},{1,65},{65,1},{2,66},{66,2},{3,67},{67,3},{4,68},{68... | collective-permute-start | bytes 196616 | tf_op jit(solution)/shard_map/ppermute | solution.py:54
  2.1 1.5 %collective-permute-start.1 = (bf16[128,256]{1,0:T(8,128)(2,1)}, bf16[128,256]{1,0:T(8,128)(2,1)S(1)}, u32[]{:S(2)}, u32[]{:S(2)}) collective-permute-start(bf16[128,256]{1,0:T(8,128)(2,1)} %v_hbm.1), channel_id=1, source_target_pairs={{0,64},{64,0},{1,65},{65,1},{2,66},{66,2},{3,67},{67,3},{4,68},{68... | collective-permute-start | bytes 196616 | tf_op jit(solution)/shard_map/ppermute | solution.py:54
  18.8 2.6 %collective-permute-start.2 = (bf16[8,128,256]{2,1,0:T(8,128)(2,1)S(1)}, bf16[8,128,256]{2,1,0:T(8,128)(2,1)S(1)}, u32[]{:S(2)}, u32[]{:S(2)}) collective-permute-start(bf16[8,128,256]{2,1,0:T(8,128)(2,1)S(1)} %half.1), channel_id=1, source_target_pairs={{0,64},{64,0},{1,65},{65,1},{2,66},{66,2},{3,67},{67,3},{4,68},{68... | collective-permute-start | bytes 1572872 | tf_op jit(solution)/shard_map/ppermute | solution.py:54
  19.9 2.3 %collective-permute-start.3 = (bf16[8,128,256]{2,1,0:T(8,128)(2,1)S(1)}, bf16[8,128,256]{2,1,0:T(8,128)(2,1)S(1)}, u32[]{:S(2)}, u32[]{:S(2)}) collective-permute-start(bf16[8,128,256]{2,1,0:T(8,128)(2,1)S(1)} %rest.1), channel_id=1, source_target_pairs={{0,64},{64,0},{1,65},{65,1},{2,66},{66,2},{3,67},{67,3},{4,68},{68... | collective-permute-start | bytes 1572872 | tf_op jit(solution)/shard_map/ppermute | solution.py:54
  32.8 2.6 %collective-permute-start.4 = (bf16[1040,256]{1,0:T(8,128)(2,1)S(1)}, bf16[1040,256]{1,0:T(8,128)(2,1)S(1)}, u32[]{:S(2)}, u32[]{:S(2)}) collective-permute-start(bf16[1040,256]{1,0:T(8,128)(2,1)S(1)} %first.1), channel_id=1, source_target_pairs={{0,64},{64,0},{1,65},{65,1},{2,66},{66,2},{3,67},{67,3},{4,68},{68... | collective-permute-start | bytes 1597448 | tf_op jit(solution)/shard_map/ppermute | solution.py:54
  34.1 2.0 %collective-permute-start.5 = (bf16[1024,256]{1,0:T(8,128)(2,1)S(1)}, bf16[1024,256]{1,0:T(8,128)(2,1)S(1)}, u32[]{:S(2)}, u32[]{:S(2)}) collective-permute-start(bf16[1024,256]{1,0:T(8,128)(2,1)S(1)} %get-tuple-element.31), channel_id=1, source_target_pairs={{0,64},{64,0},{1,65},{65,1},{2,66},{66,2},{3,67},{67,3},{4,68},{68... | collective-permute-start | bytes 1572872 | tf_op jit(solution)/shard_map/ppermute | solution.py:54
  50.4 1.5 %collective-permute-start.6 = (f32[136,256]{1,0:T(8,128)S(1)}, f32[136,256]{1,0:T(8,128)S(1)}, u32[]{:S(2)}, u32[]{:S(2)}) collective-permute-start(f32[136,256]{1,0:T(8,128)S(1)} %give.1.give_ref), channel_id=1, source_target_pairs={{0,64},{64,0},{1,65},{65,1},{2,66},{66,2},{3,67},{67,3},{4,68},{68... | collective-permute-start | bytes 417800 | tf_op jit(solution)/shard_map/ppermute | solution.py:54

commit v12 on v11

--- a/solution.py
+++ b/solution.py
@@ -21,29 +21,41 @@
 f32, bf16 = jnp.float32, jnp.bfloat16
 
 
-def groups(core, ring, pairs, fixed, order):
+ITEM_ORDER = ((7, 1, 0, 2, 6, 5, 4, 3), (2, 1, 0, 3, 4, 5, 6, 7))
+QUERY_ORDER = ((3, 2, 7, 0, 1, 6, 5, 4), (3, 4, 1, 0, 7, 6, 5, 2))
+SUM_ORDER = ((3, 1, 0, 2, 7, 5, 4, 6),) * 2
+
+
+def groups(core, ring, pairs, fixed, orders):
     def device(at):
         return ((core * 4 + at["z"]) * 4 + at["y"]) * 4 + at["x"]
 
     return [
-        [device({fixed: f, PAIR: p, ring: r}) for p in pair for r in order] for f in range(4) for pair in pairs
+        [device({fixed: f, PAIR: pair[m // 4], ring: m % 4}) for m in order]
+        for f in range(4)
+        for pair, order in zip(pairs, orders)
     ]
 
 
-def query_groups(core, order):
-    return groups(core, RING_Q, NEAR, RING_V, order)
-
-
-def item_groups(core, order):
-    return groups(core, RING_V, CROSS, RING_Q, order)
+def query_groups(core, orders):
+    return groups(core, RING_Q, NEAR, RING_V, orders)
+
+
+def item_groups(core, orders):
+    return groups(core, RING_V, CROSS, RING_Q, orders)
 
 
 def query_index():
-    return lax.axis_index(PAIR) % 2 * 4 + 3 - lax.axis_index(RING_Q)
-
-
-BULK = item_groups(ITEM, (2, 1, 0, 3)) + query_groups(1 - ITEM, (3, 2, 1, 0))
-QUERY = query_groups(0, (3, 1, 0, 2)) + query_groups(1, (3, 1, 0, 2))
+    at = lax.axis_index(PAIR)
+    member = at % 2 * 4 + lax.axis_index(RING_Q)
+    index = jnp.int32(0)
+    for k, (m0, m1) in enumerate(zip(*QUERY_ORDER)):
+        index = jnp.where(member == jnp.where(at < 2, m0, m1), k, index)
+    return index
+
+
+BULK = item_groups(ITEM, ITEM_ORDER) + query_groups(1 - ITEM, QUERY_ORDER)
+QUERY = query_groups(0, SUM_ORDER) + query_groups(1, SUM_ORDER)
 
 
 def exchange(pieces, groups):

time: 53.2 us -> 53 us (level)
  blocking collectives: 37.6 us -> 36.7 us
  starting transfers between devices: 4.37 us -> 5.11 us
    all_to_all x3, blocking collectives: 37.6 us -> 36.7 us  [exchange(): lax.all_to_all(pieces, AXES, 0, 0, tiled=True, axis_index_groups=groups)]
    ppermute x7, starting transfers between devices: 4.37 us -> 5.11 us  [swap_cores(): return lax.ppermute(value, 'blk', [(0, 1), (1, 0)])]
where the time goes in v12:
time: 53 us; the launch traced here: 52.8 us
  blocking collectives  36.7 us (69%)
  Pallas kernels  7.43 us (14%)
  starting transfers between devices  5.11 us (10%)
  waiting for transfers between devices  2.76 us (5%)
  between operations  0.75 us (1%)
    all_to_all x3, blocking collectives, exchange(): lax.all_to_all(pieces, AXES, 0, 0, tiled=True, axis_index_groups=groups)  36.7 us
    ppermute x7, starting transfers between devices, swap_cores(): return lax.ppermute(value, 'blk', [(0, 1), (1, 0)])  5.11 us
    ppermute x7, waiting for transfers between devices, swap_cores(): return lax.ppermute(value, 'blk', [(0, 1), (1, 0)])  2.76 us
    pallas_call x1, Pallas kernels, per_device(): call(first_body, [((1040, D), bf16)], 'first', flops)(e0, e1, block, sums)  1.28 us
    pallas_call x1, Pallas kernels, per_device(): call(norm_body, [(rows, bf16), ((8, 128), f32), (rows, bf16), (rows, bf16...  1.18 us
  transfers between devices with their start and end apart: 7, of which 4 were waited for; matrix products, arithmetic and copies ran while one was open for 0% of the time, Pallas kernels for 7%

profile of v12, /device:TPU:1, one launch (start us, length us, event | category | flops | bytes accessed | tf_op | source)
XLA Modules:
  0.0 52.8 jit_solution(15021542390225724410)
XLA Ops:
  0.6 1.4 %collective-permute-start = (bf16[128,256]{1,0:T(8,128)(2,1)}, bf16[128,256]{1,0:T(8,128)(2,1)S(1)}, u32[]{:S(2)}, u32[]{:S(2)}) collective-permute-start(bf16[128,256]{1,0:T(8,128)(2,1)} %q_hbm.1), channel_id=1, source_target_pairs={{0,64},{64,0},{1,65},{65,1},{2,66},{66,2},{3,67},{67,3},{4,68},{68... | collective-permute-start | bytes 196616 | tf_op jit(solution)/shard_map/ppermute | solution.py:66
  2.1 0.1 collective-permute-start.1
  2.2 1.2 %norm.1 = (bf16[128,256]{1,0:T(8,128)(2,1)S(1)}, f32[8,128]{1,0:T(8,128)S(1)}, bf16[128,256]{1,0:T(8,128)(2,1)S(1)}, bf16[128,256]{1,0:T(8,128)(2,1)S(1)}) custom-call(bf16[128,256]{1,0:T(8,128)(2,1)} %q_hbm.1, bf16[128,256]{1,0:T(8,128)(2,1)} %v_hbm.1), custom_call_target="tpu_custom_call" | custom-call | flops 1000000000 | tf_op jit(solution)/shard_map/norm/pallas_call | solution.py:411
  3.3 0.0 collective-permute-done.got_q_ref
  3.4 0.2 collective-permute-done.1.got_v_ref
  3.5 0.2 tile.1
  3.7 14.5 %all_to_all.15.block_ref = bf16[8,2,128,256]{3,2,1,0:T(8,128)(2,1)S(1)} all-to-all(bf16[8,2,128,256]{3,2,1,0:T(8,128)(2,1)S(1)} %tile.1), channel_id=1, replica_groups={{78,69,65,73,74,70,66,77},{75,71,67,79,64,68,72,76},{94,85,81,89,90,86,..., dimensions={0} | all-to-all | bytes 2097152 | tf_op jit(solution)/shard_map/all_to_all | solution.py:62
  18.3 1.9 %collective-permute-start.2 = (bf16[8,128,256]{2,1,0:T(8,128)(2,1)S(1)}, bf16[8,128,256]{2,1,0:T(8,128)(2,1)S(1)}, u32[]{:S(2)}, u32[]{:S(2)}) collective-permute-start(bf16[8,128,256]{2,1,0:T(8,128)(2,1)S(1)} %half.1), channel_id=1, source_target_pairs={{0,64},{64,0},{1,65},{65,1},{2,66},{66,2},{3,67},{67,3},{4,68},{68... | collective-permute-start | bytes 1572872 | tf_op jit(solution)/shard_map/ppermute | solution.py:66
  20.3 0.1 collective-permute-start.3
  20.4 1.4 %collective-permute-done.2.got_ref.got_a_ref = bf16[8,128,256]{2,1,0:T(8,128)(2,1)S(1)} collective-permute-done((bf16[8,128,256]{2,1,0:T(8,128)(2,1)S(1)}, bf16[8,128,256]{2,1,0:T(8,128)(2,1)S(1)}, u32[]{:S(2)}, u32[]{:S(2)}) %collective-permute-start.2) | collective-permute-done | bytes 524320 | tf_op jit(solution)/shard_map/ppermute | solution.py:66
  21.8 0.8 %score0.1 = (bf16[4,256,1024]{2,1,0:T(8,128)(2,1)S(1)}, f32[8,1024]{1,0:T(8,128)S(1)}) custom-call(bf16[8,2,128,256]{3,2,1,0:T(8,128)(2,1)S(1)} %all_to_all.15.block_ref, bf16[8,128,256]{2,1,0:T(8,128)(2,1)S(1)} %collective-permute-done.2.got_ref.got_a_ref), custom_call_target="tpu_custom_call" | custom-call | flops 1073741824 | tf_op jit(solution)/shard_map/score0/pallas_call | solution.py:428
  22.6 0.0 collective-permute-done.3.got_b_ref
  22.6 0.8 %score1.1 = (bf16[4,256,1024]{2,1,0:T(8,128)(2,1)S(1)}, f32[8,16,128]{2,1,0:T(8,128)S(1)}) custom-call(bf16[8,2,128,256]{3,2,1,0:T(8,128)(2,1)S(1)} %all_to_all.15.block_ref, bf16[8,128,256]{2,1,0:T(8,128)(2,1)S(1)} %collective-permute-done.2.got_ref.got_a_ref, bf16[8,128,256]{2,1,0:T(8,128)(2,1)S(1)} %collective-permute-done.3.got_b_ref, ...), custom_call_target="tpu_custom_call" | custom-call | flops 1073741824 | tf_op jit(solution)/shard_map/score1/pallas_call | solution.py:429
  23.4 7.9 %all_to_all.16.s_ref = f32[8,16,128]{2,1,0:T(8,128)S(1)} all-to-all(f32[8,16,128]{2,1,0:T(8,128)S(1)} %get-tuple-element.26), channel_id=1, replica_groups={{48,16,0,32,49,17,1,33},{50,18,2,34,51,19,3,35},{52,20,4,36,53,21,5,37}..., dimensions={0} | all-to-all | bytes 131072 | tf_op jit(solution)/shard_map/all_to_all | solution.py:62
  31.3 1.3 %first.1 = bf16[1040,256]{1,0:T(8,128)(2,1)S(1)} custom-call(bf16[4,256,1024]{2,1,0:T(8,128)(2,1)S(1)} %get-tuple-element.22.e0_ref, bf16[4,256,1024]{2,1,0:T(8,128)(2,1)S(1)} %get-tuple-element.25.e1_ref, bf16[8,2,128,256]{3,2,1,0:T(8,128)(2,1)S(1)} %all_to_all.15.block_ref, f32[8,16,128]{2,1,0:T(8,128)S(1)} %all_to_all.16.s_ref), custom_call_target="tpu_custom_call" | custom-call | flops 1073741824 | tf_op jit(solution)/shard_map/first/pallas_call | solution.py:434
  32.6 0.8 %collective-permute-start.4 = (bf16[1040,256]{1,0:T(8,128)(2,1)S(1)}, bf16[1040,256]{1,0:T(8,128)(2,1)S(1)}, u32[]{:S(2)}, u32[]{:S(2)}) collective-permute-start(bf16[1040,256]{1,0:T(8,128)(2,1)S(1)} %first.1), channel_id=1, source_target_pairs={{0,64},{64,0},{1,65},{65,1},{2,66},{66,2},{3,67},{67,3},{4,68},{68... | collective-permute-start | bytes 1597448 | tf_op jit(solution)/shard_map/ppermute | solution.py:66
  33.4 0.5 second.1
  33.9 0.4 collective-permute-start.5
  34.2 1.0 %third.1 = (f32[2,256,256]{2,1,0:T(8,128)S(1)}, f32[4,256,256]{2,1,0:T(8,128)S(1)}, bf16[1024,256]{1,0:T(8,128)(2,1)S(1)}) custom-call(bf16[4,256,1024]{2,1,0:T(8,128)(2,1)S(1)} %get-tuple-element.22.e0_ref, bf16[4,256,1024]{2,1,0:T(8,128)(2,1)S(1)} %get-tuple-element.25.e1_ref, bf16[8,128,256]{2,1,0:T(8,128)(2,1)S(1)} %collective-permute-done.2.got_ref.got_a_ref, ...), custom_call_target="tpu_custom_call" | custom-call | flops 1073741824 | tf_op jit(solution)/shard_map/third/pallas_call | solution.py:440
  35.2 0.0 collective-permute-done.4.got_ref
  35.2 0.2 merge.1.part_ref
  35.4 0.4 collective-permute-done.5.got_ref
  35.9 0.1 join.1
  36.0 14.3 %all_to_all.17.w_ref = bf16[8,264,256]{2,1,0:T(8,128)(2,1)S(1)} all-to-all(bf16[8,264,256]{2,1,0:T(8,128)(2,1)S(1)} %join.1), channel_id=1, replica_groups={{78,69,65,73,74,70,66,77},{75,71,67,79,64,68,72,76},{94,85,81,89,90,86,..., dimensions={0} | all-to-all | bytes 2162688 | tf_op jit(solution)/shard_map/all_to_all | solution.py:62
  50.3 0.1 give.1.give_ref
  50.3 0.4 collective-permute-start.6
  50.7 0.3 own.1.own_ref
  51.0 0.7 %collective-permute-done.6.got_ref = f32[136,256]{1,0:T(8,128)S(1)} collective-permute-done((f32[136,256]{1,0:T(8,128)S(1)}, f32[136,256]{1,0:T(8,128)S(1)}, u32[]{:S(2)}, u32[]{:S(2)}) %collective-permute-start.6) | collective-permute-done | bytes 139296 | tf_op jit(solution)/shard_map/ppermute | solution.py:66
  51.8 1.0 %final.1 = (f32[128,256]{1,0:T(8,128)}, f32[128,256]{1,0:T(8,128)}, f32[1,1]{1,0:T(1,128)}) custom-call(bf16[128,256]{1,0:T(8,128)(2,1)S(1)} %get-tuple-element.19.q_ref, bf16[128,256]{1,0:T(8,128)(2,1)S(1)} %get-tuple-element.20.v_ref, f32[128,256]{1,0:T(8,128)S(1)} %own.1.own_ref, f32[136,256]{1,0:T(8,128)S(1)} %give.1.give_ref, ...), custom_call_target="tpu_custom_call" | custom-call | tf_op jit(solution)/shard_map/final/pallas_call | solution.py:450
  (2 shorter events, 0.1 us)
Async XLA Ops:
  0.6 2.7 %collective-permute-start = (bf16[128,256]{1,0:T(8,128)(2,1)}, bf16[128,256]{1,0:T(8,128)(2,1)S(1)}, u32[]{:S(2)}, u32[]{:S(2)}) collective-permute-start(bf16[128,256]{1,0:T(8,128)(2,1)} %q_hbm.1), channel_id=1, source_target_pairs={{0,64},{64,0},{1,65},{65,1},{2,66},{66,2},{3,67},{67,3},{4,68},{68... | collective-permute-start | bytes 196616 | tf_op jit(solution)/shard_map/ppermute | solution.py:66
  2.1 1.5 %collective-permute-start.1 = (bf16[128,256]{1,0:T(8,128)(2,1)}, bf16[128,256]{1,0:T(8,128)(2,1)S(1)}, u32[]{:S(2)}, u32[]{:S(2)}) collective-permute-start(bf16[128,256]{1,0:T(8,128)(2,1)} %v_hbm.1), channel_id=1, source_target_pairs={{0,64},{64,0},{1,65},{65,1},{2,66},{66,2},{3,67},{67,3},{4,68},{68... | collective-permute-start | bytes 196616 | tf_op jit(solution)/shard_map/ppermute | solution.py:66
  18.3 3.5 %collective-permute-start.2 = (bf16[8,128,256]{2,1,0:T(8,128)(2,1)S(1)}, bf16[8,128,256]{2,1,0:T(8,128)(2,1)S(1)}, u32[]{:S(2)}, u32[]{:S(2)}) collective-permute-start(bf16[8,128,256]{2,1,0:T(8,128)(2,1)S(1)} %half.1), channel_id=1, source_target_pairs={{0,64},{64,0},{1,65},{65,1},{2,66},{66,2},{3,67},{67,3},{4,68},{68... | collective-permute-start | bytes 1572872 | tf_op jit(solution)/shard_map/ppermute | solution.py:66
  20.3 2.3 %collective-permute-start.3 = (bf16[8,128,256]{2,1,0:T(8,128)(2,1)S(1)}, bf16[8,128,256]{2,1,0:T(8,128)(2,1)S(1)}, u32[]{:S(2)}, u32[]{:S(2)}) collective-permute-start(bf16[8,128,256]{2,1,0:T(8,128)(2,1)S(1)} %rest.1), channel_id=1, source_target_pairs={{0,64},{64,0},{1,65},{65,1},{2,66},{66,2},{3,67},{67,3},{4,68},{68... | collective-permute-start | bytes 1572872 | tf_op jit(solution)/shard_map/ppermute | solution.py:66
  32.6 2.6 %collective-permute-start.4 = (bf16[1040,256]{1,0:T(8,128)(2,1)S(1)}, bf16[1040,256]{1,0:T(8,128)(2,1)S(1)}, u32[]{:S(2)}, u32[]{:S(2)}) collective-permute-start(bf16[1040,256]{1,0:T(8,128)(2,1)S(1)} %first.1), channel_id=1, source_target_pairs={{0,64},{64,0},{1,65},{65,1},{2,66},{66,2},{3,67},{67,3},{4,68},{68... | collective-permute-start | bytes 1597448 | tf_op jit(solution)/shard_map/ppermute | solution.py:66
  33.9 2.0 %collective-permute-start.5 = (bf16[1024,256]{1,0:T(8,128)(2,1)S(1)}, bf16[1024,256]{1,0:T(8,128)(2,1)S(1)}, u32[]{:S(2)}, u32[]{:S(2)}) collective-permute-start(bf16[1024,256]{1,0:T(8,128)(2,1)S(1)} %get-tuple-element.31), channel_id=1, source_target_pairs={{0,64},{64,0},{1,65},{65,1},{2,66},{66,2},{3,67},{67,3},{4,68},{68... | collective-permute-start | bytes 1572872 | tf_op jit(solution)/shard_map/ppermute | solution.py:66
  50.3 1.4 %collective-permute-start.6 = (f32[136,256]{1,0:T(8,128)S(1)}, f32[136,256]{1,0:T(8,128)S(1)}, u32[]{:S(2)}, u32[]{:S(2)}) collective-permute-start(f32[136,256]{1,0:T(8,128)S(1)} %give.1.give_ref), channel_id=1, source_target_pairs={{0,64},{64,0},{1,65},{65,1},{2,66},{66,2},{3,67},{67,3},{4,68},{68... | collective-permute-start | bytes 417800 | tf_op jit(solution)/shard_map/ppermute | solution.py:66

commit v13 on v12

--- a/solution.py
+++ b/solution.py
@@ -283,7 +283,7 @@
     r = 1.0 / row_sums(s_ref)[:8]
 
     def item():
-        weigh(e0_ref, rows_of(got_a_ref), r, keeping(keep_ref), range(2))
+        weigh(e0_ref, rows_of(got_a_ref), r, keeping(keep_ref), range(1))
 
     def query():
         weigh(e1_ref, own_queries(block_ref), r, into(give_ref))
@@ -294,7 +294,7 @@
 def third_body(e0_ref, e1_ref, got_a_ref, got_b_ref, s_ref, keep0_ref, keep1_ref, u_ref):
     def item():
         r, q = 1.0 / row_sums(s_ref)[:8], rows_of(got_a_ref)
-        weigh(e0_ref, q, r, lambda k, w: keeping(keep0_ref)(k - 2, w), range(2, 4))
+        weigh(e0_ref, q, r, lambda k, w: keeping(keep0_ref)(k - 1, w), range(1, 4))
         weigh(e1_ref, q, r, keeping(keep1_ref))
 
     def query():
@@ -306,7 +306,7 @@
 def merge_body(keep0_ref, keep1_ref, u_ref, got_ref, s_ref, out_ref):
     def item():
         for k in range(4):
-            keep = keep0_ref[k] if k < 2 else keep1_ref[k - 2]
+            keep = keep0_ref[k] if k < 1 else keep1_ref[k - 1]
             got = got_ref[k * 256 : (k + 1) * 256].astype(f32)
             out_ref[k, :256] = (keep + got).astype(bf16)
         sums = row_sums(s_ref)
@@ -434,11 +434,11 @@
     (give,) = call(first_body, [((1040, D), bf16)], "first", flops)(e0, e1, block, sums)
     got0 = swap_cores(give)
     keep0, give = call(
-        second_body, [((2, 256, D), f32), (pulled, bf16)], "second", flops
+        second_body, [((1, 256, D), f32), (pulled, bf16)], "second", flops
     )(e0, e1, block, got_a, sums)
     got1 = swap_cores(give)
     keep1, keep2, u = call(
-        third_body, [((2, 256, D), f32), ((4, 256, D), f32), (pulled, bf16)], "third", flops
+        third_body, [((3, 256, D), f32), ((4, 256, D), f32), (pulled, bf16)], "third", flops
     )(e0, e1, got_a, got_b, sums)
     packed = (GROUP, 264, D)
     (part,) = call(merge_body, [(packed, bf16)], "merge", flops)(keep0, keep1, u, got0, sums)

time: 53 us -> 52.9 us (level)
  no operation moved by 1% of the time
where the time goes in v13:
time: 52.9 us; the launch traced here: 52.7 us
  blocking collectives  36.7 us (69%)
  Pallas kernels  7.43 us (14%)
  starting transfers between devices  5.34 us (10%)
  waiting for transfers between devices  2.45 us (5%)
  between operations  0.75 us (1%)
    all_to_all x3, blocking collectives, exchange(): lax.all_to_all(pieces, AXES, 0, 0, tiled=True, axis_index_groups=groups)  36.7 us
    ppermute x7, starting transfers between devices, swap_cores(): return lax.ppermute(value, 'blk', [(0, 1), (1, 0)])  5.34 us
    ppermute x7, waiting for transfers between devices, swap_cores(): return lax.ppermute(value, 'blk', [(0, 1), (1, 0)])  2.45 us
    pallas_call x1, Pallas kernels, per_device(): call(first_body, [((1040, D), bf16)], 'first', flops)(e0, e1, block, sums)  1.28 us
    pallas_call x1, Pallas kernels, per_device(): call(norm_body, [(rows, bf16), ((8, 128), f32), (rows, bf16), (rows, bf16...  1.18 us
    pallas_call x1, Pallas kernels, per_device(): call(third_body, [((3, 256, D), f32), ((4, 256, D), f32), (pulled, bf16)]...  1.12 us
  transfers between devices with their start and end apart: 7, of which 4 were waited for; matrix products, arithmetic and copies ran while one was open for 0% of the time, Pallas kernels for 7%

profile of v13, /device:TPU:1, one launch (start us, length us, event | category | flops | bytes accessed | tf_op | source)
XLA Modules:
  0.0 52.7 jit_solution(4389659427835945125)
XLA Ops:
  0.6 1.4 %collective-permute-start = (bf16[128,256]{1,0:T(8,128)(2,1)}, bf16[128,256]{1,0:T(8,128)(2,1)S(1)}, u32[]{:S(2)}, u32[]{:S(2)}) collective-permute-start(bf16[128,256]{1,0:T(8,128)(2,1)} %q_hbm.1), channel_id=1, source_target_pairs={{0,64},{64,0},{1,65},{65,1},{2,66},{66,2},{3,67},{67,3},{4,68},{68... | collective-permute-start | bytes 196616 | tf_op jit(solution)/shard_map/ppermute | solution.py:66
  2.1 0.1 collective-permute-start.1
  2.2 1.2 %norm.1 = (bf16[128,256]{1,0:T(8,128)(2,1)S(1)}, f32[8,128]{1,0:T(8,128)S(1)}, bf16[128,256]{1,0:T(8,128)(2,1)S(1)}, bf16[128,256]{1,0:T(8,128)(2,1)S(1)}) custom-call(bf16[128,256]{1,0:T(8,128)(2,1)} %q_hbm.1, bf16[128,256]{1,0:T(8,128)(2,1)} %v_hbm.1), custom_call_target="tpu_custom_call" | custom-call | flops 1000000000 | tf_op jit(solution)/shard_map/norm/pallas_call | solution.py:411
  3.3 0.0 collective-permute-done.got_q_ref
  3.4 0.2 collective-permute-done.1.got_v_ref
  3.5 0.2 tile.1
  3.7 14.5 %all_to_all.15.block_ref = bf16[8,2,128,256]{3,2,1,0:T(8,128)(2,1)S(1)} all-to-all(bf16[8,2,128,256]{3,2,1,0:T(8,128)(2,1)S(1)} %tile.1), channel_id=1, replica_groups={{78,69,65,73,74,70,66,77},{75,71,67,79,64,68,72,76},{94,85,81,89,90,86,..., dimensions={0} | all-to-all | bytes 2097152 | tf_op jit(solution)/shard_map/all_to_all | solution.py:62
  18.3 1.9 %collective-permute-start.2 = (bf16[8,128,256]{2,1,0:T(8,128)(2,1)S(1)}, bf16[8,128,256]{2,1,0:T(8,128)(2,1)S(1)}, u32[]{:S(2)}, u32[]{:S(2)}) collective-permute-start(bf16[8,128,256]{2,1,0:T(8,128)(2,1)S(1)} %half.1), channel_id=1, source_target_pairs={{0,64},{64,0},{1,65},{65,1},{2,66},{66,2},{3,67},{67,3},{4,68},{68... | collective-permute-start | bytes 1572872 | tf_op jit(solution)/shard_map/ppermute | solution.py:66
  20.3 0.1 collective-permute-start.3
  20.4 1.4 %collective-permute-done.2.got_ref.got_a_ref = bf16[8,128,256]{2,1,0:T(8,128)(2,1)S(1)} collective-permute-done((bf16[8,128,256]{2,1,0:T(8,128)(2,1)S(1)}, bf16[8,128,256]{2,1,0:T(8,128)(2,1)S(1)}, u32[]{:S(2)}, u32[]{:S(2)}) %collective-permute-start.2) | collective-permute-done | bytes 524320 | tf_op jit(solution)/shard_map/ppermute | solution.py:66
  21.8 0.8 %score0.1 = (bf16[4,256,1024]{2,1,0:T(8,128)(2,1)S(1)}, f32[8,1024]{1,0:T(8,128)S(1)}) custom-call(bf16[8,2,128,256]{3,2,1,0:T(8,128)(2,1)S(1)} %all_to_all.15.block_ref, bf16[8,128,256]{2,1,0:T(8,128)(2,1)S(1)} %collective-permute-done.2.got_ref.got_a_ref), custom_call_target="tpu_custom_call" | custom-call | flops 1073741824 | tf_op jit(solution)/shard_map/score0/pallas_call | solution.py:428
  22.6 0.0 collective-permute-done.3.got_b_ref
  22.6 0.8 %score1.1 = (bf16[4,256,1024]{2,1,0:T(8,128)(2,1)S(1)}, f32[8,16,128]{2,1,0:T(8,128)S(1)}) custom-call(bf16[8,2,128,256]{3,2,1,0:T(8,128)(2,1)S(1)} %all_to_all.15.block_ref, bf16[8,128,256]{2,1,0:T(8,128)(2,1)S(1)} %collective-permute-done.2.got_ref.got_a_ref, bf16[8,128,256]{2,1,0:T(8,128)(2,1)S(1)} %collective-permute-done.3.got_b_ref, ...), custom_call_target="tpu_custom_call" | custom-call | flops 1073741824 | tf_op jit(solution)/shard_map/score1/pallas_call | solution.py:429
  23.4 7.9 %all_to_all.16.s_ref = f32[8,16,128]{2,1,0:T(8,128)S(1)} all-to-all(f32[8,16,128]{2,1,0:T(8,128)S(1)} %get-tuple-element.26), channel_id=1, replica_groups={{48,16,0,32,49,17,1,33},{50,18,2,34,51,19,3,35},{52,20,4,36,53,21,5,37}..., dimensions={0} | all-to-all | bytes 131072 | tf_op jit(solution)/shard_map/all_to_all | solution.py:62
  31.3 1.3 %first.1 = bf16[1040,256]{1,0:T(8,128)(2,1)S(1)} custom-call(bf16[4,256,1024]{2,1,0:T(8,128)(2,1)S(1)} %get-tuple-element.22.e0_ref, bf16[4,256,1024]{2,1,0:T(8,128)(2,1)S(1)} %get-tuple-element.25.e1_ref, bf16[8,2,128,256]{3,2,1,0:T(8,128)(2,1)S(1)} %all_to_all.15.block_ref, f32[8,16,128]{2,1,0:T(8,128)S(1)} %all_to_all.16.s_ref), custom_call_target="tpu_custom_call" | custom-call | flops 1073741824 | tf_op jit(solution)/shard_map/first/pallas_call | solution.py:434
  32.6 0.8 %collective-permute-start.4 = (bf16[1040,256]{1,0:T(8,128)(2,1)S(1)}, bf16[1040,256]{1,0:T(8,128)(2,1)S(1)}, u32[]{:S(2)}, u32[]{:S(2)}) collective-permute-start(bf16[1040,256]{1,0:T(8,128)(2,1)S(1)} %first.1), channel_id=1, source_target_pairs={{0,64},{64,0},{1,65},{65,1},{2,66},{66,2},{3,67},{67,3},{4,68},{68... | collective-permute-start | bytes 1597448 | tf_op jit(solution)/shard_map/ppermute | solution.py:66
  33.4 0.3 second.1
  33.7 0.5 collective-permute-start.5
  34.2 1.1 %third.1 = (f32[3,256,256]{2,1,0:T(8,128)S(1)}, f32[4,256,256]{2,1,0:T(8,128)S(1)}, bf16[1024,256]{1,0:T(8,128)(2,1)S(1)}) custom-call(bf16[4,256,1024]{2,1,0:T(8,128)(2,1)S(1)} %get-tuple-element.22.e0_ref, bf16[4,256,1024]{2,1,0:T(8,128)(2,1)S(1)} %get-tuple-element.25.e1_ref, bf16[8,128,256]{2,1,0:T(8,128)(2,1)S(1)} %collective-permute-done.2.got_ref.got_a_ref, ...), custom_call_target="tpu_custom_call" | custom-call | flops 1073741824 | tf_op jit(solution)/shard_map/third/pallas_call | solution.py:440
  35.4 0.0 collective-permute-done.4.got_ref
  35.4 0.2 merge.1.part_ref
  35.6 0.2 collective-permute-done.5.got_ref
  35.8 0.1 join.1
  35.9 14.3 %all_to_all.17.w_ref = bf16[8,264,256]{2,1,0:T(8,128)(2,1)S(1)} all-to-all(bf16[8,264,256]{2,1,0:T(8,128)(2,1)S(1)} %join.1), channel_id=1, replica_groups={{78,69,65,73,74,70,66,77},{75,71,67,79,64,68,72,76},{94,85,81,89,90,86,..., dimensions={0} | all-to-all | bytes 2162688 | tf_op jit(solution)/shard_map/all_to_all | solution.py:62
  50.2 0.1 give.1.give_ref
  50.3 0.4 collective-permute-start.6
  50.7 0.3 own.1.own_ref
  51.0 0.7 %collective-permute-done.6.got_ref = f32[136,256]{1,0:T(8,128)S(1)} collective-permute-done((f32[136,256]{1,0:T(8,128)S(1)}, f32[136,256]{1,0:T(8,128)S(1)}, u32[]{:S(2)}, u32[]{:S(2)}) %collective-permute-start.6) | collective-permute-done | bytes 139296 | tf_op jit(solution)/shard_map/ppermute | solution.py:66
  51.7 1.0 %final.1 = (f32[128,256]{1,0:T(8,128)}, f32[128,256]{1,0:T(8,128)}, f32[1,1]{1,0:T(1,128)}) custom-call(bf16[128,256]{1,0:T(8,128)(2,1)S(1)} %get-tuple-element.19.q_ref, bf16[128,256]{1,0:T(8,128)(2,1)S(1)} %get-tuple-element.20.v_ref, f32[128,256]{1,0:T(8,128)S(1)} %own.1.own_ref, f32[136,256]{1,0:T(8,128)S(1)} %give.1.give_ref, ...), custom_call_target="tpu_custom_call" | custom-call | tf_op jit(solution)/shard_map/final/pallas_call | solution.py:450
  (2 shorter events, 0.1 us)
Async XLA Ops:
  0.6 2.7 %collective-permute-start = (bf16[128,256]{1,0:T(8,128)(2,1)}, bf16[128,256]{1,0:T(8,128)(2,1)S(1)}, u32[]{:S(2)}, u32[]{:S(2)}) collective-permute-start(bf16[128,256]{1,0:T(8,128)(2,1)} %q_hbm.1), channel_id=1, source_target_pairs={{0,64},{64,0},{1,65},{65,1},{2,66},{66,2},{3,67},{67,3},{4,68},{68... | collective-permute-start | bytes 196616 | tf_op jit(solution)/shard_map/ppermute | solution.py:66
  2.1 1.5 %collective-permute-start.1 = (bf16[128,256]{1,0:T(8,128)(2,1)}, bf16[128,256]{1,0:T(8,128)(2,1)S(1)}, u32[]{:S(2)}, u32[]{:S(2)}) collective-permute-start(bf16[128,256]{1,0:T(8,128)(2,1)} %v_hbm.1), channel_id=1, source_target_pairs={{0,64},{64,0},{1,65},{65,1},{2,66},{66,2},{3,67},{67,3},{4,68},{68... | collective-permute-start | bytes 196616 | tf_op jit(solution)/shard_map/ppermute | solution.py:66
  18.3 3.5 %collective-permute-start.2 = (bf16[8,128,256]{2,1,0:T(8,128)(2,1)S(1)}, bf16[8,128,256]{2,1,0:T(8,128)(2,1)S(1)}, u32[]{:S(2)}, u32[]{:S(2)}) collective-permute-start(bf16[8,128,256]{2,1,0:T(8,128)(2,1)S(1)} %half.1), channel_id=1, source_target_pairs={{0,64},{64,0},{1,65},{65,1},{2,66},{66,2},{3,67},{67,3},{4,68},{68... | collective-permute-start | bytes 1572872 | tf_op jit(solution)/shard_map/ppermute | solution.py:66
  20.3 2.3 %collective-permute-start.3 = (bf16[8,128,256]{2,1,0:T(8,128)(2,1)S(1)}, bf16[8,128,256]{2,1,0:T(8,128)(2,1)S(1)}, u32[]{:S(2)}, u32[]{:S(2)}) collective-permute-start(bf16[8,128,256]{2,1,0:T(8,128)(2,1)S(1)} %rest.1), channel_id=1, source_target_pairs={{0,64},{64,0},{1,65},{65,1},{2,66},{66,2},{3,67},{67,3},{4,68},{68... | collective-permute-start | bytes 1572872 | tf_op jit(solution)/shard_map/ppermute | solution.py:66
  32.6 2.8 %collective-permute-start.4 = (bf16[1040,256]{1,0:T(8,128)(2,1)S(1)}, bf16[1040,256]{1,0:T(8,128)(2,1)S(1)}, u32[]{:S(2)}, u32[]{:S(2)}) collective-permute-start(bf16[1040,256]{1,0:T(8,128)(2,1)S(1)} %first.1), channel_id=1, source_target_pairs={{0,64},{64,0},{1,65},{65,1},{2,66},{66,2},{3,67},{67,3},{4,68},{68... | collective-permute-start | bytes 1597448 | tf_op jit(solution)/shard_map/ppermute | solution.py:66
  33.7 2.0 %collective-permute-start.5 = (bf16[1024,256]{1,0:T(8,128)(2,1)S(1)}, bf16[1024,256]{1,0:T(8,128)(2,1)S(1)}, u32[]{:S(2)}, u32[]{:S(2)}) collective-permute-start(bf16[1024,256]{1,0:T(8,128)(2,1)S(1)} %get-tuple-element.31), channel_id=1, source_target_pairs={{0,64},{64,0},{1,65},{65,1},{2,66},{66,2},{3,67},{67,3},{4,68},{68... | collective-permute-start | bytes 1572872 | tf_op jit(solution)/shard_map/ppermute | solution.py:66
  50.3 1.4 %collective-permute-start.6 = (f32[136,256]{1,0:T(8,128)S(1)}, f32[136,256]{1,0:T(8,128)S(1)}, u32[]{:S(2)}, u32[]{:S(2)}) collective-permute-start(f32[136,256]{1,0:T(8,128)S(1)} %give.1.give_ref), channel_id=1, source_target_pairs={{0,64},{64,0},{1,65},{65,1},{2,66},{66,2},{3,67},{67,3},{4,68},{68... | collective-permute-start | bytes 417800 | tf_op jit(solution)/shard_map/ppermute | solution.py:66

commit v14 on v12

--- a/solution.py
+++ b/solution.py
@@ -361,47 +361,51 @@
     return (grad - direction * along) / length
 
 
-def query_slope(u, q_ref, v_ref, s_ref):
-    q, q_len = unit(q_ref[...])
+def query_pull(u, s_ref):
     sums = row_sums(s_ref)[:8]
     mine = lax.broadcasted_iota(jnp.int32, sums.shape, 0) == query_index()
     own = jnp.sum(jnp.where(mine, sums, 0.0), axis=0, keepdims=True)
-    u = jnp.concatenate([(u[:, :128] / own).T, (u[:, 128:] / own).T], axis=1)
-    return slope(u, hat(v_ref[...]).astype(f32), q, q_len)
-
-
-def item_slope(w, q_ref, v_ref):
+    return jnp.concatenate([(u[:, :128] / own).T, (u[:, 128:] / own).T], axis=1)
+
+
+def own_body(w_ref, q_ref, v_ref, s_ref, own_ref, direction_ref, hat_ref, length_ref):
+    core = lax.axis_index("blk")
+    own = summed(w_ref, pl.multiple_of(core * 128, 128), 128)
+    q, q_len = unit(q_ref[...])
     v, v_len = unit(v_ref[...])
-    return slope(w, hat(q_ref[...]).astype(f32), v, v_len)
-
-
-def own_body(w_ref, q_ref, v_ref, s_ref, own_ref):
-    core = lax.axis_index("blk")
-    own = summed(w_ref, pl.multiple_of(core * 128, 128), 128)
-
-    @pl.when(core == ITEM)
-    def _():
-        own_ref[...] = item_slope(own, q_ref, v_ref)
-
-    @pl.when(core != ITEM)
-    def _():
-        own_ref[...] = query_slope(own, q_ref, v_ref, s_ref)
-
-
-def final_body(q_ref, v_ref, own_ref, give_ref, got_ref, s_ref, qs_ref, vs_ref, loss_ref):
-    core = lax.axis_index("blk")
-
-    @pl.when(core == ITEM)
-    def _():
+    q_hat, v_hat = q.astype(bf16).astype(f32), v.astype(bf16).astype(f32)
+
+    def leave(direction, other_hat, length):
+        direction_ref[...] = direction
+        hat_ref[...] = other_hat
+        length_ref[...] = jnp.broadcast_to(length, length_ref.shape)
+
+    def item():
+        own_ref[...] = slope(own, q_hat, v, v_len)
+        leave(q, v_hat, q_len)
+
+    def query():
+        own_ref[...] = slope(query_pull(own, s_ref), v_hat, q, q_len)
+        leave(v, q_hat, v_len)
+
+    by_role(item, query)
+
+
+def final_body(own_ref, direction_ref, hat_ref, length_ref, give_ref, got_ref, s_ref, qs_ref, vs_ref, loss_ref):
+    def other(pulled):
+        return slope(pulled, hat_ref[...], direction_ref[...], length_ref[...])
+
+    def item():
         vs_ref[...] = own_ref[...]
-        qs_ref[...] = query_slope(got_ref[:128], q_ref, v_ref, s_ref)
+        qs_ref[...] = other(query_pull(got_ref[:128], s_ref))
         loss_ref[0, 0] = jnp.max(give_ref[128:136]) / (128 * 128)
 
-    @pl.when(core != ITEM)
-    def _():
+    def query():
         qs_ref[...] = own_ref[...]
-        vs_ref[...] = item_slope(got_ref[:128], q_ref, v_ref)
+        vs_ref[...] = other(got_ref[:128])
         loss_ref[0, 0] = jnp.max(got_ref[128:136]) / (128 * 128)
+
+    by_role(item, query)
 
 
 def per_device(queries, items):
@@ -446,10 +450,10 @@
     out = exchange(out, BULK)
     (give,) = call(give_body, [((136, D), f32)], "give")(out)
     got = swap_cores(give)
-    (own,) = call(own_body, [(rows, f32)], "own", flops)(out, q_raw, v_raw, sums)
+    ready = call(own_body, [(rows, f32)] * 4, "own", flops)(out, q_raw, v_raw, sums)
     q_slope, v_slope, loss = call(
         final_body, [(rows, f32), (rows, f32), ((1, 1), f32, pltpu.SMEM)], "final"
-    )(q_raw, v_raw, own, give, got, sums)
+    )(*ready, give, got, sums)
     return loss.reshape(()), q_slope, v_slope
 
 

time: 53 us -> 53 us (level)
  transfers between devices with their start and end apart: 7 -> 7, of which waited for: 4 -> 4; matrix products, arithmetic and copies ran while one was open for 0% -> 0% of each run, Pallas kernels for 7% -> 8%
where the time goes in v14:
time: 53 us; the launch traced here: 52.7 us
  blocking collectives  36.7 us (69%)
  Pallas kernels  7.44 us (14%)
  starting transfers between devices  5.11 us (10%)
  waiting for transfers between devices  2.7 us (5%)
  between operations  0.75 us (1%)
    all_to_all x3, blocking collectives, exchange(): lax.all_to_all(pieces, AXES, 0, 0, tiled=True, axis_index_groups=groups)  36.7 us
    ppermute x7, starting transfers between devices, swap_cores(): return lax.ppermute(value, 'blk', [(0, 1), (1, 0)])  5.11 us
    ppermute x7, waiting for transfers between devices, swap_cores(): return lax.ppermute(value, 'blk', [(0, 1), (1, 0)])  2.7 us
    pallas_call x1, Pallas kernels, per_device(): call(first_body, [((1040, D), bf16)], 'first', flops)(e0, e1, block, sums)  1.28 us
    pallas_call x1, Pallas kernels, per_device(): call(norm_body, [(rows, bf16), ((8, 128), f32), (rows, bf16), (rows, bf16...  1.18 us
  transfers between devices with their start and end apart: 7, of which 4 were waited for; matrix products, arithmetic and copies ran while one was open for 0% of the time, Pallas kernels for 8%

profile of v14, /device:TPU:1, one launch (start us, length us, event | category | flops | bytes accessed | tf_op | source)
XLA Modules:
  0.0 52.7 jit_solution(4061599357282766610)
XLA Ops:
  0.6 1.4 %collective-permute-start = (bf16[128,256]{1,0:T(8,128)(2,1)}, bf16[128,256]{1,0:T(8,128)(2,1)S(1)}, u32[]{:S(2)}, u32[]{:S(2)}) collective-permute-start(bf16[128,256]{1,0:T(8,128)(2,1)} %q_hbm.1), channel_id=1, source_target_pairs={{0,64},{64,0},{1,65},{65,1},{2,66},{66,2},{3,67},{67,3},{4,68},{68... | collective-permute-start | bytes 196616 | tf_op jit(solution)/shard_map/ppermute | solution.py:66
  2.1 0.1 collective-permute-start.1
  2.2 1.2 %norm.1 = (bf16[128,256]{1,0:T(8,128)(2,1)S(1)}, f32[8,128]{1,0:T(8,128)S(1)}, bf16[128,256]{1,0:T(8,128)(2,1)S(1)}, bf16[128,256]{1,0:T(8,128)(2,1)S(1)}) custom-call(bf16[128,256]{1,0:T(8,128)(2,1)} %q_hbm.1, bf16[128,256]{1,0:T(8,128)(2,1)} %v_hbm.1), custom_call_target="tpu_custom_call" | custom-call | flops 1000000000 | tf_op jit(solution)/shard_map/norm/pallas_call | solution.py:415
  3.3 0.0 collective-permute-done.got_q_ref
  3.4 0.2 collective-permute-done.1.got_v_ref
  3.5 0.2 tile.1
  3.7 14.5 %all_to_all.15.block_ref = bf16[8,2,128,256]{3,2,1,0:T(8,128)(2,1)S(1)} all-to-all(bf16[8,2,128,256]{3,2,1,0:T(8,128)(2,1)S(1)} %tile.1), channel_id=1, replica_groups={{78,69,65,73,74,70,66,77},{75,71,67,79,64,68,72,76},{94,85,81,89,90,86,..., dimensions={0} | all-to-all | bytes 2097152 | tf_op jit(solution)/shard_map/all_to_all | solution.py:62
  18.3 1.9 %collective-permute-start.2 = (bf16[8,128,256]{2,1,0:T(8,128)(2,1)S(1)}, bf16[8,128,256]{2,1,0:T(8,128)(2,1)S(1)}, u32[]{:S(2)}, u32[]{:S(2)}) collective-permute-start(bf16[8,128,256]{2,1,0:T(8,128)(2,1)S(1)} %half.1), channel_id=1, source_target_pairs={{0,64},{64,0},{1,65},{65,1},{2,66},{66,2},{3,67},{67,3},{4,68},{68... | collective-permute-start | bytes 1572872 | tf_op jit(solution)/shard_map/ppermute | solution.py:66
  20.3 0.1 collective-permute-start.3
  20.4 1.4 %collective-permute-done.2.got_ref.got_a_ref = bf16[8,128,256]{2,1,0:T(8,128)(2,1)S(1)} collective-permute-done((bf16[8,128,256]{2,1,0:T(8,128)(2,1)S(1)}, bf16[8,128,256]{2,1,0:T(8,128)(2,1)S(1)}, u32[]{:S(2)}, u32[]{:S(2)}) %collective-permute-start.2) | collective-permute-done | bytes 524320 | tf_op jit(solution)/shard_map/ppermute | solution.py:66
  21.8 0.8 %score0.1 = (bf16[4,256,1024]{2,1,0:T(8,128)(2,1)S(1)}, f32[8,1024]{1,0:T(8,128)S(1)}) custom-call(bf16[8,2,128,256]{3,2,1,0:T(8,128)(2,1)S(1)} %all_to_all.15.block_ref, bf16[8,128,256]{2,1,0:T(8,128)(2,1)S(1)} %collective-permute-done.2.got_ref.got_a_ref), custom_call_target="tpu_custom_call" | custom-call | flops 1073741824 | tf_op jit(solution)/shard_map/score0/pallas_call | solution.py:432
  22.6 0.0 collective-permute-done.3.got_b_ref
  22.6 0.8 %score1.1 = (bf16[4,256,1024]{2,1,0:T(8,128)(2,1)S(1)}, f32[8,16,128]{2,1,0:T(8,128)S(1)}) custom-call(bf16[8,2,128,256]{3,2,1,0:T(8,128)(2,1)S(1)} %all_to_all.15.block_ref, bf16[8,128,256]{2,1,0:T(8,128)(2,1)S(1)} %collective-permute-done.2.got_ref.got_a_ref, bf16[8,128,256]{2,1,0:T(8,128)(2,1)S(1)} %collective-permute-done.3.got_b_ref, ...), custom_call_target="tpu_custom_call" | custom-call | flops 1073741824 | tf_op jit(solution)/shard_map/score1/pallas_call | solution.py:433
  23.4 7.9 %all_to_all.16.s_ref = f32[8,16,128]{2,1,0:T(8,128)S(1)} all-to-all(f32[8,16,128]{2,1,0:T(8,128)S(1)} %get-tuple-element.28), channel_id=1, replica_groups={{48,16,0,32,49,17,1,33},{50,18,2,34,51,19,3,35},{52,20,4,36,53,21,5,37}..., dimensions={0} | all-to-all | bytes 131072 | tf_op jit(solution)/shard_map/all_to_all | solution.py:62
  31.3 1.3 %first.1 = bf16[1040,256]{1,0:T(8,128)(2,1)S(1)} custom-call(bf16[4,256,1024]{2,1,0:T(8,128)(2,1)S(1)} %get-tuple-element.24.e0_ref, bf16[4,256,1024]{2,1,0:T(8,128)(2,1)S(1)} %get-tuple-element.27.e1_ref, bf16[8,2,128,256]{3,2,1,0:T(8,128)(2,1)S(1)} %all_to_all.15.block_ref, f32[8,16,128]{2,1,0:T(8,128)S(1)} %all_to_all.16.s_ref), custom_call_target="tpu_custom_call" | custom-call | flops 1073741824 | tf_op jit(solution)/shard_map/first/pallas_call | solution.py:438
  32.6 0.8 %collective-permute-start.4 = (bf16[1040,256]{1,0:T(8,128)(2,1)S(1)}, bf16[1040,256]{1,0:T(8,128)(2,1)S(1)}, u32[]{:S(2)}, u32[]{:S(2)}) collective-permute-start(bf16[1040,256]{1,0:T(8,128)(2,1)S(1)} %first.1), channel_id=1, source_target_pairs={{0,64},{64,0},{1,65},{65,1},{2,66},{66,2},{3,67},{67,3},{4,68},{68... | collective-permute-start | bytes 1597448 | tf_op jit(solution)/shard_map/ppermute | solution.py:66
  33.4 0.5 second.1
  33.9 0.4 collective-permute-start.5
  34.2 1.0 %third.1 = (f32[2,256,256]{2,1,0:T(8,128)S(1)}, f32[4,256,256]{2,1,0:T(8,128)S(1)}, bf16[1024,256]{1,0:T(8,128)(2,1)S(1)}) custom-call(bf16[4,256,1024]{2,1,0:T(8,128)(2,1)S(1)} %get-tuple-element.24.e0_ref, bf16[4,256,1024]{2,1,0:T(8,128)(2,1)S(1)} %get-tuple-element.27.e1_ref, bf16[8,128,256]{2,1,0:T(8,128)(2,1)S(1)} %collective-permute-done.2.got_ref.got_a_ref, ...), custom_call_target="tpu_custom_call" | custom-call | flops 1073741824 | tf_op jit(solution)/shard_map/third/pallas_call | solution.py:444
  35.2 0.0 collective-permute-done.4.got_ref
  35.3 0.2 merge.1.part_ref
  35.5 0.4 collective-permute-done.5.got_ref
  35.9 0.1 join.1
  36.0 14.3 %all_to_all.17.w_ref = bf16[8,264,256]{2,1,0:T(8,128)(2,1)S(1)} all-to-all(bf16[8,264,256]{2,1,0:T(8,128)(2,1)S(1)} %join.1), channel_id=1, replica_groups={{78,69,65,73,74,70,66,77},{75,71,67,79,64,68,72,76},{94,85,81,89,90,86,..., dimensions={0} | all-to-all | bytes 2162688 | tf_op jit(solution)/shard_map/all_to_all | solution.py:62
  50.3 0.1 give.1.give_ref
  50.3 0.4 collective-permute-start.6
  50.7 0.4 own.1
  51.1 0.7 %collective-permute-done.6.got_ref = f32[136,256]{1,0:T(8,128)S(1)} collective-permute-done((f32[136,256]{1,0:T(8,128)S(1)}, f32[136,256]{1,0:T(8,128)S(1)}, u32[]{:S(2)}, u32[]{:S(2)}) %collective-permute-start.6) | collective-permute-done | bytes 139296 | tf_op jit(solution)/shard_map/ppermute | solution.py:66
  51.8 0.9 %final.1 = (f32[128,256]{1,0:T(8,128)}, f32[128,256]{1,0:T(8,128)}, f32[1,1]{1,0:T(1,128)}) custom-call(f32[128,256]{1,0:T(8,128)S(1)} %get-tuple-element.36.own_ref, f32[128,256]{1,0:T(8,128)S(1)} %get-tuple-element.37.direction_ref, f32[128,256]{1,0:T(8,128)S(1)} %get-tuple-element.38.hat_ref, f32[128,256]{1,0:T(8,128)S(1)} %get-tuple-element.39.length_ref, ...), custom_call_target="tpu_custom_call" | custom-call | tf_op jit(solution)/shard_map/final/pallas_call | solution.py:454
  (2 shorter events, 0.1 us)
Async XLA Ops:
  0.6 2.7 %collective-permute-start = (bf16[128,256]{1,0:T(8,128)(2,1)}, bf16[128,256]{1,0:T(8,128)(2,1)S(1)}, u32[]{:S(2)}, u32[]{:S(2)}) collective-permute-start(bf16[128,256]{1,0:T(8,128)(2,1)} %q_hbm.1), channel_id=1, source_target_pairs={{0,64},{64,0},{1,65},{65,1},{2,66},{66,2},{3,67},{67,3},{4,68},{68... | collective-permute-start | bytes 196616 | tf_op jit(solution)/shard_map/ppermute | solution.py:66
  2.1 1.5 %collective-permute-start.1 = (bf16[128,256]{1,0:T(8,128)(2,1)}, bf16[128,256]{1,0:T(8,128)(2,1)S(1)}, u32[]{:S(2)}, u32[]{:S(2)}) collective-permute-start(bf16[128,256]{1,0:T(8,128)(2,1)} %v_hbm.1), channel_id=1, source_target_pairs={{0,64},{64,0},{1,65},{65,1},{2,66},{66,2},{3,67},{67,3},{4,68},{68... | collective-permute-start | bytes 196616 | tf_op jit(solution)/shard_map/ppermute | solution.py:66
  18.3 3.5 %collective-permute-start.2 = (bf16[8,128,256]{2,1,0:T(8,128)(2,1)S(1)}, bf16[8,128,256]{2,1,0:T(8,128)(2,1)S(1)}, u32[]{:S(2)}, u32[]{:S(2)}) collective-permute-start(bf16[8,128,256]{2,1,0:T(8,128)(2,1)S(1)} %half.1), channel_id=1, source_target_pairs={{0,64},{64,0},{1,65},{65,1},{2,66},{66,2},{3,67},{67,3},{4,68},{68... | collective-permute-start | bytes 1572872 | tf_op jit(solution)/shard_map/ppermute | solution.py:66
  20.3 2.3 %collective-permute-start.3 = (bf16[8,128,256]{2,1,0:T(8,128)(2,1)S(1)}, bf16[8,128,256]{2,1,0:T(8,128)(2,1)S(1)}, u32[]{:S(2)}, u32[]{:S(2)}) collective-permute-start(bf16[8,128,256]{2,1,0:T(8,128)(2,1)S(1)} %rest.1), channel_id=1, source_target_pairs={{0,64},{64,0},{1,65},{65,1},{2,66},{66,2},{3,67},{67,3},{4,68},{68... | collective-permute-start | bytes 1572872 | tf_op jit(solution)/shard_map/ppermute | solution.py:66
  32.6 2.6 %collective-permute-start.4 = (bf16[1040,256]{1,0:T(8,128)(2,1)S(1)}, bf16[1040,256]{1,0:T(8,128)(2,1)S(1)}, u32[]{:S(2)}, u32[]{:S(2)}) collective-permute-start(bf16[1040,256]{1,0:T(8,128)(2,1)S(1)} %first.1), channel_id=1, source_target_pairs={{0,64},{64,0},{1,65},{65,1},{2,66},{66,2},{3,67},{67,3},{4,68},{68... | collective-permute-start | bytes 1597448 | tf_op jit(solution)/shard_map/ppermute | solution.py:66
  33.9 2.0 %collective-permute-start.5 = (bf16[1024,256]{1,0:T(8,128)(2,1)S(1)}, bf16[1024,256]{1,0:T(8,128)(2,1)S(1)}, u32[]{:S(2)}, u32[]{:S(2)}) collective-permute-start(bf16[1024,256]{1,0:T(8,128)(2,1)S(1)} %get-tuple-element.33), channel_id=1, source_target_pairs={{0,64},{64,0},{1,65},{65,1},{2,66},{66,2},{3,67},{67,3},{4,68},{68... | collective-permute-start | bytes 1572872 | tf_op jit(solution)/shard_map/ppermute | solution.py:66
  50.3 1.4 %collective-permute-start.6 = (f32[136,256]{1,0:T(8,128)S(1)}, f32[136,256]{1,0:T(8,128)S(1)}, u32[]{:S(2)}, u32[]{:S(2)}) collective-permute-start(f32[136,256]{1,0:T(8,128)S(1)} %give.1.give_ref), channel_id=1, source_target_pairs={{0,64},{64,0},{1,65},{65,1},{2,66},{66,2},{3,67},{67,3},{4,68},{68... | collective-permute-start | bytes 417800 | tf_op jit(solution)/shard_map/ppermute | solution.py:66

commit v15 on v14

--- a/solution.py
+++ b/solution.py
@@ -361,16 +361,21 @@
     return (grad - direction * along) / length
 
 
-def query_pull(u, s_ref):
+def own_share(s_ref):
     sums = row_sums(s_ref)[:8]
     mine = lax.broadcasted_iota(jnp.int32, sums.shape, 0) == query_index()
-    own = jnp.sum(jnp.where(mine, sums, 0.0), axis=0, keepdims=True)
-    return jnp.concatenate([(u[:, :128] / own).T, (u[:, 128:] / own).T], axis=1)
-
-
-def own_body(w_ref, q_ref, v_ref, s_ref, own_ref, direction_ref, hat_ref, length_ref):
+    return 1.0 / jnp.sum(jnp.where(mine, sums, 0.0), axis=0, keepdims=True)
+
+
+def query_pull(u, share):
+    return jnp.concatenate([(u[:, :128] * share).T, (u[:, 128:] * share).T], axis=1)
+
+
+def own_body(w_ref, q_ref, v_ref, s_ref, own_ref, direction_ref, hat_ref, length_ref, share_ref):
     core = lax.axis_index("blk")
     own = summed(w_ref, pl.multiple_of(core * 128, 128), 128)
+    share = own_share(s_ref)
+    share_ref[...] = jnp.broadcast_to(share, share_ref.shape)
     q, q_len = unit(q_ref[...])
     v, v_len = unit(v_ref[...])
     q_hat, v_hat = q.astype(bf16).astype(f32), v.astype(bf16).astype(f32)
@@ -385,19 +390,19 @@
         leave(q, v_hat, q_len)
 
     def query():
-        own_ref[...] = slope(query_pull(own, s_ref), v_hat, q, q_len)
+        own_ref[...] = slope(query_pull(own, share), v_hat, q, q_len)
         leave(v, q_hat, v_len)
 
     by_role(item, query)
 
 
-def final_body(own_ref, direction_ref, hat_ref, length_ref, give_ref, got_ref, s_ref, qs_ref, vs_ref, loss_ref):
+def final_body(own_ref, direction_ref, hat_ref, length_ref, share_ref, give_ref, got_ref, qs_ref, vs_ref, loss_ref):
     def other(pulled):
         return slope(pulled, hat_ref[...], direction_ref[...], length_ref[...])
 
     def item():
         vs_ref[...] = own_ref[...]
-        qs_ref[...] = other(query_pull(got_ref[:128], s_ref))
+        qs_ref[...] = other(query_pull(got_ref[:128], share_ref[:1]))
         loss_ref[0, 0] = jnp.max(give_ref[128:136]) / (128 * 128)
 
     def query():
@@ -450,10 +455,10 @@
     out = exchange(out, BULK)
     (give,) = call(give_body, [((136, D), f32)], "give")(out)
     got = swap_cores(give)
-    ready = call(own_body, [(rows, f32)] * 4, "own", flops)(out, q_raw, v_raw, sums)
+    ready = call(own_body, [(rows, f32)] * 4 + [((8, 128), f32)], "own", flops)(out, q_raw, v_raw, sums)
     q_slope, v_slope, loss = call(
         final_body, [(rows, f32), (rows, f32), ((1, 1), f32, pltpu.SMEM)], "final"
-    )(*ready, give, got, sums)
+    )(*ready, give, got)
     return loss.reshape(()), q_slope, v_slope
 
 

time: 53 us -> 53 us (level)
  no operation moved by 1% of the time
where the time goes in v15:
time: 53 us; the launch traced here: 52.7 us
  blocking collectives  36.7 us (69%)
  Pallas kernels  7.43 us (14%)
  starting transfers between devices  5.11 us (10%)
  waiting for transfers between devices  2.69 us (5%)
  between operations  0.75 us (1%)
    all_to_all x3, blocking collectives, exchange(): lax.all_to_all(pieces, AXES, 0, 0, tiled=True, axis_index_groups=groups)  36.7 us
    ppermute x7, starting transfers between devices, swap_cores(): return lax.ppermute(value, 'blk', [(0, 1), (1, 0)])  5.11 us
    ppermute x7, waiting for transfers between devices, swap_cores(): return lax.ppermute(value, 'blk', [(0, 1), (1, 0)])  2.69 us
    pallas_call x1, Pallas kernels, per_device(): call(first_body, [((1040, D), bf16)], 'first', flops)(e0, e1, block, sums)  1.28 us
    pallas_call x1, Pallas kernels, per_device(): call(norm_body, [(rows, bf16), ((8, 128), f32), (rows, bf16), (rows, bf16...  1.18 us
  transfers between devices with their start and end apart: 7, of which 4 were waited for; matrix products, arithmetic and copies ran while one was open for 0% of the time, Pallas kernels for 8%

profile of v15, /device:TPU:1, one launch (start us, length us, event | category | flops | bytes accessed | tf_op | source)
XLA Modules:
  0.0 52.7 jit_solution(16012366445318046712)
XLA Ops:
  0.6 1.4 %collective-permute-start = (bf16[128,256]{1,0:T(8,128)(2,1)}, bf16[128,256]{1,0:T(8,128)(2,1)S(1)}, u32[]{:S(2)}, u32[]{:S(2)}) collective-permute-start(bf16[128,256]{1,0:T(8,128)(2,1)} %q_hbm.1), channel_id=1, source_target_pairs={{0,64},{64,0},{1,65},{65,1},{2,66},{66,2},{3,67},{67,3},{4,68},{68... | collective-permute-start | bytes 196616 | tf_op jit(solution)/shard_map/ppermute | solution.py:66
  2.1 0.1 collective-permute-start.1
  2.2 1.2 %norm.1 = (bf16[128,256]{1,0:T(8,128)(2,1)S(1)}, f32[8,128]{1,0:T(8,128)S(1)}, bf16[128,256]{1,0:T(8,128)(2,1)S(1)}, bf16[128,256]{1,0:T(8,128)(2,1)S(1)}) custom-call(bf16[128,256]{1,0:T(8,128)(2,1)} %q_hbm.1, bf16[128,256]{1,0:T(8,128)(2,1)} %v_hbm.1), custom_call_target="tpu_custom_call" | custom-call | flops 1000000000 | tf_op jit(solution)/shard_map/norm/pallas_call | solution.py:420
  3.3 0.0 collective-permute-done.got_q_ref
  3.4 0.2 collective-permute-done.1.got_v_ref
  3.5 0.2 tile.1
  3.7 14.5 %all_to_all.15.block_ref = bf16[8,2,128,256]{3,2,1,0:T(8,128)(2,1)S(1)} all-to-all(bf16[8,2,128,256]{3,2,1,0:T(8,128)(2,1)S(1)} %tile.1), channel_id=1, replica_groups={{78,69,65,73,74,70,66,77},{75,71,67,79,64,68,72,76},{94,85,81,89,90,86,..., dimensions={0} | all-to-all | bytes 2097152 | tf_op jit(solution)/shard_map/all_to_all | solution.py:62
  18.3 1.9 %collective-permute-start.2 = (bf16[8,128,256]{2,1,0:T(8,128)(2,1)S(1)}, bf16[8,128,256]{2,1,0:T(8,128)(2,1)S(1)}, u32[]{:S(2)}, u32[]{:S(2)}) collective-permute-start(bf16[8,128,256]{2,1,0:T(8,128)(2,1)S(1)} %half.1), channel_id=1, source_target_pairs={{0,64},{64,0},{1,65},{65,1},{2,66},{66,2},{3,67},{67,3},{4,68},{68... | collective-permute-start | bytes 1572872 | tf_op jit(solution)/shard_map/ppermute | solution.py:66
  20.3 0.1 collective-permute-start.3
  20.4 1.4 %collective-permute-done.2.got_ref.got_a_ref = bf16[8,128,256]{2,1,0:T(8,128)(2,1)S(1)} collective-permute-done((bf16[8,128,256]{2,1,0:T(8,128)(2,1)S(1)}, bf16[8,128,256]{2,1,0:T(8,128)(2,1)S(1)}, u32[]{:S(2)}, u32[]{:S(2)}) %collective-permute-start.2) | collective-permute-done | bytes 524320 | tf_op jit(solution)/shard_map/ppermute | solution.py:66
  21.8 0.8 %score0.1 = (bf16[4,256,1024]{2,1,0:T(8,128)(2,1)S(1)}, f32[8,1024]{1,0:T(8,128)S(1)}) custom-call(bf16[8,2,128,256]{3,2,1,0:T(8,128)(2,1)S(1)} %all_to_all.15.block_ref, bf16[8,128,256]{2,1,0:T(8,128)(2,1)S(1)} %collective-permute-done.2.got_ref.got_a_ref), custom_call_target="tpu_custom_call" | custom-call | flops 1073741824 | tf_op jit(solution)/shard_map/score0/pallas_call | solution.py:437
  22.6 0.0 collective-permute-done.3.got_b_ref
  22.6 0.8 %score1.1 = (bf16[4,256,1024]{2,1,0:T(8,128)(2,1)S(1)}, f32[8,16,128]{2,1,0:T(8,128)S(1)}) custom-call(bf16[8,2,128,256]{3,2,1,0:T(8,128)(2,1)S(1)} %all_to_all.15.block_ref, bf16[8,128,256]{2,1,0:T(8,128)(2,1)S(1)} %collective-permute-done.2.got_ref.got_a_ref, bf16[8,128,256]{2,1,0:T(8,128)(2,1)S(1)} %collective-permute-done.3.got_b_ref, ...), custom_call_target="tpu_custom_call" | custom-call | flops 1073741824 | tf_op jit(solution)/shard_map/score1/pallas_call | solution.py:438
  23.4 7.9 %all_to_all.16.s_ref = f32[8,16,128]{2,1,0:T(8,128)S(1)} all-to-all(f32[8,16,128]{2,1,0:T(8,128)S(1)} %get-tuple-element.29), channel_id=1, replica_groups={{48,16,0,32,49,17,1,33},{50,18,2,34,51,19,3,35},{52,20,4,36,53,21,5,37}..., dimensions={0} | all-to-all | bytes 131072 | tf_op jit(solution)/shard_map/all_to_all | solution.py:62
  31.3 1.3 %first.1 = bf16[1040,256]{1,0:T(8,128)(2,1)S(1)} custom-call(bf16[4,256,1024]{2,1,0:T(8,128)(2,1)S(1)} %get-tuple-element.25.e0_ref, bf16[4,256,1024]{2,1,0:T(8,128)(2,1)S(1)} %get-tuple-element.28.e1_ref, bf16[8,2,128,256]{3,2,1,0:T(8,128)(2,1)S(1)} %all_to_all.15.block_ref, f32[8,16,128]{2,1,0:T(8,128)S(1)} %all_to_all.16.s_ref), custom_call_target="tpu_custom_call" | custom-call | flops 1073741824 | tf_op jit(solution)/shard_map/first/pallas_call | solution.py:443
  32.6 0.8 %collective-permute-start.4 = (bf16[1040,256]{1,0:T(8,128)(2,1)S(1)}, bf16[1040,256]{1,0:T(8,128)(2,1)S(1)}, u32[]{:S(2)}, u32[]{:S(2)}) collective-permute-start(bf16[1040,256]{1,0:T(8,128)(2,1)S(1)} %first.1), channel_id=1, source_target_pairs={{0,64},{64,0},{1,65},{65,1},{2,66},{66,2},{3,67},{67,3},{4,68},{68... | collective-permute-start | bytes 1597448 | tf_op jit(solution)/shard_map/ppermute | solution.py:66
  33.4 0.5 second.1
  33.9 0.4 collective-permute-start.5
  34.2 1.0 %third.1 = (f32[2,256,256]{2,1,0:T(8,128)S(1)}, f32[4,256,256]{2,1,0:T(8,128)S(1)}, bf16[1024,256]{1,0:T(8,128)(2,1)S(1)}) custom-call(bf16[4,256,1024]{2,1,0:T(8,128)(2,1)S(1)} %get-tuple-element.25.e0_ref, bf16[4,256,1024]{2,1,0:T(8,128)(2,1)S(1)} %get-tuple-element.28.e1_ref, bf16[8,128,256]{2,1,0:T(8,128)(2,1)S(1)} %collective-permute-done.2.got_ref.got_a_ref, ...), custom_call_target="tpu_custom_call" | custom-call | flops 1073741824 | tf_op jit(solution)/shard_map/third/pallas_call | solution.py:449
  35.2 0.0 collective-permute-done.4.got_ref
  35.3 0.2 merge.1.part_ref
  35.5 0.4 collective-permute-done.5.got_ref
  35.9 0.1 join.1
  36.0 14.3 %all_to_all.17.w_ref = bf16[8,264,256]{2,1,0:T(8,128)(2,1)S(1)} all-to-all(bf16[8,264,256]{2,1,0:T(8,128)(2,1)S(1)} %join.1), channel_id=1, replica_groups={{78,69,65,73,74,70,66,77},{75,71,67,79,64,68,72,76},{94,85,81,89,90,86,..., dimensions={0} | all-to-all | bytes 2162688 | tf_op jit(solution)/shard_map/all_to_all | solution.py:62
  50.3 0.1 give.1.give_ref
  50.3 0.4 collective-permute-start.6
  50.7 0.4 own.1
  51.1 0.7 %collective-permute-done.6.got_ref = f32[136,256]{1,0:T(8,128)S(1)} collective-permute-done((f32[136,256]{1,0:T(8,128)S(1)}, f32[136,256]{1,0:T(8,128)S(1)}, u32[]{:S(2)}, u32[]{:S(2)}) %collective-permute-start.6) | collective-permute-done | bytes 139296 | tf_op jit(solution)/shard_map/ppermute | solution.py:66
  51.8 0.9 %final.1 = (f32[128,256]{1,0:T(8,128)}, f32[128,256]{1,0:T(8,128)}, f32[1,1]{1,0:T(1,128)}) custom-call(f32[128,256]{1,0:T(8,128)S(1)} %get-tuple-element.37.own_ref, f32[128,256]{1,0:T(8,128)S(1)} %get-tuple-element.38.direction_ref, f32[128,256]{1,0:T(8,128)S(1)} %get-tuple-element.39.hat_ref, f32[128,256]{1,0:T(8,128)S(1)} %get-tuple-element.40.length_ref, ...), custom_call_target="tpu_custom_call" | custom-call | tf_op jit(solution)/shard_map/final/pallas_call | solution.py:459
  (2 shorter events, 0.1 us)
Async XLA Ops:
  0.6 2.7 %collective-permute-start = (bf16[128,256]{1,0:T(8,128)(2,1)}, bf16[128,256]{1,0:T(8,128)(2,1)S(1)}, u32[]{:S(2)}, u32[]{:S(2)}) collective-permute-start(bf16[128,256]{1,0:T(8,128)(2,1)} %q_hbm.1), channel_id=1, source_target_pairs={{0,64},{64,0},{1,65},{65,1},{2,66},{66,2},{3,67},{67,3},{4,68},{68... | collective-permute-start | bytes 196616 | tf_op jit(solution)/shard_map/ppermute | solution.py:66
  2.1 1.5 %collective-permute-start.1 = (bf16[128,256]{1,0:T(8,128)(2,1)}, bf16[128,256]{1,0:T(8,128)(2,1)S(1)}, u32[]{:S(2)}, u32[]{:S(2)}) collective-permute-start(bf16[128,256]{1,0:T(8,128)(2,1)} %v_hbm.1), channel_id=1, source_target_pairs={{0,64},{64,0},{1,65},{65,1},{2,66},{66,2},{3,67},{67,3},{4,68},{68... | collective-permute-start | bytes 196616 | tf_op jit(solution)/shard_map/ppermute | solution.py:66
  18.3 3.5 %collective-permute-start.2 = (bf16[8,128,256]{2,1,0:T(8,128)(2,1)S(1)}, bf16[8,128,256]{2,1,0:T(8,128)(2,1)S(1)}, u32[]{:S(2)}, u32[]{:S(2)}) collective-permute-start(bf16[8,128,256]{2,1,0:T(8,128)(2,1)S(1)} %half.1), channel_id=1, source_target_pairs={{0,64},{64,0},{1,65},{65,1},{2,66},{66,2},{3,67},{67,3},{4,68},{68... | collective-permute-start | bytes 1572872 | tf_op jit(solution)/shard_map/ppermute | solution.py:66
  20.3 2.3 %collective-permute-start.3 = (bf16[8,128,256]{2,1,0:T(8,128)(2,1)S(1)}, bf16[8,128,256]{2,1,0:T(8,128)(2,1)S(1)}, u32[]{:S(2)}, u32[]{:S(2)}) collective-permute-start(bf16[8,128,256]{2,1,0:T(8,128)(2,1)S(1)} %rest.1), channel_id=1, source_target_pairs={{0,64},{64,0},{1,65},{65,1},{2,66},{66,2},{3,67},{67,3},{4,68},{68... | collective-permute-start | bytes 1572872 | tf_op jit(solution)/shard_map/ppermute | solution.py:66
  32.6 2.6 %collective-permute-start.4 = (bf16[1040,256]{1,0:T(8,128)(2,1)S(1)}, bf16[1040,256]{1,0:T(8,128)(2,1)S(1)}, u32[]{:S(2)}, u32[]{:S(2)}) collective-permute-start(bf16[1040,256]{1,0:T(8,128)(2,1)S(1)} %first.1), channel_id=1, source_target_pairs={{0,64},{64,0},{1,65},{65,1},{2,66},{66,2},{3,67},{67,3},{4,68},{68... | collective-permute-start | bytes 1597448 | tf_op jit(solution)/shard_map/ppermute | solution.py:66
  33.9 2.0 %collective-permute-start.5 = (bf16[1024,256]{1,0:T(8,128)(2,1)S(1)}, bf16[1024,256]{1,0:T(8,128)(2,1)S(1)}, u32[]{:S(2)}, u32[]{:S(2)}) collective-permute-start(bf16[1024,256]{1,0:T(8,128)(2,1)S(1)} %get-tuple-element.34), channel_id=1, source_target_pairs={{0,64},{64,0},{1,65},{65,1},{2,66},{66,2},{3,67},{67,3},{4,68},{68... | collective-permute-start | bytes 1572872 | tf_op jit(solution)/shard_map/ppermute | solution.py:66
  50.3 1.4 %collective-permute-start.6 = (f32[136,256]{1,0:T(8,128)S(1)}, f32[136,256]{1,0:T(8,128)S(1)}, u32[]{:S(2)}, u32[]{:S(2)}) collective-permute-start(f32[136,256]{1,0:T(8,128)S(1)} %give.1.give_ref), channel_id=1, source_target_pairs={{0,64},{64,0},{1,65},{65,1},{2,66},{66,2},{3,67},{67,3},{4,68},{68... | collective-permute-start | bytes 417800 | tf_op jit(solution)/shard_map/ppermute | solution.py:66
